TPU v7x, 256 devices: a whole 4x4x8 slice. The times are simulated.
256 devices in a mesh: gx: 4 (over x), gy: 8 (over y, core), ha: 8 (over z).
Axes of the slice: x: 4, y: 4, z: 8, core: 2. Of those that a mesh axis runs over, the one named last changes fastest.
Arguments:
- level_set: float32 [32, 128, 80, 128], P('gx', 'gy', 'ha'), may hold values from -4 to 4
- wind_field: float32 [2, 32, 128], P(None, 'gx', 'gy'), may hold values from -3 to 3
Outputs:
- increment: float32 [32, 128, 80, 128], P('gx', 'gy', 'ha')
All inputs are finite; a program needn't handle non-finite values.
Results may differ from a plain program's by a relative error of at most 0.000073.
Values sent between devices are 32-bit elements; how exact they have to be, the bound alone decides.
No kernel may reach another device: no remote copies, remote signals or barrier semaphores. Data moves between devices by JAX's collectives and lax.ppermute only.
A program may use at most 128 MiB of HBM per device.

v0:
```python
import math

import jax
import jax.numpy as jnp
from jax import lax
from jax.sharding import PartitionSpec as P

CELL_SIZE = 0.05
SPEED_LOW = 0.1
SPEED_SPAN = 0.4
TURN_MAX = 1.0
ACCEL_MAX = 0.05
CFL_NUMBER = 0.5
WENO_EPS = 1e-06


def from_everyone(value, axis):
    copies = jnp.broadcast_to(value, (lax.axis_size(axis), *value.shape))
    return lax.all_to_all(copies, axis, split_axis=0, concat_axis=0, tiled=True)


def over_copies(value, axis):
    everything = from_everyone(value, axis)
    return jnp.max(everything, axis=0)


def extended_2(value, sides, width):
    edges = {}
    for axis, dim in sides:
        size, length = (lax.axis_size(axis), value.shape[dim])
        up = [(i, (i + 1) % size) for i in range(size - 1)]
        last = lax.slice_in_dim(value, length - width, length, axis=dim)
        initial = lax.slice_in_dim(value, 0, width, axis=dim)
        edges[dim] = (
            lax.ppermute(last, axis, up),
            lax.ppermute(initial, axis, [(b, a) for a, b in up]),
        )
    done = []
    for _, dim in sides:
        low, high = edges[dim]
        around = [(width, width) if d in done else (0, 0) for d in range(value.ndim)]
        value = jnp.concatenate([jnp.pad(low, around), value, jnp.pad(high, around)], axis=dim)
        done.append(dim)
    return value


def with_halo(cells, sides, width):
    for axis, dim in sides:
        count = lax.axis_size(axis)
        head = lax.slice_in_dim(cells, 0, width, axis=dim)
        tail = lax.slice_in_dim(cells, cells.shape[dim] - width, cells.shape[dim], axis=dim)
        cells = jnp.concatenate(
            [
                lax.ppermute(tail, axis, [(i, (i + 1) % count) for i in range(count)]),
                cells,
                lax.ppermute(head, axis, [((i + 1) % count, i) for i in range(count)]),
            ],
            axis=dim,
        )
    return cells


def ghost_rows(values, along, at_low):
    length = values.shape[along]
    if at_low:
        edge_row = lax.slice_in_dim(values, 0, 1, axis=along)
        next_row = lax.slice_in_dim(values, 1, 2, axis=along)
        reaches = (3.0, 2.0, 1.0)
    else:
        edge_row = lax.slice_in_dim(values, length - 1, length, axis=along)
        next_row = lax.slice_in_dim(values, length - 2, length - 1, axis=along)
        reaches = (1.0, 2.0, 3.0)
    slope_edge = edge_row - next_row
    return jnp.concatenate([edge_row + distance * slope_edge for distance in reaches], axis=along)


def fix_edges(extended, along, at_start, at_end, length):
    interior = lax.slice_in_dim(extended, 3, 3 + length, axis=along)
    below_rows = jnp.where(
        at_start, ghost_rows(interior, along, True), lax.slice_in_dim(extended, 0, 3, axis=along)
    )
    above_rows = jnp.where(
        at_end,
        ghost_rows(interior, along, False),
        lax.slice_in_dim(extended, 3 + length, 6 + length, axis=along),
    )
    return jnp.concatenate([below_rows, interior, above_rows], axis=along)


def speed_shifts(values):
    length = values.shape[3]
    below_rows = ghost_rows(values, 3, True)
    above_rows = ghost_rows(values, 3, False)
    shifted = []
    for displace in range(-3, 4):
        pieces = []
        if displace < 0:
            pieces.append(lax.slice_in_dim(below_rows, 3 + displace, 3, axis=3))
        pieces.append(lax.slice_in_dim(values, max(displace, 0), length + min(displace, 0), axis=3))
        if displace > 0:
            pieces.append(lax.slice_in_dim(above_rows, 0, displace, axis=3))
        shifted.append(jnp.concatenate(pieces, axis=3) if len(pieces) > 1 else pieces[0])
    return shifted


def weno_side(left_far, left_near, middle, right_near, right_far):
    guess_one = left_far * (1.0 / 3.0) - left_near * (7.0 / 6.0) + middle * (11.0 / 6.0)
    guess_two = -left_near * (1.0 / 6.0) + middle * (5.0 / 6.0) + right_near * (1.0 / 3.0)
    guess_three = middle * (1.0 / 3.0) + right_near * (5.0 / 6.0) - right_far * (1.0 / 6.0)
    smooth_one = 13.0 / 12.0 * jnp.square(left_far - 2.0 * left_near + middle) + 0.25 * jnp.square(
        left_far - 4.0 * left_near + 3.0 * middle
    )
    smooth_two = 13.0 / 12.0 * jnp.square(
        left_near - 2.0 * middle + right_near
    ) + 0.25 * jnp.square(left_near - right_near)
    smooth_three = 13.0 / 12.0 * jnp.square(
        middle - 2.0 * right_near + right_far
    ) + 0.25 * jnp.square(3.0 * middle - 4.0 * right_near + right_far)
    weight_one = 0.1 / jnp.square(smooth_one + WENO_EPS)
    weight_two = 0.6 / jnp.square(smooth_two + WENO_EPS)
    weight_three = 0.3 / jnp.square(smooth_three + WENO_EPS)
    return (weight_one * guess_one + weight_two * guess_two + weight_three * guess_three) / (
        weight_one + weight_two + weight_three
    )


def weno_pair(shifted, spacing):
    slopes = [(shifted[position + 1] - shifted[position]) / spacing for position in range(6)]
    left_slope = weno_side(slopes[0], slopes[1], slopes[2], slopes[3], slopes[4])
    right_slope = weno_side(slopes[5], slopes[4], slopes[3], slopes[2], slopes[1])
    return (left_slope, right_slope)


def cell_rates(cos_head, sin_head, speeds, wind_x, wind_y, d_theta, d_speed):
    along_x = speeds[None, None, None, :] * cos_head[None, None, :, None] + wind_x[:, :, None, None]
    along_y = speeds[None, None, None, :] * sin_head[None, None, :, None] + wind_y[:, :, None, None]
    return (
        jnp.abs(along_x) / CELL_SIZE
        + jnp.abs(along_y) / CELL_SIZE
        + TURN_MAX / d_theta
        + ACCEL_MAX / d_speed
    )


def hamilton(x_pair, y_pair, head_pair, speed_pair, cos_head, sin_head, speeds, wind_x, wind_y):
    flow_x = speeds[None, None, None, :] * cos_head[None, None, :, None] + wind_x[:, :, None, None]
    flow_y = speeds[None, None, None, :] * sin_head[None, None, :, None] + wind_y[:, :, None, None]
    mean_x = 0.5 * (x_pair[0] + x_pair[1])
    mean_y = 0.5 * (y_pair[0] + y_pair[1])
    mean_head = 0.5 * (head_pair[0] + head_pair[1])
    mean_speed = 0.5 * (speed_pair[0] + speed_pair[1])
    value = -(
        flow_x * mean_x
        + flow_y * mean_y
        + TURN_MAX * jnp.abs(mean_head)
        + ACCEL_MAX * jnp.abs(mean_speed)
    )
    damping = 0.5 * (
        jnp.abs(flow_x) * (x_pair[1] - x_pair[0])
        + jnp.abs(flow_y) * (y_pair[1] - y_pair[0])
        + TURN_MAX * (head_pair[1] - head_pair[0])
        + ACCEL_MAX * (speed_pair[1] - speed_pair[0])
    )
    return -jnp.maximum(value - damping, 0.0)


def body(level_set, wind_field):
    cells_x, cells_y, cells_h, cells_v = level_set.shape
    n_head = cells_h * lax.axis_size("ha")
    head_base = lax.axis_index("ha") * cells_h
    start_x = lax.axis_index("gx") == 0
    end_x = lax.axis_index("gx") == lax.axis_size("gx") - 1
    start_y = lax.axis_index("gy") == 0
    end_y = lax.axis_index("gy") == lax.axis_size("gy") - 1
    wind_x = wind_field[0]
    wind_y = wind_field[1]
    d_theta = 2.0 * math.pi / n_head
    d_speed = SPEED_SPAN / cells_v
    speeds = (
        SPEED_LOW
        + SPEED_SPAN * (jnp.arange(cells_v, dtype=jnp.int32).astype(jnp.float32) + 0.5) / cells_v
    )

    def headings(offset, height):
        slots = (head_base - offset + jnp.arange(height, dtype=jnp.int32) + n_head) % n_head
        angles = slots.astype(jnp.float32) * d_theta
        return (jnp.cos(angles), jnp.sin(angles))

    every_angle = jnp.arange(n_head, dtype=jnp.int32).astype(jnp.float32) * d_theta
    end_speeds = jnp.stack([speeds[0], speeds[cells_v - 1]])
    local_top = jnp.max(
        cell_rates(
            jnp.cos(every_angle), jnp.sin(every_angle), end_speeds, wind_x, wind_y, d_theta, d_speed
        )
    )
    top_rate = over_copies(local_top, ("gx", "gy"))
    time_step = CFL_NUMBER / top_rate

    def slope_field(center, around, offset):
        height = center.shape[2]
        extended = extended_2(center, (("gx", 0), ("gy", 1)), 3)
        extended = fix_edges(extended, 0, start_x, end_x, cells_x)
        extended = fix_edges(extended, 1, start_y, end_y, cells_y)
        x_shifted = [
            extended[3 + displace : 3 + displace + cells_x, 3 : 3 + cells_y]
            for displace in range(-3, 4)
        ]
        y_shifted = [
            extended[3 : 3 + cells_x, 3 + displace : 3 + displace + cells_y]
            for displace in range(-3, 4)
        ]
        head_shifted = [
            around[:, :, 3 + displace : 3 + displace + height] for displace in range(-3, 4)
        ]
        cos_head, sin_head = headings(offset, height)
        return hamilton(
            weno_pair(x_shifted, CELL_SIZE),
            weno_pair(y_shifted, CELL_SIZE),
            weno_pair(head_shifted, d_theta),
            weno_pair(speed_shifts(center), d_speed),
            cos_head,
            sin_head,
            speeds,
            wind_x,
            wind_y,
        )

    def around_heads(surface):
        return with_halo(surface, (("ha", 2),), 3)

    section_one = level_set + time_step * slope_field(level_set, around_heads(level_set), 0)
    section_two = 0.75 * level_set + 0.25 * (
        section_one + time_step * slope_field(section_one, around_heads(section_one), 0)
    )
    advanced = 1.0 / 3.0 * level_set + 2.0 / 3.0 * (
        section_two + time_step * slope_field(section_two, around_heads(section_two), 0)
    )
    return advanced - level_set


def solution(mesh):
    return jax.shard_map(
        body,
        mesh=mesh,
        in_specs=(P("gx", "gy", "ha", None), P(None, "gx", "gy")),
        out_specs=P("gx", "gy", "ha", None),
        check_vma=False,
    )
```

profile of v0, /device:TPU:14, one launch (start us, length us, event | category | flops | bytes accessed | tf_op | source)
XLA Modules:
  0.0 154.5 jit_solution(8316435247508885770)
XLA Ops:
  0.0 1.5 copy.129
  1.5 0.7 fusion.566
  2.3 1.9 %collective-permute-start = (f32[8,3,10,128]{3,0,2,1:T(8,128)}, f32[8,3,10,128]{3,0,2,1:T(8,128)}, u32[]{:S(2)}, u32[]{:S(2)}) collective-permute-start(f32[8,3,10,128]{3,0,2,1:T(8,128)} %get-tuple-element.127), channel_id=1, source_target_pairs={{0,8},{8,16},{16,24},{24,32},{32,40},{40,48},{48,56},{1,9},{9,17},... | collective-permute-start | bytes 368648 | tf_op jit(solution)/shard_map/ppermute | solution.py:35
  4.2 3.6 %collective-permute-start.3 = (f32[8,3,10,128]{3,0,2,1:T(8,128)}, f32[8,3,10,128]{3,0,2,1:T(8,128)}, u32[]{:S(2)}, u32[]{:S(2)}) collective-permute-start(f32[8,3,10,128]{3,0,2,1:T(8,128)} %get-tuple-element.128), channel_id=1, source_target_pairs={{8,0},{16,8},{24,16},{32,24},{40,32},{48,40},{56,48},{9,1},{17,9},... | collective-permute-start | bytes 368648 | tf_op jit(solution)/shard_map/ppermute | solution.py:36
  7.8 0.8 fusion.565
  8.7 1.3 collective-permute-start.1
  10.0 4.6 %collective-permute-start.2 = (f32[3,16,10,128]{3,1,2,0:T(8,128)}, f32[3,16,10,128]{3,1,2,0:T(8,128)S(1)}, u32[]{:S(2)}, u32[]{:S(2)}) collective-permute-start(f32[3,16,10,128]{3,1,2,0:T(8,128)} %get-tuple-element.126), channel_id=1, source_target_pairs={{64,0},{128,64},{192,128},{65,1},{129,65},{193,129},{66,2},{130,66... | collective-permute-start | bytes 737288 | tf_op jit(solution)/shard_map/ppermute | solution.py:36
  15.7 1.3 pad_maximum_fusion.37
  17.1 0.7 fusion.528
  17.8 1.3 broadcast_in_dim.2
  19.1 7.6 %all-to-all-start = ((f32[32,1,1]{2,1,0:T(1,128)}), f32[32,1,1]{2,1,0:T(1,128)}, u32[]{:S(2)}, u32[]{:S(2)}) async-start(f32[32,1,1]{2,1,0:T(1,128)} %broadcast_in_dim.2), calls=%async_computation | async-start | bytes 32768 | tf_op jit(solution)/shard_map/all_to_all | solution.py:19
  26.6 0.8 fusion.567
  27.4 1.9 %collective-permute-start.4 = (f32[8,16,3,128]{3,0,2,1:T(8,128)}, f32[8,16,3,128]{3,0,2,1:T(8,128)}, u32[]{:S(2)}, u32[]{:S(2)}) collective-permute-start(f32[8,16,3,128]{3,0,2,1:T(8,128)} %get-tuple-element.131), channel_id=1, source_target_pairs={{0,1},{1,2},{2,3},{3,4},{4,5},{5,6},{6,7},{7,0},{8,9},{9,10},{10,1... | collective-permute-start | bytes 589832 | tf_op jit(solution)/shard_map/ppermute | solution.py:54
  29.3 1.8 %multiply_add_fusion.28 = (f32[8,16,10,1]{3,0,2,1:T(8,128)S(1)}, f32[8,16,10,1]{3,0,2,1:T(8,128)S(1)}, f32[8,16,10,1]{3,0,2,1:T(8,128)S(1)}, f32[8,16,10,1]{3,0,...) fusion(f32[8,16,10,128]{3,0,2,1:T(8,128)S(1)} %copy.129), kind=kLoop, calls=%fused_computation.663 | loop fusion | flops 15360 | bytes 51200 | tf_op jit(solution)/shard_map/add | solution.py:74
  31.2 1.2 fusion.568
  32.4 1.3 fusion.569
  33.7 1.3 fusion.570
  35.8 1.4 reduce_max.19
  37.9 0.9 collective-permute-done.4
  38.8 3.2 %collective-permute-start.5 = (f32[8,16,3,128]{3,0,2,1:T(8,128)}, f32[8,16,3,128]{3,0,2,1:T(8,128)S(1)}, u32[]{:S(2)}, u32[]{:S(2)}) collective-permute-start(f32[8,16,3,128]{3,0,2,1:T(8,128)} %get-tuple-element.132), channel_id=1, source_target_pairs={{1,0},{2,1},{3,2},{4,3},{5,4},{6,5},{7,6},{0,7},{9,8},{10,9},{11,1... | collective-permute-start | bytes 589832 | tf_op jit(solution)/shard_map/ppermute | solution.py:56
  41.9 0.9 constant_dynamic-update-slice_fusion.1
  43.3 3.4 %collective-permute-done.5 = f32[8,16,3,128]{3,0,2,1:T(8,128)S(1)} collective-permute-done((f32[8,16,3,128]{3,0,2,1:T(8,128)}, f32[8,16,3,128]{3,0,2,1:T(8,128)S(1)}, u32[]{:S(2)}, u32[]{:S(2)}) %collective-permute-start.5) | collective-permute-done | bytes 196640 | tf_op jit(solution)/shard_map/ppermute | solution.py:56
  46.7 1.1 copy.134
  48.1 1.3 select_maximum_fusion.4
  50.1 0.7 slice_select_fusion.5
  50.8 0.7 pad_maximum_fusion
  52.0 0.7 copy-done.7
  54.3 18.9 %fusion.24 = f32[8,16,10,128]{3,0,2,1:T(8,128)S(1)} fusion(f32[8,16,10,1]{3,0,2,1:T(8,128)S(1)} %copy-done.3, f32[8,16,10,1]{3,0,2,1:T(8,128)S(1)} %copy-done.1, f32[8,16,10,1]{3,0,2,1:T(8,128)S(1)} %copy-done.2, f32[8,16,10,125]{3,0,2,1:T(8,128)S(1)} %copy-done.9, f32[8,16,10,126]{3,0,2,1:T(8,128)S(1)} %copy-done.7, f32[8,16,10,127]{3,0,2,1:T(8,128)S(1)} %copy-done.5, ...), kind=kLoop, calls=%fused_computation.107 | loop fusion | flops 99123200 | bytes 12309508 | tf_op jit(solution)/shard_map/add | solution.py:231
  74.7 1.3 collective-permute-start.7
  76.0 4.6 %collective-permute-start.8 = (f32[3,16,10,128]{3,1,2,0:T(8,128)S(1)}, f32[3,16,10,128]{3,1,2,0:T(8,128)S(1)}, u32[]{:S(2)}, u32[]{:S(2)}) collective-permute-start(f32[3,16,10,128]{3,1,2,0:T(8,128)S(1)} %copy.163), channel_id=1, source_target_pairs={{64,0},{128,64},{192,128},{65,1},{129,65},{193,129},{66,2},{130,66... | collective-permute-start | bytes 737288 | tf_op jit(solution)/shard_map/ppermute | solution.py:36
  80.6 2.1 %collective-permute-start.6 = (f32[8,3,10,128]{3,0,2,1:T(8,128)S(1)}, f32[8,3,10,128]{3,0,2,1:T(8,128)S(1)}, u32[]{:S(2)}, u32[]{:S(2)}) collective-permute-start(f32[8,3,10,128]{3,0,2,1:T(8,128)S(1)} %get-tuple-element.109), channel_id=1, source_target_pairs={{0,8},{8,16},{16,24},{24,32},{32,40},{40,48},{48,56},{1,9},{9,17},... | collective-permute-start | bytes 368648 | tf_op jit(solution)/shard_map/ppermute | solution.py:35
  82.7 3.6 %collective-permute-start.9 = (f32[8,3,10,128]{3,0,2,1:T(8,128)S(1)}, f32[8,3,10,128]{3,0,2,1:T(8,128)S(1)}, u32[]{:S(2)}, u32[]{:S(2)}) collective-permute-start(f32[8,3,10,128]{3,0,2,1:T(8,128)S(1)} %get-tuple-element.110), channel_id=1, source_target_pairs={{8,0},{16,8},{24,16},{32,24},{40,32},{48,40},{56,48},{9,1},{17,9},... | collective-permute-start | bytes 368648 | tf_op jit(solution)/shard_map/ppermute | solution.py:36
  86.7 3.4 %collective-permute-start.11 = (f32[8,16,3,128]{3,0,2,1:T(8,128)S(1)}, f32[8,16,3,128]{3,0,2,1:T(8,128)S(1)}, u32[]{:S(2)}, u32[]{:S(2)}) collective-permute-start(f32[8,16,3,128]{3,0,2,1:T(8,128)S(1)} %get-tuple-element.112), channel_id=1, source_target_pairs={{1,0},{2,1},{3,2},{4,3},{5,4},{6,5},{7,6},{0,7},{9,8},{10,9},{11,1... | collective-permute-start | bytes 589832 | tf_op jit(solution)/shard_map/ppermute | solution.py:56
  91.6 0.8 slice_select_fusion.3
  92.4 0.7 pad_maximum_fusion.1
  93.4 1.6 %collective-permute-done.10 = f32[8,16,3,128]{3,0,2,1:T(8,128)S(1)} collective-permute-done((f32[8,16,3,128]{3,0,2,1:T(8,128)S(1)}, f32[8,16,3,128]{3,0,2,1:T(8,128)S(1)}, u32[]{:S(2)}, u32[]{:S(2)}) %collective-permute-start.10) | collective-permute-done | bytes 196640 | tf_op jit(solution)/shard_map/ppermute | solution.py:54
  95.0 18.3 %fusion.35 = f32[8,16,10,128]{3,0,2,1:T(8,128)S(1)} fusion(f32[8,16,10,128]{3,0,2,1:T(8,128)S(1)} %fusion.24, f32[8,16,10,1]{3,0,2,1:T(8,128)S(1)} %get-tuple-element.119, f32[8,16,10,1]{3,0,2,1:T(8,128)S(1)} %get-tuple-element.118, f32[8,16,10,1]{3,0,2,1:T(8,128)S(1)} %get-tuple-element.122, f32[8,16,10,125]{3,0,2,1:T(8,128)S(1)} %get-tuple-element.124, ...), kind=kLoop, calls=%fused_computation.118 | loop fusion | flops 100597760 | bytes 9425924 | tf_op jit(solution)/shard_map/add | solution.py:232
  114.8 1.3 collective-permute-start.13
  116.2 4.6 %collective-permute-start.14 = (f32[3,16,10,128]{3,1,2,0:T(8,128)S(1)}, f32[3,16,10,128]{3,1,2,0:T(8,128)S(1)}, u32[]{:S(2)}, u32[]{:S(2)}) collective-permute-start(f32[3,16,10,128]{3,1,2,0:T(8,128)S(1)} %copy.167), channel_id=1, source_target_pairs={{64,0},{128,64},{192,128},{65,1},{129,65},{193,129},{66,2},{130,66... | collective-permute-start | bytes 737288 | tf_op jit(solution)/shard_map/ppermute | solution.py:36
  120.8 1.9 %collective-permute-start.12 = (f32[8,3,10,128]{3,0,2,1:T(8,128)S(1)}, f32[8,3,10,128]{3,0,2,1:T(8,128)S(1)}, u32[]{:S(2)}, u32[]{:S(2)}) collective-permute-start(f32[8,3,10,128]{3,0,2,1:T(8,128)S(1)} %get-tuple-element.91), channel_id=1, source_target_pairs={{0,8},{8,16},{16,24},{24,32},{32,40},{40,48},{48,56},{1,9},{9,17},... | collective-permute-start | bytes 368648 | tf_op jit(solution)/shard_map/ppermute | solution.py:35
  122.7 3.6 %collective-permute-start.15 = (f32[8,3,10,128]{3,0,2,1:T(8,128)S(1)}, f32[8,3,10,128]{3,0,2,1:T(8,128)S(1)}, u32[]{:S(2)}, u32[]{:S(2)}) collective-permute-start(f32[8,3,10,128]{3,0,2,1:T(8,128)S(1)} %get-tuple-element.92), channel_id=1, source_target_pairs={{8,0},{16,8},{24,16},{32,24},{40,32},{48,40},{56,48},{9,1},{17,9},... | collective-permute-start | bytes 368648 | tf_op jit(solution)/shard_map/ppermute | solution.py:36
  126.4 2.5 %collective-permute-start.16 = (f32[8,16,3,128]{3,0,2,1:T(8,128)S(1)}, f32[8,16,3,128]{3,0,2,1:T(8,128)S(1)}, u32[]{:S(2)}, u32[]{:S(2)}) collective-permute-start(f32[8,16,3,128]{3,0,2,1:T(8,128)S(1)} %get-tuple-element.93), channel_id=1, source_target_pairs={{0,1},{1,2},{2,3},{3,4},{4,5},{5,6},{6,7},{7,0},{8,9},{9,10},{10,1... | collective-permute-start | bytes 589832 | tf_op jit(solution)/shard_map/ppermute | solution.py:54
  128.9 0.9 collective-permute-start.17
  131.3 0.7 slice_select_fusion.1
  133.1 1.1 collective-permute-done.16
  134.1 0.9 collective-permute-done.17
  135.0 18.5 %fusion.47 = f32[8,16,10,128]{3,0,2,1:T(8,128)S(1)} fusion(f32[8,16,10,128]{3,0,2,1:T(8,128)S(1)} %fusion.35, f32[8,16,10,1]{3,0,2,1:T(8,128)S(1)} %get-tuple-element.101, f32[8,16,10,1]{3,0,2,1:T(8,128)S(1)} %get-tuple-element.100, f32[8,16,10,1]{3,0,2,1:T(8,128)S(1)} %get-tuple-element.104, f32[8,16,10,125]{3,0,2,1:T(8,128)S(1)} %get-tuple-element.106, ...), kind=kLoop, calls=%fused_computation.130 | loop fusion | flops 100761600 | bytes 9425924 | tf_op jit(solution)/shard_map/sub | solution.py:238
  153.5 1.0 copy.171
  (93 shorter events, 13.0 us)
Async XLA Ops:
  0.0 7.8 %copy-start = (f32[8,16,10,128]{3,1,2,0:T(8,128)S(1)}, f32[8,16,10,128]{3,1,2,0:T(8,128)}, u32[]{:S(2)}) copy-start(f32[8,16,10,128]{3,1,2,0:T(8,128)} %param.2) | copy-start | bytes 1966084
  0.0 15.7 %copy-start.10 = (f32[2,8,16]{2,1,0:T(8,128)S(1)}, f32[2,8,16]{2,1,0:T(8,128)}, u32[]{:S(2)}) copy-start(f32[2,8,16]{2,1,0:T(8,128)} %param.3) | copy-start | bytes 3076
  2.3 45.8 %collective-permute-start = (f32[8,3,10,128]{3,0,2,1:T(8,128)}, f32[8,3,10,128]{3,0,2,1:T(8,128)}, u32[]{:S(2)}, u32[]{:S(2)}) collective-permute-start(f32[8,3,10,128]{3,0,2,1:T(8,128)} %get-tuple-element.127), channel_id=1, source_target_pairs={{0,8},{8,16},{16,24},{24,32},{32,40},{40,48},{48,56},{1,9},{9,17},... | collective-permute-start | bytes 368648 | tf_op jit(solution)/shard_map/ppermute | solution.py:35
  4.2 43.9 %collective-permute-start.3 = (f32[8,3,10,128]{3,0,2,1:T(8,128)}, f32[8,3,10,128]{3,0,2,1:T(8,128)}, u32[]{:S(2)}, u32[]{:S(2)}) collective-permute-start(f32[8,3,10,128]{3,0,2,1:T(8,128)} %get-tuple-element.128), channel_id=1, source_target_pairs={{8,0},{16,8},{24,16},{32,24},{40,32},{48,40},{56,48},{9,1},{17,9},... | collective-permute-start | bytes 368648 | tf_op jit(solution)/shard_map/ppermute | solution.py:36
  8.7 38.0 %collective-permute-start.1 = (f32[3,16,10,128]{3,1,2,0:T(8,128)}, f32[3,16,10,128]{3,1,2,0:T(8,128)}, u32[]{:S(2)}, u32[]{:S(2)}) collective-permute-start(f32[3,16,10,128]{3,1,2,0:T(8,128)} %get-tuple-element.125), channel_id=1, source_target_pairs={{0,64},{64,128},{128,192},{1,65},{65,129},{129,193},{2,66},{66,130... | collective-permute-start | bytes 737288 | tf_op jit(solution)/shard_map/ppermute | solution.py:35
  10.0 37.9 %collective-permute-start.2 = (f32[3,16,10,128]{3,1,2,0:T(8,128)}, f32[3,16,10,128]{3,1,2,0:T(8,128)S(1)}, u32[]{:S(2)}, u32[]{:S(2)}) collective-permute-start(f32[3,16,10,128]{3,1,2,0:T(8,128)} %get-tuple-element.126), channel_id=1, source_target_pairs={{64,0},{128,64},{192,128},{65,1},{129,65},{193,129},{66,2},{130,66... | collective-permute-start | bytes 737288 | tf_op jit(solution)/shard_map/ppermute | solution.py:36
  14.5 0.5 copy-start.11
  19.1 16.8 %all-to-all-start = ((f32[32,1,1]{2,1,0:T(1,128)}), f32[32,1,1]{2,1,0:T(1,128)}, u32[]{:S(2)}, u32[]{:S(2)}) async-start(f32[32,1,1]{2,1,0:T(1,128)} %broadcast_in_dim.2), calls=%async_computation | async-start | bytes 32768 | tf_op jit(solution)/shard_map/all_to_all | solution.py:19
  27.4 11.4 %collective-permute-start.4 = (f32[8,16,3,128]{3,0,2,1:T(8,128)}, f32[8,16,3,128]{3,0,2,1:T(8,128)}, u32[]{:S(2)}, u32[]{:S(2)}) collective-permute-start(f32[8,16,3,128]{3,0,2,1:T(8,128)} %get-tuple-element.131), channel_id=1, source_target_pairs={{0,1},{1,2},{2,3},{3,4},{4,5},{5,6},{6,7},{7,0},{8,9},{9,10},{10,1... | collective-permute-start | bytes 589832 | tf_op jit(solution)/shard_map/ppermute | solution.py:54
  38.8 7.9 %collective-permute-start.5 = (f32[8,16,3,128]{3,0,2,1:T(8,128)}, f32[8,16,3,128]{3,0,2,1:T(8,128)S(1)}, u32[]{:S(2)}, u32[]{:S(2)}) collective-permute-start(f32[8,16,3,128]{3,0,2,1:T(8,128)} %get-tuple-element.132), channel_id=1, source_target_pairs={{1,0},{2,1},{3,2},{4,3},{5,4},{6,5},{7,6},{0,7},{9,8},{10,9},{11,1... | collective-permute-start | bytes 589832 | tf_op jit(solution)/shard_map/ppermute | solution.py:56
  51.6 1.1 copy-start.7
  51.6 1.3 copy-start.8
  51.6 1.5 copy-start.9
  51.7 1.6 %copy-start.1 = (f32[8,16,10,1]{3,0,2,1:T(8,128)S(1)}, f32[8,16,10,1]{3,0,2,1:T(8,128)}, u32[]{:S(2)}) copy-start(f32[8,16,10,1]{3,0,2,1:T(8,128)} %get-tuple-element.140) | copy-start | bytes 15364
  51.7 1.8 %copy-start.2 = (f32[8,16,10,1]{3,0,2,1:T(8,128)S(1)}, f32[8,16,10,1]{3,0,2,1:T(8,128)}, u32[]{:S(2)}) copy-start(f32[8,16,10,1]{3,0,2,1:T(8,128)} %get-tuple-element.141) | copy-start | bytes 15364
  51.7 2.0 %copy-start.3 = (f32[8,16,10,1]{3,0,2,1:T(8,128)S(1)}, f32[8,16,10,1]{3,0,2,1:T(8,128)}, u32[]{:S(2)}) copy-start(f32[8,16,10,1]{3,0,2,1:T(8,128)} %get-tuple-element.142) | copy-start | bytes 15364
  51.7 2.2 %copy-start.4 = (f32[8,16,10,127]{3,0,2,1:T(8,128)S(1)}, f32[8,16,10,127]{3,0,2,1:T(8,128)}, u32[]{:S(2)}) copy-start(f32[8,16,10,127]{3,0,2,1:T(8,128)} %get-tuple-element.133) | copy-start | bytes 1950724
  51.7 2.4 %copy-start.5 = (f32[8,16,10,127]{3,0,2,1:T(8,128)S(1)}, f32[8,16,10,127]{3,0,2,1:T(8,128)}, u32[]{:S(2)}) copy-start(f32[8,16,10,127]{3,0,2,1:T(8,128)} %get-tuple-element.134) | copy-start | bytes 1950724
  51.8 2.5 %copy-start.6 = (f32[8,16,10,126]{3,0,2,1:T(8,128)S(1)}, f32[8,16,10,126]{3,0,2,1:T(8,128)}, u32[]{:S(2)}) copy-start(f32[8,16,10,126]{3,0,2,1:T(8,128)} %get-tuple-element.135) | copy-start | bytes 1935364
  74.7 12.1 %collective-permute-start.7 = (f32[3,16,10,128]{3,1,2,0:T(8,128)S(1)}, f32[3,16,10,128]{3,1,2,0:T(8,128)S(1)}, u32[]{:S(2)}, u32[]{:S(2)}) collective-permute-start(f32[3,16,10,128]{3,1,2,0:T(8,128)S(1)} %copy.162), channel_id=1, source_target_pairs={{0,64},{64,128},{128,192},{1,65},{65,129},{129,193},{2,66},{66,130... | collective-permute-start | bytes 737288 | tf_op jit(solution)/shard_map/ppermute | solution.py:35
  76.0 14.3 %collective-permute-start.8 = (f32[3,16,10,128]{3,1,2,0:T(8,128)S(1)}, f32[3,16,10,128]{3,1,2,0:T(8,128)S(1)}, u32[]{:S(2)}, u32[]{:S(2)}) collective-permute-start(f32[3,16,10,128]{3,1,2,0:T(8,128)S(1)} %copy.163), channel_id=1, source_target_pairs={{64,0},{128,64},{192,128},{65,1},{129,65},{193,129},{66,2},{130,66... | collective-permute-start | bytes 737288 | tf_op jit(solution)/shard_map/ppermute | solution.py:36
  80.6 9.9 %collective-permute-start.6 = (f32[8,3,10,128]{3,0,2,1:T(8,128)S(1)}, f32[8,3,10,128]{3,0,2,1:T(8,128)S(1)}, u32[]{:S(2)}, u32[]{:S(2)}) collective-permute-start(f32[8,3,10,128]{3,0,2,1:T(8,128)S(1)} %get-tuple-element.109), channel_id=1, source_target_pairs={{0,8},{8,16},{16,24},{24,32},{32,40},{40,48},{48,56},{1,9},{9,17},... | collective-permute-start | bytes 368648 | tf_op jit(solution)/shard_map/ppermute | solution.py:35
  82.7 7.8 %collective-permute-start.9 = (f32[8,3,10,128]{3,0,2,1:T(8,128)S(1)}, f32[8,3,10,128]{3,0,2,1:T(8,128)S(1)}, u32[]{:S(2)}, u32[]{:S(2)}) collective-permute-start(f32[8,3,10,128]{3,0,2,1:T(8,128)S(1)} %get-tuple-element.110), channel_id=1, source_target_pairs={{8,0},{16,8},{24,16},{32,24},{40,32},{48,40},{56,48},{9,1},{17,9},... | collective-permute-start | bytes 368648 | tf_op jit(solution)/shard_map/ppermute | solution.py:36
  86.4 8.6 %collective-permute-start.10 = (f32[8,16,3,128]{3,0,2,1:T(8,128)S(1)}, f32[8,16,3,128]{3,0,2,1:T(8,128)S(1)}, u32[]{:S(2)}, u32[]{:S(2)}) collective-permute-start(f32[8,16,3,128]{3,0,2,1:T(8,128)S(1)} %get-tuple-element.111), channel_id=1, source_target_pairs={{0,1},{1,2},{2,3},{3,4},{4,5},{5,6},{6,7},{7,0},{8,9},{9,10},{10,1... | collective-permute-start | bytes 589832 | tf_op jit(solution)/shard_map/ppermute | solution.py:54
  86.7 8.3 %collective-permute-start.11 = (f32[8,16,3,128]{3,0,2,1:T(8,128)S(1)}, f32[8,16,3,128]{3,0,2,1:T(8,128)S(1)}, u32[]{:S(2)}, u32[]{:S(2)}) collective-permute-start(f32[8,16,3,128]{3,0,2,1:T(8,128)S(1)} %get-tuple-element.112), channel_id=1, source_target_pairs={{1,0},{2,1},{3,2},{4,3},{5,4},{6,5},{7,6},{0,7},{9,8},{10,9},{11,1... | collective-permute-start | bytes 589832 | tf_op jit(solution)/shard_map/ppermute | solution.py:56
  114.8 14.1 %collective-permute-start.13 = (f32[3,16,10,128]{3,1,2,0:T(8,128)S(1)}, f32[3,16,10,128]{3,1,2,0:T(8,128)S(1)}, u32[]{:S(2)}, u32[]{:S(2)}) collective-permute-start(f32[3,16,10,128]{3,1,2,0:T(8,128)S(1)} %copy.166), channel_id=1, source_target_pairs={{0,64},{64,128},{128,192},{1,65},{65,129},{129,193},{2,66},{66,130... | collective-permute-start | bytes 737288 | tf_op jit(solution)/shard_map/ppermute | solution.py:35
  116.2 13.8 %collective-permute-start.14 = (f32[3,16,10,128]{3,1,2,0:T(8,128)S(1)}, f32[3,16,10,128]{3,1,2,0:T(8,128)S(1)}, u32[]{:S(2)}, u32[]{:S(2)}) collective-permute-start(f32[3,16,10,128]{3,1,2,0:T(8,128)S(1)} %copy.167), channel_id=1, source_target_pairs={{64,0},{128,64},{192,128},{65,1},{129,65},{193,129},{66,2},{130,66... | collective-permute-start | bytes 737288 | tf_op jit(solution)/shard_map/ppermute | solution.py:36
  120.8 9.4 %collective-permute-start.12 = (f32[8,3,10,128]{3,0,2,1:T(8,128)S(1)}, f32[8,3,10,128]{3,0,2,1:T(8,128)S(1)}, u32[]{:S(2)}, u32[]{:S(2)}) collective-permute-start(f32[8,3,10,128]{3,0,2,1:T(8,128)S(1)} %get-tuple-element.91), channel_id=1, source_target_pairs={{0,8},{8,16},{16,24},{24,32},{32,40},{40,48},{48,56},{1,9},{9,17},... | collective-permute-start | bytes 368648 | tf_op jit(solution)/shard_map/ppermute | solution.py:35
  122.7 7.5 %collective-permute-start.15 = (f32[8,3,10,128]{3,0,2,1:T(8,128)S(1)}, f32[8,3,10,128]{3,0,2,1:T(8,128)S(1)}, u32[]{:S(2)}, u32[]{:S(2)}) collective-permute-start(f32[8,3,10,128]{3,0,2,1:T(8,128)S(1)} %get-tuple-element.92), channel_id=1, source_target_pairs={{8,0},{16,8},{24,16},{32,24},{40,32},{48,40},{56,48},{9,1},{17,9},... | collective-permute-start | bytes 368648 | tf_op jit(solution)/shard_map/ppermute | solution.py:36
  126.4 7.8 %collective-permute-start.16 = (f32[8,16,3,128]{3,0,2,1:T(8,128)S(1)}, f32[8,16,3,128]{3,0,2,1:T(8,128)S(1)}, u32[]{:S(2)}, u32[]{:S(2)}) collective-permute-start(f32[8,16,3,128]{3,0,2,1:T(8,128)S(1)} %get-tuple-element.93), channel_id=1, source_target_pairs={{0,1},{1,2},{2,3},{3,4},{4,5},{5,6},{6,7},{7,0},{8,9},{9,10},{10,1... | collective-permute-start | bytes 589832 | tf_op jit(solution)/shard_map/ppermute | solution.py:54
  128.9 6.1 %collective-permute-start.17 = (f32[8,16,3,128]{3,0,2,1:T(8,128)S(1)}, f32[8,16,3,128]{3,0,2,1:T(8,128)S(1)}, u32[]{:S(2)}, u32[]{:S(2)}) collective-permute-start(f32[8,16,3,128]{3,0,2,1:T(8,128)S(1)} %get-tuple-element.94), channel_id=1, source_target_pairs={{1,0},{2,1},{3,2},{4,3},{5,4},{6,5},{7,6},{0,7},{9,8},{10,9},{11,1... | collective-permute-start | bytes 589832 | tf_op jit(solution)/shard_map/ppermute | solution.py:56
where the time goes:
time: 155 us
  other arithmetic  71.8 us (46%)
  starting transfers between devices  54.2 us (35%)
  local copies, waits for them, and re-layouts  19.3 us (12%)
  waiting for transfers between devices  7.83 us (5%)
    ppermute x6, starting transfers between devices, extended_2(): lax.ppermute(initial, axis, [(b, a) for a, b in up])  24.6 us
    add x1, other arithmetic, body(): level_set + time_step * slope_field(level_set, around_heads(level_set), 0)  18.9 us
    sub x1, other arithmetic, body(): return advanced - level_set  18.5 us
    add x1, other arithmetic, body(): 0.75 * level_set  18.3 us
    ppermute x6, starting transfers between devices, extended_2(): lax.ppermute(last, axis, up)  9.8 us
    all_to_all x1, starting transfers between devices, from_everyone(): return lax.all_to_all(copies, axis, split_axis=0, concat_axis=0, tiled=True)  7.55 us
    ppermute x3, starting transfers between devices, with_halo(): lax.ppermute(head, axis, [((i + 1) % count, i) for i in range(count)])  7.5 us
    unnamed x26, local copies, waits for them, and re-layouts  5.3 us
  transfers between devices with their start and end apart: 19, of which 5 were waited for; matrix products, arithmetic and copies ran while one was open for 15% of the time, Pallas kernels for 0%

commit v1 on v0

v1 whole, which is shorter than its diff:
```python
import functools
import math

import jax
import jax.numpy as jnp
import numpy as np
from jax import lax
from jax.experimental import pallas as pl
from jax.experimental.pallas import tpu as pltpu
from jax.sharding import PartitionSpec as P

CELL_SIZE = 0.05
SPEED_LOW = 0.1
SPEED_SPAN = 0.4
TURN_MAX = 1.0
ACCEL_MAX = 0.05
CFL_NUMBER = 0.5
WENO_EPS = 1e-06

LEAN = 1.375
LEVEL = 0.625
REST = 0.609375
UP = 24


def floor_of(spacing):
    return 0.75 * WENO_EPS * spacing * spacing


def squared(value):
    return value * value


def inverse_square(value):
    return squared(1.0 / value)


def one_sided(flow, below_two, below, center, above, above_two, rise, floor):
    ahead = flow > 0.0
    far = jnp.where(ahead, above_two, below_two)
    near = jnp.where(ahead, above, below)
    back = jnp.where(ahead, below, above)
    near_rest = squared(near) * REST + floor
    center_rest = squared(center) * REST + floor
    lean = center * LEAN
    weight_one = inverse_square(squared(far - near * LEAN) + near_rest)
    weight_two = inverse_square(squared(near - center * LEVEL) + center_rest) * 6.0
    weight_three = inverse_square(squared(back - lean) + center_rest) * 3.0
    step = near - center
    fourth_here = (step - (center - back)) * (1.0 / 6.0)
    fourth_near = ((far - near) - step) * (1.0 / 3.0)
    total = weight_one + weight_two + weight_three
    shift = (weight_one * fourth_near + weight_three * fourth_here) / total - 0.5 * fourth_here
    middle = rise - 0.5 * center - (above - below) * (1.0 / 12.0)
    return flow * middle + jnp.abs(flow) * shift


def column_parts(line, floor):
    rise = [line[i + 1] - line[i] for i in range(len(line) - 1)]
    bend = [rise[i + 1] - rise[i] for i in range(len(rise) - 1)]
    turn = [bend[i + 1] - bend[i] for i in range(len(bend) - 1)]
    fourth = [(turn[i + 1] - turn[i]) * (1.0 / 3.0) for i in range(len(turn) - 1)]
    count = len(line) - 6
    at = lambda j: bend[j + 2]
    rest = {j: squared(at(j)) * REST + floor for j in range(-1, count + 1)}
    lean = {j: at(j) * LEAN for j in range(-1, count + 1)}
    to_up = {j: inverse_square(squared(at(j + 1) - lean[j]) + rest[j]) for j in range(0, count + 1)}
    to_down = {j: inverse_square(squared(at(j - 1) - lean[j]) + rest[j]) for j in range(-1, count)}
    pair = {
        j: inverse_square(squared(at(j - 1) - at(j) * LEVEL) + rest[j]) * 6.0
        for j in range(0, count + 1)
    }
    middle = [
        rise[i + 3] - 0.5 * at(i) - (at(i + 1) - at(i - 1)) * (1.0 / 12.0) for i in range(count)
    ]
    return (lambda j: fourth[j + 1]), to_up, to_down, pair, middle


def two_sided(fourth, to_up, to_down, to_up_3, to_down_3, pair, middle, i):
    half = 0.5 * fourth(i)
    right = (to_up[i + 1] * fourth(i + 1) + to_down_3[i] * half) / (
        to_up[i + 1] + to_down_3[i] + pair[i + 1]
    )
    left = (to_down[i - 1] * fourth(i - 1) + to_up_3[i] * half) / (
        to_down[i - 1] + to_up_3[i] + pair[i]
    )
    return jnp.maximum(right + middle[i], left - middle[i]) - 0.5 * half


def picked(flow, fourth, to_up, to_down, pair, middle, i):
    ahead = flow > 0.0
    weight_one = jnp.where(ahead, to_up[i + 1], to_down[i - 1])
    weight_two = jnp.where(ahead, pair[i + 1], pair[i])
    weight_three = jnp.where(ahead, to_down[i], to_up[i]) * 3.0
    far = jnp.where(ahead, fourth(i + 1), fourth(i - 1))
    half = 0.5 * fourth(i)
    shift = (weight_one * far + weight_three * half) / (
        weight_one + weight_two + weight_three
    ) - 0.5 * half
    return flow * middle[i] + jnp.abs(flow) * shift


def speed_kernel(u_ref, out_ref, *, d_speed):
    nx, nh, ny, nv = u_ref.shape
    floor = floor_of(d_speed)
    lane = lax.broadcasted_iota(jnp.int32, (ny, nv), 1)
    first = lane == 0
    last = lane == nv - 1
    inside = jnp.logical_not(jnp.logical_or(first, last))

    def before(value):
        return pltpu.roll(value, 1, 1)

    def after(value):
        return pltpu.roll(value, nv - 1, 1)

    top = 1.0 / (floor * floor)

    def step(k, carry):
        x = k // nh
        h = k % nh
        u = u_ref[x, h]
        rise_here = u - before(u)
        rise_next = after(u) - u
        bend = jnp.where(inside, rise_next - rise_here, 0.0)
        rise = jnp.where(last, rise_here, rise_next)
        below = before(bend)
        above = after(bend)
        rest = squared(bend) * REST + floor
        lean = bend * LEAN
        to_up = inverse_square(squared(above - lean) + rest)
        to_down = inverse_square(squared(below - lean) + rest)
        pair = inverse_square(squared(below - bend * LEVEL) + rest) * 6.0
        fourth = ((above - bend) - (bend - below)) * (1.0 / 3.0)
        half = 0.5 * fourth
        down_before = jnp.where(first, top, before(to_down))
        up_after = jnp.where(last, top, after(to_up))
        fourth_before = jnp.where(first, 0.0, before(fourth))
        fourth_after = jnp.where(last, 0.0, after(fourth))
        up_3 = to_up * 3.0
        down_3 = to_down * 3.0
        middle = rise - 0.5 * bend - (above - below) * (1.0 / 12.0)
        right = (up_after * fourth_after + down_3 * half) / (up_after + down_3 + after(pair))
        left = (down_before * fourth_before + up_3 * half) / (down_before + up_3 + pair)
        out_ref[x, h] = (jnp.maximum(right + middle, left - middle) - 0.5 * half) * (
            ACCEL_MAX / d_speed
        )
        return carry

    lax.fori_loop(0, nx * nh, step, 0, unroll=2)


def ghosts(edge, inner):
    slope = edge - inner
    one = edge + slope
    two = edge + 2.0 * slope
    three = edge + 3.0 * slope
    return one, two, three


def main_kernel(
    flag_ref, dt_ref, u_ref, part_ref, *refs, stage, d_theta
):
    refs = list(refs)
    base_ref = refs.pop(0) if stage > 1 else None
    xlo, xhi, ylo, yhi, hlo, hhi, vel_ref, wind_ref = refs[:8]
    out_ref = refs[8]
    faces = refs[9:-3]
    pad_ref, bend_ref, acc_ref = refs[-3:]
    nx, nh, ny, nv = u_ref.shape
    halves = ny // 8
    floor = floor_of(CELL_SIZE)
    start_x = flag_ref[0] == 1
    end_x = flag_ref[1] == 1
    start_y = flag_ref[2] == 1
    end_y = flag_ref[3] == 1

    def fill(k, carry):
        x = k // nh
        h = k % nh
        pad_ref[k, 8 : 8 + ny] = u_ref[x, h]
        one, two, three = ghosts(u_ref[x, h, 0:1], u_ref[x, h, 1:2])
        low = jnp.concatenate([three, two, one], axis=0)
        pad_ref[k, 5:8] = jnp.where(start_y, low, ylo[x, h])
        one, two, three = ghosts(u_ref[x, h, ny - 1 : ny], u_ref[x, h, ny - 2 : ny - 1])
        high = jnp.concatenate([one, two, three], axis=0)
        pad_ref[k, 8 + ny : 11 + ny] = jnp.where(end_y, high, yhi[x, h])
        return carry

    lax.fori_loop(0, nx * nh, fill, 0, unroll=2)

    def bend(k, carry):
        for r in range(0, UP, 8):
            here = pad_ref[k, r + 6 : r + 14]
            bend_ref[k, r : r + 8] = (pad_ref[k, r + 7 : r + 15] - here) - (
                here - pad_ref[k, r + 5 : r + 13]
            )
        return carry

    lax.fori_loop(0, nx * nh, bend, 0, unroll=2)

    def along_y(k, carry):
        x = k // nh
        h = k % nh
        for half in range(halves):
            r = 8 * half
            flow = vel_ref[1, h] + wind_ref[1, x, r : r + 8]
            rise = pad_ref[k, 9 + r : 17 + r] - pad_ref[k, 8 + r : 16 + r]
            near = [bend_ref[k, r + s : r + s + 8] for s in range(5)]
            acc_ref[x, h, r : r + 8] = part_ref[x, h, r : r + 8] + one_sided(
                flow, *near, rise, floor
            )
        return carry

    lax.fori_loop(0, nx * nh, along_y, 0, unroll=2)

    def along_x(k, carry):
        h = k // halves
        rows = pl.ds(pl.multiple_of((k % halves) * 8, 8), 8)
        mine = [u_ref[x, h, rows] for x in range(nx)]
        low = ghosts(mine[0], mine[1])
        high = ghosts(mine[nx - 1], mine[nx - 2])
        line = (
            [jnp.where(start_x, low[2 - r], xlo[r, h, rows]) for r in range(3)]
            + mine
            + [jnp.where(end_x, high[r], xhi[r, h, rows]) for r in range(3)]
        )
        fourth, to_up, to_down, pair, middle = column_parts(line, floor)
        speed = vel_ref[0, h]
        for x in range(nx):
            flow = speed + wind_ref[0, x, rows]
            acc_ref[x, h, rows] = acc_ref[x, h, rows] + picked(
                flow, fourth, to_up, to_down, pair, middle, x
            )
        return carry

    lax.fori_loop(0, nh * halves, along_x, 0)

    dt = dt_ref[0]
    theta_floor = floor_of(d_theta)

    def along_heading(k, carry):
        x = k // halves
        rows = pl.ds(pl.multiple_of((k % halves) * 8, 8), 8)
        line = (
            [hlo[x, r, rows] for r in range(3)]
            + [u_ref[x, h, rows] for h in range(nh)]
            + [hhi[x, r, rows] for r in range(3)]
        )
        fourth, to_up, to_down, pair, middle = column_parts(line, theta_floor)
        up_3 = {j: to_up[j] * 3.0 for j in range(nh)}
        down_3 = {j: to_down[j] * 3.0 for j in range(nh)}
        for h in range(nh):
            term = two_sided(fourth, to_up, to_down, up_3, down_3, pair, middle, h)
            change = dt * jnp.minimum(acc_ref[x, h, rows] + term * (TURN_MAX / d_theta), 0.0)
            u = line[h + 3]
            if stage == 1:
                value = u + change
            elif stage == 2:
                value = 0.75 * base_ref[x, h, rows] + 0.25 * (u + change)
            else:
                value = (2.0 / 3.0) * ((u - base_ref[x, h, rows]) + change)
            out_ref[x, h, rows] = value
            if stage < 3:
                if h < 3:
                    faces[2][x, h, rows] = value
                if h >= nh - 3:
                    faces[3][x, h - nh + 3, rows] = value
        return carry

    lax.fori_loop(0, nx * halves, along_heading, 0)

    if stage < 3:

        def edge(k, carry):
            x = k // nh
            h = k % nh
            faces[0][x, h] = out_ref[x, h, 0:3]
            faces[1][x, h] = out_ref[x, h, ny - 3 : ny]
            return carry

        lax.fori_loop(0, nx * nh, edge, 0, unroll=4)


def rate_kernel(table_ref, wind_ref, out_ref):
    fast_x = jnp.abs(table_ref[0] + wind_ref[0])
    fast_y = jnp.abs(table_ref[1] + wind_ref[1])
    out_ref[0, 0] = jnp.max(fast_x + fast_y)


VMEM = pl.BlockSpec(memory_space=pltpu.VMEM)
SMEM = pl.BlockSpec(memory_space=pltpu.SMEM)


def ring(count, step):
    return [(i, (i + step) % count) for i in range(count)]


def body(level_set, wind_field):
    field = jnp.transpose(level_set, (0, 2, 1, 3))
    nx, nh, ny, nv = field.shape
    n_head = nh * lax.axis_size("ha")
    d_theta = 2.0 * math.pi / n_head
    d_speed = SPEED_SPAN / nv
    gx, gy = lax.axis_index("gx"), lax.axis_index("gy")
    flags = jnp.stack(
        [gx == 0, gx == lax.axis_size("gx") - 1, gy == 0, gy == lax.axis_size("gy") - 1]
    ).astype(jnp.int32)

    every_angle = np.arange(n_head, dtype=np.float32) * np.float32(d_theta)
    ends = [SPEED_LOW + SPEED_SPAN * 0.5 / nv, SPEED_LOW + SPEED_SPAN * (nv - 0.5) / nv]
    table = np.stack(
        [
            np.concatenate([np.float32(v) * way(every_angle) for v in ends])
            for way in (np.cos, np.sin)
        ]
    ).astype(np.float32)
    table = np.ascontiguousarray(np.broadcast_to(table[:, :, None], (*table.shape, nx * ny)))
    local_top = pl.pallas_call(
        rate_kernel,
        out_shape=jax.ShapeDtypeStruct((1, 1), jnp.float32),
        in_specs=[VMEM, VMEM],
        out_specs=SMEM,
        name="rate",
    )(jnp.asarray(table), wind_field.reshape(2, 1, nx * ny))[0, 0]

    speeds = SPEED_LOW + SPEED_SPAN * (jnp.arange(nv, dtype=jnp.float32) + 0.5) / nv
    angles = (lax.axis_index("ha") * nh + jnp.arange(nh, dtype=jnp.int32)).astype(
        jnp.float32
    ) * d_theta
    heading = jnp.stack([jnp.cos(angles), jnp.sin(angles)])
    velocity = heading[:, :, None, None] * jnp.broadcast_to(
        speeds * (1.0 / CELL_SIZE), (2, nh, 8, nv)
    )
    wind = jnp.broadcast_to((wind_field * (1.0 / CELL_SIZE))[..., None], (2, nx, ny, nv))

    shape = jax.ShapeDtypeStruct(field.shape, jnp.float32)
    x_face = jax.ShapeDtypeStruct((3, nh, ny, nv), jnp.float32)
    y_face = jax.ShapeDtypeStruct((nx, nh, 3, nv), jnp.float32)
    h_face = jax.ShapeDtypeStruct((nx, 3, ny, nv), jnp.float32)

    def speed_part(u):
        return pl.pallas_call(
            functools.partial(speed_kernel, d_speed=d_speed),
            out_shape=shape,
            in_specs=[VMEM],
            out_specs=VMEM,
            cost_estimate=pl.CostEstimate(
                flops=100 * nx * nh * ny * nv, bytes_accessed=8 * nx * nh * ny * nv, transcendentals=0
            ),
            compiler_params=pltpu.CompilerParams(vmem_limit_bytes=8 << 20),
            name="speed",
        )(u)

    def main(stage, u, part, halos, time_step, base):
        outs = [shape]
        if stage < 3:
            outs += [y_face, y_face, h_face, h_face]
        ins = [flags, time_step, u, part] + ([base] if stage > 1 else []) + [*halos, velocity, wind]
        return pl.pallas_call(
            functools.partial(main_kernel, stage=stage, d_theta=d_theta),
            out_shape=outs,
            in_specs=[SMEM, SMEM] + [VMEM] * (len(ins) - 2),
            out_specs=[VMEM] * len(outs),
            scratch_shapes=[
                pltpu.VMEM((nx * nh, ny + 16, nv), jnp.float32),
                pltpu.VMEM((nx * nh, UP, nv), jnp.float32),
                pltpu.VMEM((nx, nh, ny, nv), jnp.float32),
            ],
            cost_estimate=pl.CostEstimate(
                flops=300 * nx * nh * ny * nv, bytes_accessed=16 * nx * nh * ny * nv, transcendentals=0
            ),
            compiler_params=pltpu.CompilerParams(vmem_limit_bytes=24 << 20),
            name=f"main{stage}",
        )(*ins)

    def exchange(u, y_first, y_last, h_first, h_last):
        xlo = lax.ppermute(u[nx - 3 :], "gx", ring(lax.axis_size("gx"), 1))
        xhi = lax.ppermute(u[:3], "gx", ring(lax.axis_size("gx"), -1))
        hlo = lax.ppermute(h_last, "ha", ring(lax.axis_size("ha"), 1))
        hhi = lax.ppermute(h_first, "ha", ring(lax.axis_size("ha"), -1))
        ylo = lax.ppermute(y_last, "gy", ring(lax.axis_size("gy"), 1))
        yhi = lax.ppermute(y_first, "gy", ring(lax.axis_size("gy"), -1))
        return xlo, xhi, ylo, yhi, hlo, hhi

    faces = (field[:, :, :3], field[:, :, ny - 3 :], field[:, :3], field[:, nh - 3 :])
    halos = exchange(field, *faces)
    copies = jnp.broadcast_to(local_top, (lax.axis_size(("gx", "gy")), 1, 1))
    tops = lax.all_to_all(copies, ("gx", "gy"), split_axis=0, concat_axis=0, tiled=True)
    top_rate = jnp.max(tops) / CELL_SIZE + TURN_MAX / d_theta + ACCEL_MAX / d_speed
    time_step = (CFL_NUMBER / top_rate).reshape(1)

    u = field
    for stage in (1, 2, 3):
        part = speed_part(u)
        u, *faces = main(stage, u, part, halos, time_step, field)
        if stage < 3:
            halos = exchange(u, *faces)
    return jnp.transpose(u, (0, 2, 1, 3))


def solution(mesh):
    return jax.shard_map(
        body,
        mesh=mesh,
        in_specs=(P("gx", "gy", "ha", None), P(None, "gx", "gy")),
        out_specs=P("gx", "gy", "ha", None),
        check_vma=False,
    )
```

time: 155 us -> 99.1 us (0.64)
  the two profiles are of different devices: /device:TPU:14 before, /device:TPU:6 now
where the time goes in v1:
time: 99.1 us; the launch traced here: 98.8 us
  Pallas kernels  55.7 us (56%)
  starting transfers between devices  36.4 us (37%)
  local copies, waits for them, and re-layouts  4.73 us (5%)
  between operations  1.01 us (1%)
    pallas_call x3, Pallas kernels, speed_part(): pl.pallas_call(functools.partial(speed_kernel, d_speed=d_speed), out_shap...  30 us
    pallas_call x3, Pallas kernels, main(): pl.pallas_call(functools.partial(main_kernel, stage=stage, d_theta=d_thet...  24.1 us
    ppermute x3, starting transfers between devices, exchange(): hhi = lax.ppermute(h_first, 'ha', ring(lax.axis_size('ha'), -1))  12.4 us
    ppermute x3, starting transfers between devices, exchange(): xlo = lax.ppermute(u[nx - 3:], 'gx', ring(lax.axis_size('gx'), 1))  8.96 us
    all_to_all x1, starting transfers between devices, body(): lax.all_to_all(copies, ('gx', 'gy'), split_axis=0, concat_axis=0, tiled=T...  7.61 us
    ppermute x3, starting transfers between devices, exchange(): yhi = lax.ppermute(y_first, 'gy', ring(lax.axis_size('gy'), -1))  6.35 us
  transfers between devices with their start and end apart: 19, of which 0 were waited for; matrix products, arithmetic and copies ran while one was open for 3% of the time, Pallas kernels for 30%

profile of v1, /device:TPU:6, one launch (start us, length us, event | category | flops | bytes accessed | tf_op | source)
XLA Modules:
  0.0 98.8 jit_solution(5065737193830401821)
XLA Ops:
  0.0 1.4 %reshape.28.wind_ref = f32[2,1,128]{2,1,0:T(1,128)} reshape(f32[2,8,16]{2,1,0:T(8,128)} %param.4) | data formatting | bytes 2048 | tf_op jit(solution)/shard_map/reshape | solution.py:325
  1.4 1.6 %rate.1 = f32[1,1]{1,0:T(1,128)} custom-call(f32[2,160,128]{2,1,0:T(8,128)} %constant.45.clone.table_ref, f32[2,1,128]{2,1,0:T(1,128)} %reshape.28.wind_ref), custom_call_target="tpu_custom_call" | custom-call | tf_op jit(solution)/shard_map/rate/pallas_call | solution.py:319
  3.0 1.3 %broadcast_in_dim.6 = f32[32,1,1]{2,1,0:T(1,128)} broadcast(f32[]{:T(128)} %bitcast.4), dimensions={} | broadcast | bytes 132 | tf_op jit(solution)/shard_map/broadcast_in_dim | solution.py:388
  4.3 7.6 %all-to-all-start = ((f32[32,1,1]{2,1,0:T(1,128)}), f32[32,1,1]{2,1,0:T(1,128)S(1)}, u32[]{:S(2)}, u32[]{:S(2)}) async-start(f32[32,1,1]{2,1,0:T(1,128)} %broadcast_in_dim.6), calls=%async_computation | async-start | bytes 32768 | tf_op jit(solution)/shard_map/all_to_all | solution.py:389
  11.9 1.8 %fusion.5 = (f32[8,10,3,128]{3,2,1,0:T(4,128)S(1)}, f32[8,10,3,128]{3,2,1,0:T(4,128)}) fusion(f32[8,10,16,128]{3,2,1,0:T(8,128)} %bitcast.8), kind=kLoop, calls=%fused_computation.11 | loop fusion | bytes 491520 | tf_op jit(solution)/shard_map/slice | solution.py:386
  13.7 2.4 %collective-permute-start.3 = (f32[8,10,3,128]{3,2,1,0:T(4,128)S(1)}, f32[8,10,3,128]{3,2,1,0:T(4,128)S(1)}, u32[]{:S(2)}, u32[]{:S(2)}) collective-permute-start(f32[8,10,3,128]{3,2,1,0:T(4,128)S(1)} %get-tuple-element.31), channel_id=1, source_target_pairs={{0,56},{8,0},{16,8},{24,16},{32,24},{40,32},{48,40},{56,48},{1,57}... | collective-permute-start | bytes 368648 | tf_op jit(solution)/shard_map/ppermute | solution.py:383
  16.1 0.0 collective-permute-start.2
  16.2 5.9 %collective-permute-start.5 = (f32[8,3,16,128]{3,2,1,0:T(8,128)S(1)}, f32[8,3,16,128]{3,2,1,0:T(8,128)S(1)}, u32[]{:S(2)}, u32[]{:S(2)}) collective-permute-start(f32[8,3,16,128]{3,2,1,0:T(8,128)S(1)} %get-tuple-element.29), channel_id=1, source_target_pairs={{0,7},{1,0},{2,1},{3,2},{4,3},{5,4},{6,5},{7,6},{8,15},{9,8},{10,9... | collective-permute-start | bytes 589832 | tf_op jit(solution)/shard_map/ppermute | solution.py:381
  22.1 0.0 collective-permute-start.4
  22.1 0.9 collective-permute-start.1
  23.1 0.0 copy-start.1
  23.1 0.1 broadcast_multiply_fusion.refs_6_.refs_7_
  23.2 0.0 collective-permute-done.3.refs_3_
  23.2 2.5 %collective-permute-start = (f32[3,10,16,128]{3,2,1,0:T(8,128)S(1)}, f32[3,10,16,128]{3,2,1,0:T(8,128)S(1)}, u32[]{:S(2)}, u32[]{:S(2)}) collective-permute-start(f32[3,10,16,128]{3,2,1,0:T(8,128)S(1)} %get-tuple-element.34), channel_id=1, source_target_pairs={{0,64},{64,128},{128,192},{192,0},{1,65},{65,129},{129,193},{193,1... | collective-permute-start | bytes 737288 | tf_op jit(solution)/shard_map/ppermute | solution.py:378
  25.7 0.1 add_convert_fusion.flag_ref
  25.8 10.0 %speed.3.part_ref = f32[8,10,16,128]{3,2,1,0:T(8,128)S(1)} custom-call(f32[8,10,16,128]{3,2,1,0:T(8,128)S(1)} %bitcast.11), custom_call_target="tpu_custom_call" | custom-call | flops 16384000 | bytes 1310720 | tf_op jit(solution)/shard_map/speed/pallas_call | solution.py:343
  35.8 0.0 all-to-all-done
  35.8 0.7 reduce_max.9
  37.2 0.0 collective-permute-done.2.refs_2_
  37.2 0.0 collective-permute-done.5.refs_5_
  37.3 0.0 collective-permute-done.4.refs_4_
  37.3 0.0 collective-permute-done.1.refs_1_
  37.3 0.0 collective-permute-done.refs_0_
  37.3 0.1 broadcast_in_dim.15.refs_7_.refs_8_
  37.4 8.0 %main1.1 = (f32[8,10,16,128]{3,2,1,0:T(8,128)S(1)}, f32[8,10,3,128]{3,2,1,0:T(4,128)S(1)}, f32[8,10,3,128]{3,2,1,0:T(4,128)S(1)}, f32[8,3,16,128]{3,2,1,0:T(8,128)S(1)}, f32[8,3,16,128]{3,2,1,0:T(8,128)S(1)}) custom-call(s32[4]{0:T(128)S(1)} %add_convert_fusion.flag_ref, f32[1]{0:T(128)} %bitcast.5.dt_ref, f32[8,10,16,128]{3,2,1,0:T(8,128)S(1)} %bitcast.12, ...), custom_call_target="tpu_custom_call" | custom-call | flops 49152000 | bytes 2621440 | tf_op jit(solution)/shard_map/main1/pallas_call | solution.py:360
  45.4 0.0 collective-permute-start.8
  45.4 0.1 collective-permute-start.7
  45.5 3.2 %collective-permute-start.6 = (f32[3,10,16,128]{3,2,1,0:T(8,128)S(1)}, f32[3,10,16,128]{3,2,1,0:T(8,128)S(1)}, u32[]{:S(2)}, u32[]{:S(2)}) collective-permute-start(f32[3,10,16,128]{3,2,1,0:T(8,128)S(1)} %get-tuple-element.28), channel_id=1, source_target_pairs={{0,64},{64,128},{128,192},{192,0},{1,65},{65,129},{129,193},{193,1... | collective-permute-start | bytes 737288 | tf_op jit(solution)/shard_map/ppermute | solution.py:378
  48.7 0.0 collective-permute-start.10
  48.7 3.2 %collective-permute-start.11 = (f32[8,3,16,128]{3,2,1,0:T(8,128)S(1)}, f32[8,3,16,128]{3,2,1,0:T(8,128)S(1)}, u32[]{:S(2)}, u32[]{:S(2)}) collective-permute-start(f32[8,3,16,128]{3,2,1,0:T(8,128)S(1)} %get-tuple-element.19), channel_id=1, source_target_pairs={{0,7},{1,0},{2,1},{3,2},{4,3},{5,4},{6,5},{7,6},{8,15},{9,8},{10,9... | collective-permute-start | bytes 589832 | tf_op jit(solution)/shard_map/ppermute | solution.py:381
  52.0 0.0 collective-permute-done.8.refs_3_
  52.0 2.1 %collective-permute-start.9 = (f32[8,10,3,128]{3,2,1,0:T(4,128)S(1)}, f32[8,10,3,128]{3,2,1,0:T(4,128)S(1)}, u32[]{:S(2)}, u32[]{:S(2)}) collective-permute-start(f32[8,10,3,128]{3,2,1,0:T(4,128)S(1)} %get-tuple-element.17), channel_id=1, source_target_pairs={{0,56},{8,0},{16,8},{24,16},{32,24},{40,32},{48,40},{56,48},{1,57}... | collective-permute-start | bytes 368648 | tf_op jit(solution)/shard_map/ppermute | solution.py:383
  54.1 10.0 %speed.4.part_ref = f32[8,10,16,128]{3,2,1,0:T(8,128)S(1)} custom-call(f32[8,10,16,128]{3,2,1,0:T(8,128)S(1)} %get-tuple-element.15.u_ref), custom_call_target="tpu_custom_call" | custom-call | flops 16384000 | bytes 1310720 | tf_op jit(solution)/shard_map/speed/pallas_call | solution.py:343
  64.1 0.0 collective-permute-done.9.refs_4_
  64.1 0.0 collective-permute-done.10.refs_5_
  64.1 0.0 collective-permute-done.11.refs_6_
  64.1 0.0 collective-permute-done.7.refs_2_
  64.1 8.0 %main2.1 = (f32[8,10,16,128]{3,2,1,0:T(8,128)S(1)}, f32[8,10,3,128]{3,2,1,0:T(4,128)S(1)}, f32[8,10,3,128]{3,2,1,0:T(4,128)S(1)}, f32[8,3,16,128]{3,2,1,0:T(8,128)S(1)}, f32[8,3,16,128]{3,2,1,0:T(8,128)S(1)}) custom-call(s32[4]{0:T(128)S(1)} %add_convert_fusion.flag_ref, f32[1]{0:T(128)} %bitcast.5.dt_ref, f32[8,10,16,128]{3,2,1,0:T(8,128)S(1)} %get-tuple-element.15.u_ref, ...), custom_call_target="tpu_custom_call" | custom-call | flops 49152000 | bytes 2621440 | tf_op jit(solution)/shard_map/main2/pallas_call | solution.py:360
  72.2 0.0 collective-permute-start.14
  72.2 0.1 collective-permute-start.13
  72.3 3.2 %collective-permute-start.12 = (f32[3,10,16,128]{3,2,1,0:T(8,128)S(1)}, f32[3,10,16,128]{3,2,1,0:T(8,128)S(1)}, u32[]{:S(2)}, u32[]{:S(2)}) collective-permute-start(f32[3,10,16,128]{3,2,1,0:T(8,128)S(1)} %get-tuple-element.26), channel_id=1, source_target_pairs={{0,64},{64,128},{128,192},{192,0},{1,65},{65,129},{129,193},{193,1... | collective-permute-start | bytes 737288 | tf_op jit(solution)/shard_map/ppermute | solution.py:378
  75.5 0.0 collective-permute-start.16
  75.5 3.2 %collective-permute-start.17 = (f32[8,3,16,128]{3,2,1,0:T(8,128)S(1)}, f32[8,3,16,128]{3,2,1,0:T(8,128)S(1)}, u32[]{:S(2)}, u32[]{:S(2)}) collective-permute-start(f32[8,3,16,128]{3,2,1,0:T(8,128)S(1)} %get-tuple-element.24), channel_id=1, source_target_pairs={{0,7},{1,0},{2,1},{3,2},{4,3},{5,4},{6,5},{7,6},{8,15},{9,8},{10,9... | collective-permute-start | bytes 589832 | tf_op jit(solution)/shard_map/ppermute | solution.py:381
  78.8 1.8 %collective-permute-start.15 = (f32[8,10,3,128]{3,2,1,0:T(4,128)S(1)}, f32[8,10,3,128]{3,2,1,0:T(4,128)S(1)}, u32[]{:S(2)}, u32[]{:S(2)}) collective-permute-start(f32[8,10,3,128]{3,2,1,0:T(4,128)S(1)} %get-tuple-element.22), channel_id=1, source_target_pairs={{0,56},{8,0},{16,8},{24,16},{32,24},{40,32},{48,40},{56,48},{1,57}... | collective-permute-start | bytes 368648 | tf_op jit(solution)/shard_map/ppermute | solution.py:383
  80.6 10.0 %speed.5.part_ref = f32[8,10,16,128]{3,2,1,0:T(8,128)S(1)} custom-call(f32[8,10,16,128]{3,2,1,0:T(8,128)S(1)} %get-tuple-element.20.u_ref), custom_call_target="tpu_custom_call" | custom-call | flops 16384000 | bytes 1310720 | tf_op jit(solution)/shard_map/speed/pallas_call | solution.py:343
  90.6 0.0 collective-permute-done.16.refs_5_
  90.6 0.0 collective-permute-done.12.refs_1_
  90.6 8.2 %main3.1 = f32[8,10,16,128]{3,2,1,0:T(8,128)} custom-call(s32[4]{0:T(128)S(1)} %add_convert_fusion.flag_ref, f32[1]{0:T(128)} %bitcast.5.dt_ref, f32[8,10,16,128]{3,2,1,0:T(8,128)S(1)} %get-tuple-element.20.u_ref, f32[8,10,16,128]{3,2,1,0:T(8,128)S(1)} %speed.5.part_ref, f32[8,10,16,128]{3,2,1,0:T(8,128)S(1)} %bitcast.14, ...), custom_call_target="tpu_custom_call" | custom-call | flops 49152000 | bytes 2621440 | tf_op jit(solution)/shard_map/main3/pallas_call | solution.py:360
  (16 shorter events, 0.2 us)
Async XLA Ops:
  0.0 16.1 %copy-start = (f32[8,16,10,128]{3,1,2,0:T(8,128)S(1)}, f32[8,16,10,128]{3,1,2,0:T(8,128)}, u32[]{:S(2)}) copy-start(f32[8,16,10,128]{3,1,2,0:T(8,128)} %param.3) | copy-start | bytes 1966084
  4.3 31.5 %all-to-all-start = ((f32[32,1,1]{2,1,0:T(1,128)}), f32[32,1,1]{2,1,0:T(1,128)S(1)}, u32[]{:S(2)}, u32[]{:S(2)}) async-start(f32[32,1,1]{2,1,0:T(1,128)} %broadcast_in_dim.6), calls=%async_computation | async-start | bytes 32768 | tf_op jit(solution)/shard_map/all_to_all | solution.py:389
  13.7 9.5 %collective-permute-start.3 = (f32[8,10,3,128]{3,2,1,0:T(4,128)S(1)}, f32[8,10,3,128]{3,2,1,0:T(4,128)S(1)}, u32[]{:S(2)}, u32[]{:S(2)}) collective-permute-start(f32[8,10,3,128]{3,2,1,0:T(4,128)S(1)} %get-tuple-element.31), channel_id=1, source_target_pairs={{0,56},{8,0},{16,8},{24,16},{32,24},{40,32},{48,40},{56,48},{1,57}... | collective-permute-start | bytes 368648 | tf_op jit(solution)/shard_map/ppermute | solution.py:383
  16.1 21.1 %collective-permute-start.2 = (f32[8,10,3,128]{3,2,1,0:T(4,128)}, f32[8,10,3,128]{3,2,1,0:T(4,128)S(1)}, u32[]{:S(2)}, u32[]{:S(2)}) collective-permute-start(f32[8,10,3,128]{3,2,1,0:T(4,128)} %get-tuple-element.32), channel_id=1, source_target_pairs={{0,8},{8,16},{16,24},{24,32},{32,40},{40,48},{48,56},{56,0},{1,9},... | collective-permute-start | bytes 368648 | tf_op jit(solution)/shard_map/ppermute | solution.py:382
  16.2 21.1 %collective-permute-start.5 = (f32[8,3,16,128]{3,2,1,0:T(8,128)S(1)}, f32[8,3,16,128]{3,2,1,0:T(8,128)S(1)}, u32[]{:S(2)}, u32[]{:S(2)}) collective-permute-start(f32[8,3,16,128]{3,2,1,0:T(8,128)S(1)} %get-tuple-element.29), channel_id=1, source_target_pairs={{0,7},{1,0},{2,1},{3,2},{4,3},{5,4},{6,5},{7,6},{8,15},{9,8},{10,9... | collective-permute-start | bytes 589832 | tf_op jit(solution)/shard_map/ppermute | solution.py:381
  22.1 15.2 %collective-permute-start.4 = (f32[8,3,16,128]{3,2,1,0:T(8,128)S(1)}, f32[8,3,16,128]{3,2,1,0:T(8,128)S(1)}, u32[]{:S(2)}, u32[]{:S(2)}) collective-permute-start(f32[8,3,16,128]{3,2,1,0:T(8,128)S(1)} %get-tuple-element.30), channel_id=1, source_target_pairs={{0,1},{1,2},{2,3},{3,4},{4,5},{5,6},{6,7},{7,0},{8,9},{9,10},{10,1... | collective-permute-start | bytes 589832 | tf_op jit(solution)/shard_map/ppermute | solution.py:380
  22.1 15.1 %collective-permute-start.1 = (f32[3,10,16,128]{3,2,1,0:T(8,128)S(1)}, f32[3,10,16,128]{3,2,1,0:T(8,128)S(1)}, u32[]{:S(2)}, u32[]{:S(2)}) collective-permute-start(f32[3,10,16,128]{3,2,1,0:T(8,128)S(1)} %get-tuple-element.33), channel_id=1, source_target_pairs={{0,192},{64,0},{128,64},{192,128},{1,193},{65,1},{129,65},{193,129... | collective-permute-start | bytes 737288 | tf_op jit(solution)/shard_map/ppermute | solution.py:379
  23.1 2.6 %copy-start.1 = (f32[2,8,16]{2,1,0:T(8,128)S(1)}, f32[2,8,16]{2,1,0:T(8,128)}, u32[]{:S(2)}) copy-start(f32[2,8,16]{2,1,0:T(8,128)} %param.4) | copy-start | bytes 3076
  23.2 14.1 %collective-permute-start = (f32[3,10,16,128]{3,2,1,0:T(8,128)S(1)}, f32[3,10,16,128]{3,2,1,0:T(8,128)S(1)}, u32[]{:S(2)}, u32[]{:S(2)}) collective-permute-start(f32[3,10,16,128]{3,2,1,0:T(8,128)S(1)} %get-tuple-element.34), channel_id=1, source_target_pairs={{0,64},{64,128},{128,192},{192,0},{1,65},{65,129},{129,193},{193,1... | collective-permute-start | bytes 737288 | tf_op jit(solution)/shard_map/ppermute | solution.py:378
  45.4 6.6 %collective-permute-start.8 = (f32[8,10,3,128]{3,2,1,0:T(4,128)S(1)}, f32[8,10,3,128]{3,2,1,0:T(4,128)S(1)}, u32[]{:S(2)}, u32[]{:S(2)}) collective-permute-start(f32[8,10,3,128]{3,2,1,0:T(4,128)S(1)} %get-tuple-element.16), channel_id=1, source_target_pairs={{0,8},{8,16},{16,24},{24,32},{32,40},{40,48},{48,56},{56,0},{1,9},... | collective-permute-start | bytes 368648 | tf_op jit(solution)/shard_map/ppermute | solution.py:382
  45.4 18.7 %collective-permute-start.7 = (f32[3,10,16,128]{3,2,1,0:T(8,128)S(1)}, f32[3,10,16,128]{3,2,1,0:T(8,128)S(1)}, u32[]{:S(2)}, u32[]{:S(2)}) collective-permute-start(f32[3,10,16,128]{3,2,1,0:T(8,128)S(1)} %get-tuple-element.27), channel_id=1, source_target_pairs={{0,192},{64,0},{128,64},{192,128},{1,193},{65,1},{129,65},{193,129... | collective-permute-start | bytes 737288 | tf_op jit(solution)/shard_map/ppermute | solution.py:379
  45.5 18.6 %collective-permute-start.6 = (f32[3,10,16,128]{3,2,1,0:T(8,128)S(1)}, f32[3,10,16,128]{3,2,1,0:T(8,128)S(1)}, u32[]{:S(2)}, u32[]{:S(2)}) collective-permute-start(f32[3,10,16,128]{3,2,1,0:T(8,128)S(1)} %get-tuple-element.28), channel_id=1, source_target_pairs={{0,64},{64,128},{128,192},{192,0},{1,65},{65,129},{129,193},{193,1... | collective-permute-start | bytes 737288 | tf_op jit(solution)/shard_map/ppermute | solution.py:378
  48.7 15.3 %collective-permute-start.10 = (f32[8,3,16,128]{3,2,1,0:T(8,128)S(1)}, f32[8,3,16,128]{3,2,1,0:T(8,128)S(1)}, u32[]{:S(2)}, u32[]{:S(2)}) collective-permute-start(f32[8,3,16,128]{3,2,1,0:T(8,128)S(1)} %get-tuple-element.18), channel_id=1, source_target_pairs={{0,1},{1,2},{2,3},{3,4},{4,5},{5,6},{6,7},{7,0},{8,9},{9,10},{10,1... | collective-permute-start | bytes 589832 | tf_op jit(solution)/shard_map/ppermute | solution.py:380
  48.7 15.4 %collective-permute-start.11 = (f32[8,3,16,128]{3,2,1,0:T(8,128)S(1)}, f32[8,3,16,128]{3,2,1,0:T(8,128)S(1)}, u32[]{:S(2)}, u32[]{:S(2)}) collective-permute-start(f32[8,3,16,128]{3,2,1,0:T(8,128)S(1)} %get-tuple-element.19), channel_id=1, source_target_pairs={{0,7},{1,0},{2,1},{3,2},{4,3},{5,4},{6,5},{7,6},{8,15},{9,8},{10,9... | collective-permute-start | bytes 589832 | tf_op jit(solution)/shard_map/ppermute | solution.py:381
  52.0 12.1 %collective-permute-start.9 = (f32[8,10,3,128]{3,2,1,0:T(4,128)S(1)}, f32[8,10,3,128]{3,2,1,0:T(4,128)S(1)}, u32[]{:S(2)}, u32[]{:S(2)}) collective-permute-start(f32[8,10,3,128]{3,2,1,0:T(4,128)S(1)} %get-tuple-element.17), channel_id=1, source_target_pairs={{0,56},{8,0},{16,8},{24,16},{32,24},{40,32},{48,40},{56,48},{1,57}... | collective-permute-start | bytes 368648 | tf_op jit(solution)/shard_map/ppermute | solution.py:383
  72.2 6.6 %collective-permute-start.14 = (f32[8,10,3,128]{3,2,1,0:T(4,128)S(1)}, f32[8,10,3,128]{3,2,1,0:T(4,128)S(1)}, u32[]{:S(2)}, u32[]{:S(2)}) collective-permute-start(f32[8,10,3,128]{3,2,1,0:T(4,128)S(1)} %get-tuple-element.21), channel_id=1, source_target_pairs={{0,8},{8,16},{16,24},{24,32},{32,40},{40,48},{48,56},{56,0},{1,9},... | collective-permute-start | bytes 368648 | tf_op jit(solution)/shard_map/ppermute | solution.py:382
  72.2 18.4 %collective-permute-start.13 = (f32[3,10,16,128]{3,2,1,0:T(8,128)S(1)}, f32[3,10,16,128]{3,2,1,0:T(8,128)S(1)}, u32[]{:S(2)}, u32[]{:S(2)}) collective-permute-start(f32[3,10,16,128]{3,2,1,0:T(8,128)S(1)} %get-tuple-element.25), channel_id=1, source_target_pairs={{0,192},{64,0},{128,64},{192,128},{1,193},{65,1},{129,65},{193,129... | collective-permute-start | bytes 737288 | tf_op jit(solution)/shard_map/ppermute | solution.py:379
  72.3 18.3 %collective-permute-start.12 = (f32[3,10,16,128]{3,2,1,0:T(8,128)S(1)}, f32[3,10,16,128]{3,2,1,0:T(8,128)S(1)}, u32[]{:S(2)}, u32[]{:S(2)}) collective-permute-start(f32[3,10,16,128]{3,2,1,0:T(8,128)S(1)} %get-tuple-element.26), channel_id=1, source_target_pairs={{0,64},{64,128},{128,192},{192,0},{1,65},{65,129},{129,193},{193,1... | collective-permute-start | bytes 737288 | tf_op jit(solution)/shard_map/ppermute | solution.py:378
  75.5 15.1 %collective-permute-start.16 = (f32[8,3,16,128]{3,2,1,0:T(8,128)S(1)}, f32[8,3,16,128]{3,2,1,0:T(8,128)S(1)}, u32[]{:S(2)}, u32[]{:S(2)}) collective-permute-start(f32[8,3,16,128]{3,2,1,0:T(8,128)S(1)} %get-tuple-element.23), channel_id=1, source_target_pairs={{0,1},{1,2},{2,3},{3,4},{4,5},{5,6},{6,7},{7,0},{8,9},{9,10},{10,1... | collective-permute-start | bytes 589832 | tf_op jit(solution)/shard_map/ppermute | solution.py:380
  75.5 15.1 %collective-permute-start.17 = (f32[8,3,16,128]{3,2,1,0:T(8,128)S(1)}, f32[8,3,16,128]{3,2,1,0:T(8,128)S(1)}, u32[]{:S(2)}, u32[]{:S(2)}) collective-permute-start(f32[8,3,16,128]{3,2,1,0:T(8,128)S(1)} %get-tuple-element.24), channel_id=1, source_target_pairs={{0,7},{1,0},{2,1},{3,2},{4,3},{5,4},{6,5},{7,6},{8,15},{9,8},{10,9... | collective-permute-start | bytes 589832 | tf_op jit(solution)/shard_map/ppermute | solution.py:381
  78.8 11.8 %collective-permute-start.15 = (f32[8,10,3,128]{3,2,1,0:T(4,128)S(1)}, f32[8,10,3,128]{3,2,1,0:T(4,128)S(1)}, u32[]{:S(2)}, u32[]{:S(2)}) collective-permute-start(f32[8,10,3,128]{3,2,1,0:T(4,128)S(1)} %get-tuple-element.22), channel_id=1, source_target_pairs={{0,56},{8,0},{16,8},{24,16},{32,24},{40,32},{48,40},{56,48},{1,57}... | collective-permute-start | bytes 368648 | tf_op jit(solution)/shard_map/ppermute | solution.py:383

commit v2 on v1

v2 whole, which is shorter than its diff:
```python
import functools
import math

import jax
import jax.numpy as jnp
import numpy as np
from jax import lax
from jax.experimental import pallas as pl
from jax.experimental.pallas import tpu as pltpu
from jax.sharding import PartitionSpec as P


CELL_SIZE = 0.05
SPEED_LOW = 0.1
SPEED_SPAN = 0.4
TURN_MAX = 1.0
ACCEL_MAX = 0.05
CFL_NUMBER = 0.5
WENO_EPS = 1e-06

LEAN = 1.375
LEVEL = 0.625
REST = 0.609375
UP = 24


def floor_of(spacing):
    return 0.75 * WENO_EPS * spacing * spacing


def squared(value):
    return value * value


def inverse_square(value):
    return squared(1.0 / value)


def one_sided(flow, below_two, below, center, above, above_two, across, floor):
    ahead = flow > 0.0
    far = jnp.where(ahead, above_two, below_two)
    near = jnp.where(ahead, above, below)
    back = jnp.where(ahead, below, above)
    near_rest = squared(near) * REST + floor
    center_rest = squared(center) * REST + floor
    weight_one = inverse_square(squared(far - near * LEAN) + near_rest)
    weight_two = inverse_square(squared(near - center * LEVEL) + center_rest) * 6.0
    weight_three = inverse_square(squared(back - center * LEAN) + center_rest) * 3.0
    step = near - center
    fourth_here = (step - (center - back)) * (1.0 / 3.0)
    fourth_near = ((far - near) - step) * (2.0 / 3.0)
    total = weight_one + weight_two + weight_three
    shift = (weight_one * fourth_near + weight_three * fourth_here) / total - 0.5 * fourth_here
    middle = across - (above - below) * (1.0 / 6.0)
    return flow * middle + jnp.abs(flow) * shift


def column_parts(line, floor):
    rise = [line[i + 1] - line[i] for i in range(len(line) - 1)]
    bend = [rise[i + 1] - rise[i] for i in range(len(rise) - 1)]
    turn = [bend[i + 1] - bend[i] for i in range(len(bend) - 1)]
    fourth = [(turn[i + 1] - turn[i]) * (2.0 / 3.0) for i in range(len(turn) - 1)]
    count = len(line) - 6
    at = lambda j: bend[j + 2]
    rest = {j: squared(at(j)) * REST + floor for j in range(-1, count + 1)}
    lean = {j: at(j) * LEAN for j in range(-1, count + 1)}
    to_up = {j: inverse_square(squared(at(j + 1) - lean[j]) + rest[j]) for j in range(0, count + 1)}
    to_down = {j: inverse_square(squared(at(j - 1) - lean[j]) + rest[j]) for j in range(-1, count)}
    pair = {
        j: inverse_square(squared(at(j - 1) - at(j) * LEVEL) + rest[j]) * 6.0
        for j in range(0, count + 1)
    }
    middle = [
        (line[i + 4] - line[i + 2]) - (at(i + 1) - at(i - 1)) * (1.0 / 6.0) for i in range(count)
    ]
    return (lambda j: fourth[j + 1]), to_up, to_down, pair, middle


def two_sided(fourth, to_up, to_down, to_up_3, to_down_3, pair, middle, i):
    half = 0.5 * fourth(i)
    right = (to_up[i + 1] * fourth(i + 1) + to_down_3[i] * half) / (
        to_up[i + 1] + to_down_3[i] + pair[i + 1]
    )
    left = (to_down[i - 1] * fourth(i - 1) + to_up_3[i] * half) / (
        to_down[i - 1] + to_up_3[i] + pair[i]
    )
    return jnp.maximum(right + middle[i], left - middle[i]) - 0.5 * half


def picked(flow, fourth, to_up, to_down, pair, middle, i):
    ahead = flow > 0.0
    weight_one = jnp.where(ahead, to_up[i + 1], to_down[i - 1])
    weight_two = jnp.where(ahead, pair[i + 1], pair[i])
    weight_three = jnp.where(ahead, to_down[i], to_up[i]) * 3.0
    far = jnp.where(ahead, fourth(i + 1), fourth(i - 1))
    half = 0.5 * fourth(i)
    shift = (weight_one * far + weight_three * half) / (
        weight_one + weight_two + weight_three
    ) - 0.5 * half
    return flow * middle[i] + jnp.abs(flow) * shift


def speed_kernel(u_ref, out_ref, *, d_speed):
    nx, nh, ny, nv = u_ref.shape
    floor = floor_of(d_speed)
    lane = lax.broadcasted_iota(jnp.int32, (ny, nv), 1)
    first = lane == 0
    last = lane == nv - 1
    inside = jnp.logical_not(jnp.logical_or(first, last))

    def before(value):
        return pltpu.roll(value, 1, 1)

    def after(value):
        return pltpu.roll(value, nv - 1, 1)

    top = 1.0 / (floor * floor)

    def one(x, h):
        u = u_ref[x, h]
        u_before = before(u)
        u_after = after(u)
        rise_here = u - u_before
        rise_next = u_after - u
        bend = jnp.where(inside, rise_next - rise_here, 0.0)
        across = jnp.where(
            first, 2.0 * rise_next, jnp.where(last, 2.0 * rise_here, u_after - u_before)
        )
        below = before(bend)
        above = after(bend)
        rest = squared(bend) * REST + floor
        lean = bend * LEAN
        to_up = inverse_square(squared(above - lean) + rest)
        to_down = inverse_square(squared(below - lean) + rest)
        pair = inverse_square(squared(below - bend * LEVEL) + rest) * 6.0
        fourth = ((above - bend) - (bend - below)) * (2.0 / 3.0)
        half = 0.5 * fourth
        down_before = jnp.where(first, top, before(to_down))
        up_after = jnp.where(last, top, after(to_up))
        fourth_before = jnp.where(first, 0.0, before(fourth))
        fourth_after = jnp.where(last, 0.0, after(fourth))
        up_3 = to_up * 3.0
        down_3 = to_down * 3.0
        middle = across - (above - below) * (1.0 / 6.0)
        right = (up_after * fourth_after + down_3 * half) / (up_after + down_3 + after(pair))
        left = (down_before * fourth_before + up_3 * half) / (down_before + up_3 + pair)
        out_ref[x, h] = (jnp.maximum(right + middle, left - middle) - 0.5 * half) * (
            0.5 * ACCEL_MAX / d_speed
        )

    def step(x, carry):
        for h in range(nh):
            one(x, h)
        return carry

    lax.fori_loop(0, nx, step, 0)


def ghosts(edge, inner):
    slope = edge - inner
    one = edge + slope
    two = one + slope
    return one, two, two + slope


def plane_kernel(
    flag_ref, u_ref, part_ref, xlo, xhi, ylo, yhi, vel_ref, wind_ref, acc_ref, pad_ref, bend_ref
):
    nx, nh, ny, nv = u_ref.shape
    halves = ny // 8
    floor = floor_of(CELL_SIZE)
    start_x = flag_ref[0] == 1
    end_x = flag_ref[1] == 1
    start_y = flag_ref[2] == 1
    end_y = flag_ref[3] == 1
    row = lax.broadcasted_iota(jnp.int32, (3, nv), 0).astype(jnp.float32)
    reach_low = 3.0 - row
    reach_high = 1.0 + row

    def fill(x, carry):
        for h in range(nh):
            pad_ref[x, h, 8 : 8 + ny] = u_ref[x, h]
            edge = u_ref[x, h, pl.ds(0, 3, stride=0)]
            inner = u_ref[x, h, pl.ds(1, 3, stride=0)]
            pad_ref[x, h, 5:8] = jnp.where(start_y, edge + reach_low * (edge - inner), ylo[x, h])
            edge = u_ref[x, h, pl.ds(ny - 1, 3, stride=0)]
            inner = u_ref[x, h, pl.ds(ny - 2, 3, stride=0)]
            pad_ref[x, h, 8 + ny : 11 + ny] = jnp.where(
                end_y, edge + reach_high * (edge - inner), yhi[x, h]
            )
        for h in range(nh):
            for r in range(0, UP, 8):
                here = pad_ref[x, h, r + 6 : r + 14]
                bend_ref[x, h, r : r + 8] = (pad_ref[x, h, r + 7 : r + 15] - here) - (
                    here - pad_ref[x, h, r + 5 : r + 13]
                )
        return carry

    lax.fori_loop(0, nx, fill, 0)

    def along_y(x, carry):
        for h in range(nh):
            for r in range(0, ny, 8):
                flow = vel_ref[1, h] + wind_ref[1, x, r : r + 8]
                across = pad_ref[x, h, 9 + r : 17 + r] - pad_ref[x, h, 7 + r : 15 + r]
                near = [bend_ref[x, h, r + s : r + s + 8] for s in range(5)]
                acc_ref[x, h, r : r + 8] = part_ref[x, h, r : r + 8] + one_sided(
                    flow, *near, across, floor
                )
        return carry

    lax.fori_loop(0, nx, along_y, 0)

    def along_x(h, carry):
        for half in range(halves):
            rows = slice(8 * half, 8 * half + 8)
            mine = [u_ref[x, h, rows] for x in range(nx)]
            low = ghosts(mine[0], mine[1])
            high = ghosts(mine[nx - 1], mine[nx - 2])
            line = (
                [jnp.where(start_x, low[2 - r], xlo[r, h, rows]) for r in range(3)]
                + mine
                + [jnp.where(end_x, high[r], xhi[r, h, rows]) for r in range(3)]
            )
            fourth, to_up, to_down, pair, middle = column_parts(line, floor)
            speed = vel_ref[0, h]
            for x in range(nx):
                flow = speed + wind_ref[0, x, rows]
                acc_ref[x, h, rows] = acc_ref[x, h, rows] + picked(
                    flow, fourth, to_up, to_down, pair, middle, x
                )
        return carry

    lax.fori_loop(0, nh, along_x, 0)


def heading_kernel(dt_ref, u_ref, acc_ref, *refs, stage, d_theta):
    refs = list(refs)
    base_ref = refs.pop(0) if stage > 1 else None
    hlo, hhi, out_ref, *faces = refs
    nx, nh, ny, _ = u_ref.shape
    halves = ny // 8
    dt = dt_ref[0]
    theta_floor = floor_of(d_theta)

    def along_heading(x, carry):
        for half in range(halves):
            rows = slice(8 * half, 8 * half + 8)
            line = (
                [hlo[x, r, rows] for r in range(3)]
                + [u_ref[x, h, rows] for h in range(nh)]
                + [hhi[x, r, rows] for r in range(3)]
            )
            fourth, to_up, to_down, pair, middle = column_parts(line, theta_floor)
            up_3 = {j: to_up[j] * 3.0 for j in range(nh)}
            down_3 = {j: to_down[j] * 3.0 for j in range(nh)}
            for h in range(nh):
                term = two_sided(fourth, to_up, to_down, up_3, down_3, pair, middle, h)
                change = dt * jnp.minimum(
                    acc_ref[x, h, rows] + term * (0.5 * TURN_MAX / d_theta), 0.0
                )
                u = line[h + 3]
                if stage == 1:
                    value = u + change
                elif stage == 2:
                    value = 0.75 * base_ref[x, h, rows] + 0.25 * (u + change)
                else:
                    value = (2.0 / 3.0) * ((u - base_ref[x, h, rows]) + change)
                out_ref[x, h, rows] = value
                if stage < 3:
                    if h < 3:
                        faces[2][x, h, rows] = value
                    if h >= nh - 3:
                        faces[3][x, h - nh + 3, rows] = value
                    if half == 0:
                        faces[0][x, h] = value[0:3]
        if stage < 3:
            for h in range(nh):
                faces[1][x, h] = out_ref[x, h, ny - 3 : ny]
        return carry

    lax.fori_loop(0, nx, along_heading, 0)


def rate_kernel(wind_ref, out_ref, *, spots):
    wind_x = wind_ref[0]
    wind_y = wind_ref[1]
    top = None
    for move_x, move_y in spots:
        fast = jnp.abs(wind_x + move_x) + jnp.abs(wind_y + move_y)
        top = fast if top is None else jnp.maximum(top, fast)
    out_ref[...] = jnp.full(out_ref.shape, jnp.max(top), jnp.float32)


VMEM = pl.BlockSpec(memory_space=pltpu.VMEM)
SMEM = pl.BlockSpec(memory_space=pltpu.SMEM)


def ring(count, step):
    return [(i, (i + step) % count) for i in range(count)]


def body(level_set, wind_field):
    field = jnp.transpose(level_set, (0, 2, 1, 3))
    nx, nh, ny, nv = field.shape
    n_head = nh * lax.axis_size("ha")
    d_theta = 2.0 * math.pi / n_head
    d_speed = SPEED_SPAN / nv
    gx, gy = lax.axis_index("gx"), lax.axis_index("gy")
    flags = jnp.stack(
        [gx == 0, gx == lax.axis_size("gx") - 1, gy == 0, gy == lax.axis_size("gy") - 1]
    ).astype(jnp.int32)

    every_angle = np.arange(n_head, dtype=np.float32) * np.float32(d_theta)
    ends = [SPEED_LOW + SPEED_SPAN * 0.5 / nv, SPEED_LOW + SPEED_SPAN * (nv - 0.5) / nv]
    spots = [
        (float(np.float32(v) * np.cos(angle)), float(np.float32(v) * np.sin(angle)))
        for v in ends
        for angle in every_angle
    ]
    top = pl.pallas_call(
        functools.partial(rate_kernel, spots=spots),
        out_shape=jax.ShapeDtypeStruct((8, 128), jnp.float32),
        in_specs=[VMEM],
        out_specs=VMEM,
        compiler_params=pltpu.CompilerParams(vmem_limit_bytes=4 << 20),
        name="rate",
    )(wind_field)

    speeds = SPEED_LOW + SPEED_SPAN * (jnp.arange(nv, dtype=jnp.float32) + 0.5) / nv
    angles = (lax.axis_index("ha") * nh + jnp.arange(nh, dtype=jnp.int32)).astype(
        jnp.float32
    ) * d_theta
    heading = jnp.stack([jnp.cos(angles), jnp.sin(angles)])
    velocity = heading[:, :, None, None] * jnp.broadcast_to(
        speeds * (0.5 / CELL_SIZE), (2, nh, 8, nv)
    )
    wind = jnp.broadcast_to((wind_field * (0.5 / CELL_SIZE))[..., None], (2, nx, ny, nv))

    shape = jax.ShapeDtypeStruct(field.shape, jnp.float32)
    y_face = jax.ShapeDtypeStruct((nx, nh, 3, nv), jnp.float32)
    h_face = jax.ShapeDtypeStruct((nx, 3, ny, nv), jnp.float32)

    def speed_part(u):
        return pl.pallas_call(
            functools.partial(speed_kernel, d_speed=d_speed),
            out_shape=shape,
            in_specs=[VMEM],
            out_specs=VMEM,
            cost_estimate=pl.CostEstimate(
                flops=100 * nx * nh * ny * nv, bytes_accessed=8 * nx * nh * ny * nv, transcendentals=0
            ),
            compiler_params=pltpu.CompilerParams(vmem_limit_bytes=8 << 20),
            name="speed",
        )(u)

    def plane_part(u, part, xlo, xhi, ylo, yhi):
        return pl.pallas_call(
            plane_kernel,
            out_shape=shape,
            in_specs=[SMEM] + [VMEM] * 8,
            out_specs=VMEM,
            scratch_shapes=[
                pltpu.VMEM((nx, nh, ny + 16, nv), jnp.float32),
                pltpu.VMEM((nx, nh, UP, nv), jnp.float32),
            ],
            cost_estimate=pl.CostEstimate(
                flops=200 * nx * nh * ny * nv, bytes_accessed=16 * nx * nh * ny * nv, transcendentals=0
            ),
            compiler_params=pltpu.CompilerParams(vmem_limit_bytes=24 << 20),
            name="plane",
        )(flags, u, part, xlo, xhi, ylo, yhi, velocity, wind)

    def heading_part(stage, u, acc, hlo, hhi):
        outs = [shape]
        if stage < 3:
            outs += [y_face, y_face, h_face, h_face]
        ins = [time_step, u, acc] + ([field] if stage > 1 else []) + [hlo, hhi]
        return pl.pallas_call(
            functools.partial(heading_kernel, stage=stage, d_theta=d_theta),
            out_shape=outs,
            in_specs=[SMEM] + [VMEM] * (len(ins) - 1),
            out_specs=[VMEM] * len(outs),
            cost_estimate=pl.CostEstimate(
                flops=100 * nx * nh * ny * nv, bytes_accessed=16 * nx * nh * ny * nv, transcendentals=0
            ),
            compiler_params=pltpu.CompilerParams(vmem_limit_bytes=24 << 20),
        )(*ins)

    def exchange(u, y_first, y_last, h_first, h_last):
        def halo(value, axis, step):
            return lax.ppermute(value, axis, ring(lax.axis_size(axis), step))

        xlo = halo(u[nx - 3 :], "gx", 1)
        xhi = halo(u[:3], "gx", -1)
        ylo = halo(y_last, "gy", 1)
        yhi = halo(y_first, "gy", -1)
        hlo = halo(h_last, "ha", 1)
        hhi = halo(h_first, "ha", -1)
        return xlo, xhi, ylo, yhi, hlo, hhi

    for axis, bit in [("gx", 1), ("gx", 2), ("gy", 1), ("gy", 2), ("gy", 4)]:
        other = lax.ppermute(top, axis, [(j, j ^ bit) for j in range(lax.axis_size(axis))])
        top = jnp.maximum(top, other)
    top_rate = top[0, :1] / CELL_SIZE + TURN_MAX / d_theta + ACCEL_MAX / d_speed
    time_step = CFL_NUMBER / top_rate

    u = field
    faces = (field[:, :, :3], field[:, :, ny - 3 :], field[:, :3], field[:, nh - 3 :])
    for stage in (1, 2, 3):
        xlo, xhi, ylo, yhi, hlo, hhi = exchange(u, *faces)
        part = speed_part(u)
        acc = plane_part(u, part, xlo, xhi, ylo, yhi)
        u, *faces = heading_part(stage, u, acc, hlo, hhi)
    return jnp.transpose(u, (0, 2, 1, 3))


def solution(mesh):
    return jax.shard_map(
        body,
        mesh=mesh,
        in_specs=(P("gx", "gy", "ha", None), P(None, "gx", "gy")),
        out_specs=P("gx", "gy", "ha", None),
        check_vma=False,
    )
```

time: 99.1 us -> 74.9 us (0.76)
  the two profiles are of different devices: /device:TPU:6 before, /device:TPU:25 now
where the time goes in v2:
time: 74.9 us; the launch traced here: 74.7 us
  starting transfers between devices  30.8 us (41%)
  Pallas kernels  24.8 us (33%)
  waiting for transfers between devices  15.4 us (21%)
  local copies, waits for them, and re-layouts  2.56 us (3%)
  between operations  0.94 us (1%)
    ppermute x18, starting transfers between devices, halo(): return lax.ppermute(value, axis, ring(lax.axis_size(axis), step))  25.9 us
    pallas_call x3, Pallas kernels, plane_part(): pl.pallas_call(plane_kernel, out_shape=shape, in_specs=[SMEM] + [VMEM] *...  10.9 us
    pallas_call x3, Pallas kernels, speed_part(): pl.pallas_call(functools.partial(speed_kernel, d_speed=d_speed), out_shap...  8.1 us
    ppermute x5, waiting for transfers between devices, body(): lax.ppermute(top, axis, [(j, j ^ bit) for j in range(lax.axis_size(axis))])  7.96 us
    ppermute x18, waiting for transfers between devices, halo(): return lax.ppermute(value, axis, ring(lax.axis_size(axis), step))  7.42 us
    pallas_call x3, Pallas kernels, heading_part(): pl.pallas_call(functools.partial(heading_kernel, stage=stage, d_theta=d_t...  5.52 us
    ppermute x5, starting transfers between devices, body(): lax.ppermute(top, axis, [(j, j ^ bit) for j in range(lax.axis_size(axis))])  4.82 us
  transfers between devices with their start and end apart: 23, of which 7 were waited for; matrix products, arithmetic and copies ran while one was open for 3% of the time, Pallas kernels for 25%

profile of v2, /device:TPU:25, one launch (start us, length us, event | category | flops | bytes accessed | tf_op | source)
XLA Modules:
  0.0 74.7 jit_solution(42018420773523013)
XLA Ops:
  0.0 0.7 copy-done.1
  0.7 0.3 rate.1
  1.0 1.3 %collective-permute-start = (f32[8,128]{1,0:T(8,128)S(1)}, f32[8,128]{1,0:T(8,128)S(1)}, u32[]{:S(2)}, u32[]{:S(2)}) collective-permute-start(f32[8,128]{1,0:T(8,128)S(1)} %rate.1), channel_id=1, source_target_pairs={{0,64},{64,0},{128,192},{192,128},{1,65},{65,1},{129,193},{193,129... | collective-permute-start | bytes 12296 | tf_op jit(solution)/shard_map/ppermute | solution.py:403
  2.3 1.1 %fusion.5 = (f32[8,10,3,128]{3,2,1,0:T(4,128)S(1)}, f32[8,10,3,128]{3,2,1,0:T(4,128)S(1)}) fusion(f32[8,10,16,128]{3,2,1,0:T(8,128)} %bitcast.7), kind=kLoop, calls=%fused_computation.11 | loop fusion | bytes 491520 | tf_op jit(solution)/shard_map/slice | solution.py:409
  3.4 1.0 %collective-permute-start.8 = (f32[8,10,3,128]{3,2,1,0:T(4,128)S(1)}, f32[8,10,3,128]{3,2,1,0:T(4,128)S(1)}, u32[]{:S(2)}, u32[]{:S(2)}) collective-permute-start(f32[8,10,3,128]{3,2,1,0:T(4,128)S(1)} %get-tuple-element.31), channel_id=1, source_target_pairs={{0,56},{8,0},{16,8},{24,16},{32,24},{40,32},{48,40},{56,48},{1,57}... | collective-permute-start | bytes 368648 | tf_op jit(solution)/shard_map/ppermute | solution.py:392
  4.4 2.0 %collective-permute-start.7 = (f32[8,10,3,128]{3,2,1,0:T(4,128)S(1)}, f32[8,10,3,128]{3,2,1,0:T(4,128)S(1)}, u32[]{:S(2)}, u32[]{:S(2)}) collective-permute-start(f32[8,10,3,128]{3,2,1,0:T(4,128)S(1)} %get-tuple-element.32), channel_id=1, source_target_pairs={{0,8},{8,16},{16,24},{24,32},{32,40},{40,48},{48,56},{56,0},{1,9},... | collective-permute-start | bytes 368648 | tf_op jit(solution)/shard_map/ppermute | solution.py:392
  6.4 5.7 %collective-permute-start.10 = (f32[8,3,16,128]{3,2,1,0:T(8,128)S(1)}, f32[8,3,16,128]{3,2,1,0:T(8,128)S(1)}, u32[]{:S(2)}, u32[]{:S(2)}) collective-permute-start(f32[8,3,16,128]{3,2,1,0:T(8,128)S(1)} %get-tuple-element.29), channel_id=1, source_target_pairs={{0,7},{1,0},{2,1},{3,2},{4,3},{5,4},{6,5},{7,6},{8,15},{9,8},{10,9... | collective-permute-start | bytes 589832 | tf_op jit(solution)/shard_map/ppermute | solution.py:392
  12.2 2.5 %collective-permute-start.1 = (f32[8,128]{1,0:T(8,128)S(1)}, f32[8,128]{1,0:T(8,128)S(1)}, u32[]{:S(2)}, u32[]{:S(2)}) collective-permute-start(f32[8,128]{1,0:T(8,128)S(1)} %max.15), channel_id=1, source_target_pairs={{0,128},{64,192},{128,0},{192,64},{1,129},{65,193},{129,1},{193,65... | collective-permute-start | bytes 12296 | tf_op jit(solution)/shard_map/ppermute | solution.py:403
  14.7 1.5 %collective-permute-done.1 = f32[8,128]{1,0:T(8,128)S(1)} collective-permute-done((f32[8,128]{1,0:T(8,128)S(1)}, f32[8,128]{1,0:T(8,128)S(1)}, u32[]{:S(2)}, u32[]{:S(2)}) %collective-permute-start.1) | collective-permute-done | bytes 4128 | tf_op jit(solution)/shard_map/ppermute | solution.py:403
  16.2 0.0 collective-permute-start.2
  16.2 1.2 %collective-permute-done.2 = f32[8,128]{1,0:T(8,128)S(1)} collective-permute-done((f32[8,128]{1,0:T(8,128)S(1)}, f32[8,128]{1,0:T(8,128)S(1)}, u32[]{:S(2)}, u32[]{:S(2)}) %collective-permute-start.2) | collective-permute-done | bytes 4128 | tf_op jit(solution)/shard_map/ppermute | solution.py:403
  17.4 0.1 collective-permute-start.3
  17.4 2.4 %collective-permute-done.3 = f32[8,128]{1,0:T(8,128)S(1)} collective-permute-done((f32[8,128]{1,0:T(8,128)S(1)}, f32[8,128]{1,0:T(8,128)S(1)}, u32[]{:S(2)}, u32[]{:S(2)}) %collective-permute-start.3) | collective-permute-done | bytes 4128 | tf_op jit(solution)/shard_map/ppermute | solution.py:403
  19.8 0.9 %collective-permute-start.4 = (f32[8,128]{1,0:T(8,128)S(1)}, f32[8,128]{1,0:T(8,128)S(1)}, u32[]{:S(2)}, u32[]{:S(2)}) collective-permute-start(f32[8,128]{1,0:T(8,128)S(1)} %max.18), channel_id=1, source_target_pairs={{0,32},{8,40},{16,48},{24,56},{32,0},{40,8},{48,16},{56,24},{1,33}... | collective-permute-start | bytes 12296 | tf_op jit(solution)/shard_map/ppermute | solution.py:403
  20.8 0.1 broadcast_multiply_fusion.vel_ref
  20.9 2.9 %collective-permute-done.4 = f32[8,128]{1,0:T(8,128)S(1)} collective-permute-done((f32[8,128]{1,0:T(8,128)S(1)}, f32[8,128]{1,0:T(8,128)S(1)}, u32[]{:S(2)}, u32[]{:S(2)}) %collective-permute-start.4) | collective-permute-done | bytes 4128 | tf_op jit(solution)/shard_map/ppermute | solution.py:403
  23.8 1.8 %collective-permute-start.6 = (f32[3,10,16,128]{3,2,1,0:T(8,128)S(1)}, f32[3,10,16,128]{3,2,1,0:T(8,128)S(1)}, u32[]{:S(2)}, u32[]{:S(2)}) collective-permute-start(f32[3,10,16,128]{3,2,1,0:T(8,128)S(1)} %get-tuple-element.33), channel_id=1, source_target_pairs={{0,192},{64,0},{128,64},{192,128},{1,193},{65,1},{129,65},{193,129... | collective-permute-start | bytes 737288 | tf_op jit(solution)/shard_map/ppermute | solution.py:392
  25.7 2.7 %speed.3.part_ref = f32[8,10,16,128]{3,2,1,0:T(8,128)S(1)} custom-call(f32[8,10,16,128]{3,2,1,0:T(8,128)S(1)} %bitcast.10), custom_call_target="tpu_custom_call" | custom-call | flops 16384000 | bytes 1310720 | tf_op jit(solution)/shard_map/speed/pallas_call | solution.py:345
  28.4 0.1 add_convert_fusion.flag_ref
  28.4 0.5 slice.33
  29.7 0.0 collective-permute-done.7.ylo
  29.7 2.2 %collective-permute-done.5.xlo = f32[3,10,16,128]{3,2,1,0:T(8,128)S(1)} collective-permute-done((f32[3,10,16,128]{3,2,1,0:T(8,128)S(1)}, f32[3,10,16,128]{3,2,1,0:T(8,128)S(1)}, u32[]{:S(2)}, u32[]{:S(2)}) %collective-permute-start.5) | collective-permute-done | bytes 245792 | tf_op jit(solution)/shard_map/ppermute | solution.py:392
  31.9 0.1 broadcast_in_dim.5.wind_ref
  32.0 3.6 %plane.3.acc_ref = f32[8,10,16,128]{3,2,1,0:T(8,128)S(1)} custom-call(s32[4]{0:T(128)S(1)} %add_convert_fusion.flag_ref, f32[8,10,16,128]{3,2,1,0:T(8,128)S(1)} %bitcast.11, f32[8,10,16,128]{3,2,1,0:T(8,128)S(1)} %speed.3.part_ref, f32[3,10,16,128]{3,2,1,0:T(8,128)S(1)} %collective-permute-done.5.xlo, f32[3,10,16,128]{3,2,1,0:T(8,128)S(1)} %collective-permute-done.6.xhi, ...), custom_call_target="tpu_custom_call" | custom-call | flops 32768000 | bytes 2621440 | tf_op jit(solution)/shard_map/plane/pallas_call | solution.py:358
  35.6 0.0 collective-permute-done.9.refs_0_
  35.6 1.6 %shard_map.28 = (f32[8,10,16,128]{3,2,1,0:T(8,128)S(1)}, f32[8,10,3,128]{3,2,1,0:T(4,128)S(1)}, f32[8,10,3,128]{3,2,1,0:T(4,128)S(1)}, f32[8,3,16,128]{3,2,1,0:T(8,128)S(1)}, f32[8,3,16,128]{3,2,1,0:T(8,128)S(1)}) custom-call(f32[1]{0:T(128)} %bitcast.dt_ref, f32[8,10,16,128]{3,2,1,0:T(8,128)S(1)} %bitcast.12, f32[8,10,16,128]{3,2,1,0:T(8,128)S(1)} %plane.3.acc_ref, ...), custom_call_target="tpu_custom_call" | custom-call | flops 16384000 | bytes 2621440 | tf_op jit(solution)/shard_map/pallas_call | solution.py:379
  37.2 5.2 %collective-permute-start.13 = (f32[8,10,3,128]{3,2,1,0:T(4,128)S(1)}, f32[8,10,3,128]{3,2,1,0:T(4,128)S(1)}, u32[]{:S(2)}, u32[]{:S(2)}) collective-permute-start(f32[8,10,3,128]{3,2,1,0:T(4,128)S(1)} %get-tuple-element.16), channel_id=1, source_target_pairs={{0,8},{8,16},{16,24},{24,32},{32,40},{40,48},{48,56},{56,0},{1,9},... | collective-permute-start | bytes 368648 | tf_op jit(solution)/shard_map/ppermute | solution.py:392
  42.4 0.1 collective-permute-start.12
  42.5 1.5 %collective-permute-start.11 = (f32[3,10,16,128]{3,2,1,0:T(8,128)S(1)}, f32[3,10,16,128]{3,2,1,0:T(8,128)S(1)}, u32[]{:S(2)}, u32[]{:S(2)}) collective-permute-start(f32[3,10,16,128]{3,2,1,0:T(8,128)S(1)} %get-tuple-element.28), channel_id=1, source_target_pairs={{0,64},{64,128},{128,192},{192,0},{1,65},{65,129},{129,193},{193,1... | collective-permute-start | bytes 737288 | tf_op jit(solution)/shard_map/ppermute | solution.py:392
  44.0 0.0 collective-permute-start.15
  44.0 3.0 %collective-permute-start.16 = (f32[8,3,16,128]{3,2,1,0:T(8,128)S(1)}, f32[8,3,16,128]{3,2,1,0:T(8,128)S(1)}, u32[]{:S(2)}, u32[]{:S(2)}) collective-permute-start(f32[8,3,16,128]{3,2,1,0:T(8,128)S(1)} %get-tuple-element.19), channel_id=1, source_target_pairs={{0,7},{1,0},{2,1},{3,2},{4,3},{5,4},{6,5},{7,6},{8,15},{9,8},{10,9... | collective-permute-start | bytes 589832 | tf_op jit(solution)/shard_map/ppermute | solution.py:392
  46.9 0.0 collective-permute-done.13.ylo
  46.9 0.0 collective-permute-start.14
  46.9 2.7 %speed.4.part_ref = f32[8,10,16,128]{3,2,1,0:T(8,128)S(1)} custom-call(f32[8,10,16,128]{3,2,1,0:T(8,128)S(1)} %get-tuple-element.15.u_ref), custom_call_target="tpu_custom_call" | custom-call | flops 16384000 | bytes 1310720 | tf_op jit(solution)/shard_map/speed/pallas_call | solution.py:345
  49.6 3.2 %collective-permute-done.14.yhi = f32[8,10,3,128]{3,2,1,0:T(4,128)S(1)} collective-permute-done((f32[8,10,3,128]{3,2,1,0:T(4,128)S(1)}, f32[8,10,3,128]{3,2,1,0:T(4,128)S(1)}, u32[]{:S(2)}, u32[]{:S(2)}) %collective-permute-start.14) | collective-permute-done | bytes 122912 | tf_op jit(solution)/shard_map/ppermute | solution.py:392
  52.9 0.0 collective-permute-done.11.xlo
  52.9 3.6 %plane.4.acc_ref = f32[8,10,16,128]{3,2,1,0:T(8,128)S(1)} custom-call(s32[4]{0:T(128)S(1)} %add_convert_fusion.flag_ref, f32[8,10,16,128]{3,2,1,0:T(8,128)S(1)} %get-tuple-element.15.u_ref, f32[8,10,16,128]{3,2,1,0:T(8,128)S(1)} %speed.4.part_ref, f32[3,10,16,128]{3,2,1,0:T(8,128)S(1)} %collective-permute-done.11.xlo, ...), custom_call_target="tpu_custom_call" | custom-call | flops 32768000 | bytes 2621440 | tf_op jit(solution)/shard_map/plane/pallas_call | solution.py:358
  56.5 1.6 %shard_map.29 = (f32[8,10,16,128]{3,2,1,0:T(8,128)S(1)}, f32[8,10,3,128]{3,2,1,0:T(4,128)S(1)}, f32[8,10,3,128]{3,2,1,0:T(4,128)S(1)}, f32[8,3,16,128]{3,2,1,0:T(8,128)S(1)}, f32[8,3,16,128]{3,2,1,0:T(8,128)S(1)}) custom-call(f32[1]{0:T(128)} %bitcast.dt_ref, f32[8,10,16,128]{3,2,1,0:T(8,128)S(1)} %get-tuple-element.15.u_ref, ...), custom_call_target="tpu_custom_call" | custom-call | flops 16384000 | bytes 2621440 | tf_op jit(solution)/shard_map/pallas_call | solution.py:379
  58.2 0.0 collective-permute-start.19
  58.3 1.4 %collective-permute-start.18 = (f32[3,10,16,128]{3,2,1,0:T(8,128)S(1)}, f32[3,10,16,128]{3,2,1,0:T(8,128)S(1)}, u32[]{:S(2)}, u32[]{:S(2)}) collective-permute-start(f32[3,10,16,128]{3,2,1,0:T(8,128)S(1)} %get-tuple-element.25), channel_id=1, source_target_pairs={{0,192},{64,0},{128,64},{192,128},{1,193},{65,1},{129,65},{193,129... | collective-permute-start | bytes 737288 | tf_op jit(solution)/shard_map/ppermute | solution.py:392
  59.6 0.2 collective-permute-start.17
  59.8 0.0 collective-permute-start.21
  59.8 2.7 %collective-permute-start.22 = (f32[8,3,16,128]{3,2,1,0:T(8,128)S(1)}, f32[8,3,16,128]{3,2,1,0:T(8,128)S(1)}, u32[]{:S(2)}, u32[]{:S(2)}) collective-permute-start(f32[8,3,16,128]{3,2,1,0:T(8,128)S(1)} %get-tuple-element.24), channel_id=1, source_target_pairs={{0,7},{1,0},{2,1},{3,2},{4,3},{5,4},{6,5},{7,6},{8,15},{9,8},{10,9... | collective-permute-start | bytes 589832 | tf_op jit(solution)/shard_map/ppermute | solution.py:392
  62.5 1.6 %collective-permute-start.20 = (f32[8,10,3,128]{3,2,1,0:T(4,128)S(1)}, f32[8,10,3,128]{3,2,1,0:T(4,128)S(1)}, u32[]{:S(2)}, u32[]{:S(2)}) collective-permute-start(f32[8,10,3,128]{3,2,1,0:T(4,128)S(1)} %get-tuple-element.22), channel_id=1, source_target_pairs={{0,56},{8,0},{16,8},{24,16},{32,24},{40,32},{48,40},{56,48},{1,57}... | collective-permute-start | bytes 368648 | tf_op jit(solution)/shard_map/ppermute | solution.py:392
  64.1 2.7 %speed.5.part_ref = f32[8,10,16,128]{3,2,1,0:T(8,128)S(1)} custom-call(f32[8,10,16,128]{3,2,1,0:T(8,128)S(1)} %get-tuple-element.20.u_ref), custom_call_target="tpu_custom_call" | custom-call | flops 16384000 | bytes 1310720 | tf_op jit(solution)/shard_map/speed/pallas_call | solution.py:345
  66.8 1.9 %collective-permute-done.20.yhi = f32[8,10,3,128]{3,2,1,0:T(4,128)S(1)} collective-permute-done((f32[8,10,3,128]{3,2,1,0:T(4,128)S(1)}, f32[8,10,3,128]{3,2,1,0:T(4,128)S(1)}, u32[]{:S(2)}, u32[]{:S(2)}) %collective-permute-start.20) | collective-permute-done | bytes 122912 | tf_op jit(solution)/shard_map/ppermute | solution.py:392
  68.7 3.6 %plane.5.acc_ref = f32[8,10,16,128]{3,2,1,0:T(8,128)S(1)} custom-call(s32[4]{0:T(128)S(1)} %add_convert_fusion.flag_ref, f32[8,10,16,128]{3,2,1,0:T(8,128)S(1)} %get-tuple-element.20.u_ref, f32[8,10,16,128]{3,2,1,0:T(8,128)S(1)} %speed.5.part_ref, f32[3,10,16,128]{3,2,1,0:T(8,128)S(1)} %collective-permute-done.17.xlo, ...), custom_call_target="tpu_custom_call" | custom-call | flops 32768000 | bytes 2621440 | tf_op jit(solution)/shard_map/plane/pallas_call | solution.py:358
  72.4 2.3 %shard_map.30 = f32[8,10,16,128]{3,2,1,0:T(8,128)} custom-call(f32[1]{0:T(128)} %bitcast.dt_ref, f32[8,10,16,128]{3,2,1,0:T(8,128)S(1)} %get-tuple-element.20.u_ref, f32[8,10,16,128]{3,2,1,0:T(8,128)S(1)} %plane.5.acc_ref, f32[8,10,16,128]{3,2,1,0:T(8,128)S(1)} %bitcast.14, f32[8,3,16,128]{3,2,1,0:T(8,128)S(1)} %collective-permute-done.21.refs_1_, ...), custom_call_target="tpu_custom_call" | custom-call | flops 16384000 | bytes 2621440 | tf_op jit(solution)/shard_map/pallas_call | solution.py:379
  (32 shorter events, 0.3 us)
Async XLA Ops:
  0.0 0.7 copy-start.1
  0.7 5.7 %copy-start = (f32[8,16,10,128]{3,1,2,0:T(8,128)S(1)}, f32[8,16,10,128]{3,1,2,0:T(8,128)}, u32[]{:S(2)}) copy-start(f32[8,16,10,128]{3,1,2,0:T(8,128)} %param.2) | copy-start | bytes 1966084
  1.0 11.1 %collective-permute-start = (f32[8,128]{1,0:T(8,128)S(1)}, f32[8,128]{1,0:T(8,128)S(1)}, u32[]{:S(2)}, u32[]{:S(2)}) collective-permute-start(f32[8,128]{1,0:T(8,128)S(1)} %rate.1), channel_id=1, source_target_pairs={{0,64},{64,0},{128,192},{192,128},{1,65},{65,1},{129,193},{193,129... | collective-permute-start | bytes 12296 | tf_op jit(solution)/shard_map/ppermute | solution.py:403
  3.4 22.2 %collective-permute-start.8 = (f32[8,10,3,128]{3,2,1,0:T(4,128)S(1)}, f32[8,10,3,128]{3,2,1,0:T(4,128)S(1)}, u32[]{:S(2)}, u32[]{:S(2)}) collective-permute-start(f32[8,10,3,128]{3,2,1,0:T(4,128)S(1)} %get-tuple-element.31), channel_id=1, source_target_pairs={{0,56},{8,0},{16,8},{24,16},{32,24},{40,32},{48,40},{56,48},{1,57}... | collective-permute-start | bytes 368648 | tf_op jit(solution)/shard_map/ppermute | solution.py:392
  4.4 25.3 %collective-permute-start.7 = (f32[8,10,3,128]{3,2,1,0:T(4,128)S(1)}, f32[8,10,3,128]{3,2,1,0:T(4,128)S(1)}, u32[]{:S(2)}, u32[]{:S(2)}) collective-permute-start(f32[8,10,3,128]{3,2,1,0:T(4,128)S(1)} %get-tuple-element.32), channel_id=1, source_target_pairs={{0,8},{8,16},{16,24},{24,32},{32,40},{40,48},{48,56},{56,0},{1,9},... | collective-permute-start | bytes 368648 | tf_op jit(solution)/shard_map/ppermute | solution.py:392
  6.4 29.2 %collective-permute-start.10 = (f32[8,3,16,128]{3,2,1,0:T(8,128)S(1)}, f32[8,3,16,128]{3,2,1,0:T(8,128)S(1)}, u32[]{:S(2)}, u32[]{:S(2)}) collective-permute-start(f32[8,3,16,128]{3,2,1,0:T(8,128)S(1)} %get-tuple-element.29), channel_id=1, source_target_pairs={{0,7},{1,0},{2,1},{3,2},{4,3},{5,4},{6,5},{7,6},{8,15},{9,8},{10,9... | collective-permute-start | bytes 589832 | tf_op jit(solution)/shard_map/ppermute | solution.py:392
  12.1 23.6 %collective-permute-start.9 = (f32[8,3,16,128]{3,2,1,0:T(8,128)S(1)}, f32[8,3,16,128]{3,2,1,0:T(8,128)S(1)}, u32[]{:S(2)}, u32[]{:S(2)}) collective-permute-start(f32[8,3,16,128]{3,2,1,0:T(8,128)S(1)} %get-tuple-element.30), channel_id=1, source_target_pairs={{0,1},{1,2},{2,3},{3,4},{4,5},{5,6},{6,7},{7,0},{8,9},{9,10},{10,1... | collective-permute-start | bytes 589832 | tf_op jit(solution)/shard_map/ppermute | solution.py:392
  12.2 4.0 %collective-permute-start.1 = (f32[8,128]{1,0:T(8,128)S(1)}, f32[8,128]{1,0:T(8,128)S(1)}, u32[]{:S(2)}, u32[]{:S(2)}) collective-permute-start(f32[8,128]{1,0:T(8,128)S(1)} %max.15), channel_id=1, source_target_pairs={{0,128},{64,192},{128,0},{192,64},{1,129},{65,193},{129,1},{193,65... | collective-permute-start | bytes 12296 | tf_op jit(solution)/shard_map/ppermute | solution.py:403
  16.2 1.2 %collective-permute-start.2 = (f32[8,128]{1,0:T(8,128)S(1)}, f32[8,128]{1,0:T(8,128)S(1)}, u32[]{:S(2)}, u32[]{:S(2)}) collective-permute-start(f32[8,128]{1,0:T(8,128)S(1)} %max.16), channel_id=1, source_target_pairs={{0,8},{8,0},{16,24},{24,16},{32,40},{40,32},{48,56},{56,48},{1,9},... | collective-permute-start | bytes 12296 | tf_op jit(solution)/shard_map/ppermute | solution.py:403
  17.4 2.5 %collective-permute-start.3 = (f32[8,128]{1,0:T(8,128)S(1)}, f32[8,128]{1,0:T(8,128)S(1)}, u32[]{:S(2)}, u32[]{:S(2)}) collective-permute-start(f32[8,128]{1,0:T(8,128)S(1)} %max.17), channel_id=1, source_target_pairs={{0,16},{8,24},{16,0},{24,8},{32,48},{40,56},{48,32},{56,40},{1,17}... | collective-permute-start | bytes 12296 | tf_op jit(solution)/shard_map/ppermute | solution.py:403
  19.8 4.0 %collective-permute-start.4 = (f32[8,128]{1,0:T(8,128)S(1)}, f32[8,128]{1,0:T(8,128)S(1)}, u32[]{:S(2)}, u32[]{:S(2)}) collective-permute-start(f32[8,128]{1,0:T(8,128)S(1)} %max.18), channel_id=1, source_target_pairs={{0,32},{8,40},{16,48},{24,56},{32,0},{40,8},{48,16},{56,24},{1,33}... | collective-permute-start | bytes 12296 | tf_op jit(solution)/shard_map/ppermute | solution.py:403
  20.8 4.9 %copy-start.2 = (f32[2,8,16]{2,1,0:T(8,128)S(1)}, f32[2,8,16]{2,1,0:T(8,128)}, u32[]{:S(2)}) copy-start(f32[2,8,16]{2,1,0:T(8,128)} %wind_ref.1) | copy-start | bytes 3076
  23.8 5.9 %collective-permute-start.6 = (f32[3,10,16,128]{3,2,1,0:T(8,128)S(1)}, f32[3,10,16,128]{3,2,1,0:T(8,128)S(1)}, u32[]{:S(2)}, u32[]{:S(2)}) collective-permute-start(f32[3,10,16,128]{3,2,1,0:T(8,128)S(1)} %get-tuple-element.33), channel_id=1, source_target_pairs={{0,192},{64,0},{128,64},{192,128},{1,193},{65,1},{129,65},{193,129... | collective-permute-start | bytes 737288 | tf_op jit(solution)/shard_map/ppermute | solution.py:392
  25.6 6.3 %collective-permute-start.5 = (f32[3,10,16,128]{3,2,1,0:T(8,128)S(1)}, f32[3,10,16,128]{3,2,1,0:T(8,128)S(1)}, u32[]{:S(2)}, u32[]{:S(2)}) collective-permute-start(f32[3,10,16,128]{3,2,1,0:T(8,128)S(1)} %get-tuple-element.34), channel_id=1, source_target_pairs={{0,64},{64,128},{128,192},{192,0},{1,65},{65,129},{129,193},{193,1... | collective-permute-start | bytes 737288 | tf_op jit(solution)/shard_map/ppermute | solution.py:392
  37.2 9.7 %collective-permute-start.13 = (f32[8,10,3,128]{3,2,1,0:T(4,128)S(1)}, f32[8,10,3,128]{3,2,1,0:T(4,128)S(1)}, u32[]{:S(2)}, u32[]{:S(2)}) collective-permute-start(f32[8,10,3,128]{3,2,1,0:T(4,128)S(1)} %get-tuple-element.16), channel_id=1, source_target_pairs={{0,8},{8,16},{16,24},{24,32},{32,40},{40,48},{48,56},{56,0},{1,9},... | collective-permute-start | bytes 368648 | tf_op jit(solution)/shard_map/ppermute | solution.py:392
  42.4 10.5 %collective-permute-start.12 = (f32[3,10,16,128]{3,2,1,0:T(8,128)S(1)}, f32[3,10,16,128]{3,2,1,0:T(8,128)S(1)}, u32[]{:S(2)}, u32[]{:S(2)}) collective-permute-start(f32[3,10,16,128]{3,2,1,0:T(8,128)S(1)} %get-tuple-element.27), channel_id=1, source_target_pairs={{0,192},{64,0},{128,64},{192,128},{1,193},{65,1},{129,65},{193,129... | collective-permute-start | bytes 737288 | tf_op jit(solution)/shard_map/ppermute | solution.py:392
  42.5 10.4 %collective-permute-start.11 = (f32[3,10,16,128]{3,2,1,0:T(8,128)S(1)}, f32[3,10,16,128]{3,2,1,0:T(8,128)S(1)}, u32[]{:S(2)}, u32[]{:S(2)}) collective-permute-start(f32[3,10,16,128]{3,2,1,0:T(8,128)S(1)} %get-tuple-element.28), channel_id=1, source_target_pairs={{0,64},{64,128},{128,192},{192,0},{1,65},{65,129},{129,193},{193,1... | collective-permute-start | bytes 737288 | tf_op jit(solution)/shard_map/ppermute | solution.py:392
  44.0 12.6 %collective-permute-start.15 = (f32[8,3,16,128]{3,2,1,0:T(8,128)S(1)}, f32[8,3,16,128]{3,2,1,0:T(8,128)S(1)}, u32[]{:S(2)}, u32[]{:S(2)}) collective-permute-start(f32[8,3,16,128]{3,2,1,0:T(8,128)S(1)} %get-tuple-element.18), channel_id=1, source_target_pairs={{0,1},{1,2},{2,3},{3,4},{4,5},{5,6},{6,7},{7,0},{8,9},{9,10},{10,1... | collective-permute-start | bytes 589832 | tf_op jit(solution)/shard_map/ppermute | solution.py:392
  44.0 12.6 %collective-permute-start.16 = (f32[8,3,16,128]{3,2,1,0:T(8,128)S(1)}, f32[8,3,16,128]{3,2,1,0:T(8,128)S(1)}, u32[]{:S(2)}, u32[]{:S(2)}) collective-permute-start(f32[8,3,16,128]{3,2,1,0:T(8,128)S(1)} %get-tuple-element.19), channel_id=1, source_target_pairs={{0,7},{1,0},{2,1},{3,2},{4,3},{5,4},{6,5},{7,6},{8,15},{9,8},{10,9... | collective-permute-start | bytes 589832 | tf_op jit(solution)/shard_map/ppermute | solution.py:392
  46.9 6.0 %collective-permute-start.14 = (f32[8,10,3,128]{3,2,1,0:T(4,128)S(1)}, f32[8,10,3,128]{3,2,1,0:T(4,128)S(1)}, u32[]{:S(2)}, u32[]{:S(2)}) collective-permute-start(f32[8,10,3,128]{3,2,1,0:T(4,128)S(1)} %get-tuple-element.17), channel_id=1, source_target_pairs={{0,56},{8,0},{16,8},{24,16},{32,24},{40,32},{48,40},{56,48},{1,57}... | collective-permute-start | bytes 368648 | tf_op jit(solution)/shard_map/ppermute | solution.py:392
  58.2 4.3 %collective-permute-start.19 = (f32[8,10,3,128]{3,2,1,0:T(4,128)S(1)}, f32[8,10,3,128]{3,2,1,0:T(4,128)S(1)}, u32[]{:S(2)}, u32[]{:S(2)}) collective-permute-start(f32[8,10,3,128]{3,2,1,0:T(4,128)S(1)} %get-tuple-element.21), channel_id=1, source_target_pairs={{0,8},{8,16},{16,24},{24,32},{32,40},{40,48},{48,56},{56,0},{1,9},... | collective-permute-start | bytes 368648 | tf_op jit(solution)/shard_map/ppermute | solution.py:392
  58.3 10.5 %collective-permute-start.18 = (f32[3,10,16,128]{3,2,1,0:T(8,128)S(1)}, f32[3,10,16,128]{3,2,1,0:T(8,128)S(1)}, u32[]{:S(2)}, u32[]{:S(2)}) collective-permute-start(f32[3,10,16,128]{3,2,1,0:T(8,128)S(1)} %get-tuple-element.25), channel_id=1, source_target_pairs={{0,192},{64,0},{128,64},{192,128},{1,193},{65,1},{129,65},{193,129... | collective-permute-start | bytes 737288 | tf_op jit(solution)/shard_map/ppermute | solution.py:392
  59.6 9.1 %collective-permute-start.17 = (f32[3,10,16,128]{3,2,1,0:T(8,128)S(1)}, f32[3,10,16,128]{3,2,1,0:T(8,128)S(1)}, u32[]{:S(2)}, u32[]{:S(2)}) collective-permute-start(f32[3,10,16,128]{3,2,1,0:T(8,128)S(1)} %get-tuple-element.26), channel_id=1, source_target_pairs={{0,64},{64,128},{128,192},{192,0},{1,65},{65,129},{129,193},{193,1... | collective-permute-start | bytes 737288 | tf_op jit(solution)/shard_map/ppermute | solution.py:392
  59.8 12.6 %collective-permute-start.21 = (f32[8,3,16,128]{3,2,1,0:T(8,128)S(1)}, f32[8,3,16,128]{3,2,1,0:T(8,128)S(1)}, u32[]{:S(2)}, u32[]{:S(2)}) collective-permute-start(f32[8,3,16,128]{3,2,1,0:T(8,128)S(1)} %get-tuple-element.23), channel_id=1, source_target_pairs={{0,1},{1,2},{2,3},{3,4},{4,5},{5,6},{6,7},{7,0},{8,9},{9,10},{10,1... | collective-permute-start | bytes 589832 | tf_op jit(solution)/shard_map/ppermute | solution.py:392
  59.8 12.6 %collective-permute-start.22 = (f32[8,3,16,128]{3,2,1,0:T(8,128)S(1)}, f32[8,3,16,128]{3,2,1,0:T(8,128)S(1)}, u32[]{:S(2)}, u32[]{:S(2)}) collective-permute-start(f32[8,3,16,128]{3,2,1,0:T(8,128)S(1)} %get-tuple-element.24), channel_id=1, source_target_pairs={{0,7},{1,0},{2,1},{3,2},{4,3},{5,4},{6,5},{7,6},{8,15},{9,8},{10,9... | collective-permute-start | bytes 589832 | tf_op jit(solution)/shard_map/ppermute | solution.py:392
  62.5 6.2 %collective-permute-start.20 = (f32[8,10,3,128]{3,2,1,0:T(4,128)S(1)}, f32[8,10,3,128]{3,2,1,0:T(4,128)S(1)}, u32[]{:S(2)}, u32[]{:S(2)}) collective-permute-start(f32[8,10,3,128]{3,2,1,0:T(4,128)S(1)} %get-tuple-element.22), channel_id=1, source_target_pairs={{0,56},{8,0},{16,8},{24,16},{32,24},{40,32},{48,40},{56,48},{1,57}... | collective-permute-start | bytes 368648 | tf_op jit(solution)/shard_map/ppermute | solution.py:392

commit v3 on v2

--- a/solution.py
+++ b/solution.py
@@ -100,60 +100,81 @@
     return flow * middle[i] + jnp.abs(flow) * shift
 
 
-def speed_kernel(u_ref, out_ref, *, d_speed):
-    nx, nh, ny, nv = u_ref.shape
+def speed_kernel(u_ref, *refs, d_speed, blocks):
+    out_ref, turned, bent, up_ref, down_ref, pair_ref, fourth_ref, done_ref = refs[-8:]
+    nv = u_ref.shape[1]
     floor = floor_of(d_speed)
-    lane = lax.broadcasted_iota(jnp.int32, (ny, nv), 1)
-    first = lane == 0
-    last = lane == nv - 1
-    inside = jnp.logical_not(jnp.logical_or(first, last))
-
-    def before(value):
-        return pltpu.roll(value, 1, 1)
-
-    def after(value):
-        return pltpu.roll(value, nv - 1, 1)
-
     top = 1.0 / (floor * floor)
-
-    def one(x, h):
-        u = u_ref[x, h]
-        u_before = before(u)
-        u_after = after(u)
-        rise_here = u - u_before
-        rise_next = u_after - u
-        bend = jnp.where(inside, rise_next - rise_here, 0.0)
-        across = jnp.where(
-            first, 2.0 * rise_next, jnp.where(last, 2.0 * rise_here, u_after - u_before)
+    first, last = 8, 8 + nv
+
+    for b in range(*blocks):
+        turned[b, first:last] = u_ref[128 * b : 128 * b + 128].T
+
+    def bends(b, carry):
+        zero = jnp.zeros((8, 128), jnp.float32)
+        turned[b, first - 1 : first] = (
+            2.0 * turned[b, first : first + 1] - turned[b, first + 1 : first + 2]
         )
-        below = before(bend)
-        above = after(bend)
-        rest = squared(bend) * REST + floor
-        lean = bend * LEAN
-        to_up = inverse_square(squared(above - lean) + rest)
-        to_down = inverse_square(squared(below - lean) + rest)
-        pair = inverse_square(squared(below - bend * LEVEL) + rest) * 6.0
-        fourth = ((above - bend) - (bend - below)) * (2.0 / 3.0)
-        half = 0.5 * fourth
-        down_before = jnp.where(first, top, before(to_down))
-        up_after = jnp.where(last, top, after(to_up))
-        fourth_before = jnp.where(first, 0.0, before(fourth))
-        fourth_after = jnp.where(last, 0.0, after(fourth))
-        up_3 = to_up * 3.0
-        down_3 = to_down * 3.0
-        middle = across - (above - below) * (1.0 / 6.0)
-        right = (up_after * fourth_after + down_3 * half) / (up_after + down_3 + after(pair))
-        left = (down_before * fourth_before + up_3 * half) / (down_before + up_3 + pair)
-        out_ref[x, h] = (jnp.maximum(right + middle, left - middle) - 0.5 * half) * (
-            0.5 * ACCEL_MAX / d_speed
+        turned[b, last : last + 1] = (
+            2.0 * turned[b, last - 1 : last] - turned[b, last - 2 : last - 1]
         )
-
-    def step(x, carry):
-        for h in range(nh):
-            one(x, h)
-        return carry
-
-    lax.fori_loop(0, nx, step, 0)
+        for ref, low, high in (
+            (bent, zero, zero),
+            (fourth_ref, zero, zero),
+            (down_ref, zero + top, None),
+            (up_ref, None, zero + top),
+            (pair_ref, None, zero + 6.0 * top),
+        ):
+            if low is not None:
+                ref[b, first - 8 : first] = low
+            if high is not None:
+                ref[b, last : last + 8] = high
+        for r in range(first, last, 8):
+            here = turned[b, r : r + 8]
+            bent[b, r : r + 8] = (turned[b, r + 1 : r + 9] - here) - (
+                here - turned[b, r - 1 : r + 7]
+            )
+        return carry
+
+    lax.fori_loop(*blocks, bends, 0)
+
+    def weights(b, carry):
+        for r in range(first, last, 8):
+            below, bend, above = (bent[b, r + d : r + d + 8] for d in (-1, 0, 1))
+            rest = squared(bend) * REST + floor
+            lean = bend * LEAN
+            up_ref[b, r : r + 8] = inverse_square(squared(above - lean) + rest)
+            down_ref[b, r : r + 8] = inverse_square(squared(below - lean) + rest)
+            pair_ref[b, r : r + 8] = inverse_square(squared(below - bend * LEVEL) + rest) * 6.0
+            fourth_ref[b, r : r + 8] = ((above - bend) - (bend - below)) * (2.0 / 3.0)
+        return carry
+
+    lax.fori_loop(*blocks, weights, 0)
+
+    def combine(b, carry):
+        for r in range(first, last, 8):
+            half = 0.5 * fourth_ref[b, r : r + 8]
+            up_3 = up_ref[b, r : r + 8] * 3.0
+            down_3 = down_ref[b, r : r + 8] * 3.0
+            up_after = up_ref[b, r + 1 : r + 9]
+            down_before = down_ref[b, r - 1 : r + 7]
+            middle = (turned[b, r + 1 : r + 9] - turned[b, r - 1 : r + 7]) - (
+                bent[b, r + 1 : r + 9] - bent[b, r - 1 : r + 7]
+            ) * (1.0 / 6.0)
+            right = (up_after * fourth_ref[b, r + 1 : r + 9] + down_3 * half) / (
+                up_after + down_3 + pair_ref[b, r + 1 : r + 9]
+            )
+            left = (down_before * fourth_ref[b, r - 1 : r + 7] + up_3 * half) / (
+                down_before + up_3 + pair_ref[b, r : r + 8]
+            )
+            done_ref[b, r : r + 8] = (jnp.maximum(right + middle, left - middle) - 0.5 * half) * (
+                0.5 * ACCEL_MAX / d_speed
+            )
+        return carry
+
+    lax.fori_loop(*blocks, combine, 0)
+    for b in range(*blocks):
+        out_ref[128 * b : 128 * b + 128] = done_ref[b, first:last].T
 
 
 def ghosts(edge, inner):
@@ -164,29 +185,31 @@
 
 
 def plane_kernel(
-    flag_ref, u_ref, part_ref, xlo, xhi, ylo, yhi, vel_ref, wind_ref, acc_ref, pad_ref, bend_ref
+    u_ref, part_ref, xlo, xhi, ymate, yother, vel_ref, wind_ref, acc_ref, pad_ref, bend_ref
 ):
     nx, nh, ny, nv = u_ref.shape
     halves = ny // 8
     floor = floor_of(CELL_SIZE)
-    start_x = flag_ref[0] == 1
-    end_x = flag_ref[1] == 1
-    start_y = flag_ref[2] == 1
-    end_y = flag_ref[3] == 1
-    row = lax.broadcasted_iota(jnp.int32, (3, nv), 0).astype(jnp.float32)
-    reach_low = 3.0 - row
-    reach_high = 1.0 + row
+    gx, gy = lax.axis_index("gx"), lax.axis_index("gy")
+    start_x = gx == 0
+    end_x = gx == lax.axis_size("gx") - 1
+    at_edge = jnp.logical_or(gy == 0, gy == lax.axis_size("gy") - 1)
+    odd = lax.rem(gy, 2)
+    mate_at = 8 + ny - odd * (ny + 3)
+    other_at = 5 + odd * (ny + 3)
+    edge_row = odd * (ny - 1)
+    inner_row = 1 + odd * (ny - 3)
+    row = lax.broadcasted_iota(jnp.int32, (3, nv), 0)
+    reach = (3 - row + odd * (2 * row - 2)).astype(jnp.float32)
 
     def fill(x, carry):
         for h in range(nh):
             pad_ref[x, h, 8 : 8 + ny] = u_ref[x, h]
-            edge = u_ref[x, h, pl.ds(0, 3, stride=0)]
-            inner = u_ref[x, h, pl.ds(1, 3, stride=0)]
-            pad_ref[x, h, 5:8] = jnp.where(start_y, edge + reach_low * (edge - inner), ylo[x, h])
-            edge = u_ref[x, h, pl.ds(ny - 1, 3, stride=0)]
-            inner = u_ref[x, h, pl.ds(ny - 2, 3, stride=0)]
-            pad_ref[x, h, 8 + ny : 11 + ny] = jnp.where(
-                end_y, edge + reach_high * (edge - inner), yhi[x, h]
+            pad_ref[x, h, pl.ds(mate_at, 3)] = ymate[x, h]
+            edge = u_ref[x, h, pl.ds(edge_row, 3, stride=0)]
+            inner = u_ref[x, h, pl.ds(inner_row, 3, stride=0)]
+            pad_ref[x, h, pl.ds(other_at, 3)] = jnp.where(
+                at_edge, edge + reach * (edge - inner), yother[x, h]
             )
         for h in range(nh):
             for r in range(0, UP, 8):
@@ -234,13 +257,19 @@
     lax.fori_loop(0, nh, along_x, 0)
 
 
-def heading_kernel(dt_ref, u_ref, acc_ref, *refs, stage, d_theta):
+def heading_kernel(top_ref, u_ref, acc_ref, *refs, stage, d_theta, d_speed):
     refs = list(refs)
     base_ref = refs.pop(0) if stage > 1 else None
     hlo, hhi, out_ref, *faces = refs
+    if stage == 3:
+        whole_ref, out_ref, sent = out_ref, *faces
+        faces = None
     nx, nh, ny, _ = u_ref.shape
     halves = ny // 8
-    dt = dt_ref[0]
+    mate_row = (1 - lax.rem(lax.axis_index("gy"), 2)) * (ny - 3)
+    dt = CFL_NUMBER / (
+        top_ref[...] * (1.0 / CELL_SIZE) + (TURN_MAX / d_theta + ACCEL_MAX / d_speed)
+    )
     theta_floor = floor_of(d_theta)
 
     def along_heading(x, carry):
@@ -272,14 +301,18 @@
                         faces[2][x, h, rows] = value
                     if h >= nh - 3:
                         faces[3][x, h - nh + 3, rows] = value
-                    if half == 0:
-                        faces[0][x, h] = value[0:3]
         if stage < 3:
             for h in range(nh):
-                faces[1][x, h] = out_ref[x, h, ny - 3 : ny]
+                faces[0][x, h] = out_ref[x, h, pl.ds(mate_row, 3)]
+                faces[1][x, h] = out_ref[x, h, pl.ds(ny - 3 - mate_row, 3)]
+        else:
+            pltpu.make_async_copy(out_ref.at[x], whole_ref.at[x], sent.at[x]).start()
         return carry
 
     lax.fori_loop(0, nx, along_heading, 0)
+    if stage == 3:
+        for x in range(nx):
+            pltpu.make_async_copy(out_ref.at[x], whole_ref.at[x], sent.at[x]).wait()
 
 
 def rate_kernel(wind_ref, out_ref, *, spots):
@@ -293,11 +326,6 @@
 
 
 VMEM = pl.BlockSpec(memory_space=pltpu.VMEM)
-SMEM = pl.BlockSpec(memory_space=pltpu.SMEM)
-
-
-def ring(count, step):
-    return [(i, (i + step) % count) for i in range(count)]
 
 
 def body(level_set, wind_field):
@@ -306,11 +334,6 @@
     n_head = nh * lax.axis_size("ha")
     d_theta = 2.0 * math.pi / n_head
     d_speed = SPEED_SPAN / nv
-    gx, gy = lax.axis_index("gx"), lax.axis_index("gy")
-    flags = jnp.stack(
-        [gx == 0, gx == lax.axis_size("gx") - 1, gy == 0, gy == lax.axis_size("gy") - 1]
-    ).astype(jnp.int32)
-
     every_angle = np.arange(n_head, dtype=np.float32) * np.float32(d_theta)
     ends = [SPEED_LOW + SPEED_SPAN * 0.5 / nv, SPEED_LOW + SPEED_SPAN * (nv - 0.5) / nv]
     spots = [
@@ -341,24 +364,30 @@
     y_face = jax.ShapeDtypeStruct((nx, nh, 3, nv), jnp.float32)
     h_face = jax.ShapeDtypeStruct((nx, 3, ny, nv), jnp.float32)
 
-    def speed_part(u):
+    def speed_part(u, share=(0, 1), filled=()):
+        flat = (nx * nh * ny, nv)
+        count = flat[0] // 128
         return pl.pallas_call(
-            functools.partial(speed_kernel, d_speed=d_speed),
-            out_shape=shape,
-            in_specs=[VMEM],
+            functools.partial(
+                speed_kernel, d_speed=d_speed, blocks=tuple(int(count * s) for s in share)
+            ),
+            out_shape=jax.ShapeDtypeStruct(flat, jnp.float32),
+            in_specs=[VMEM] * (1 + len(filled)),
             out_specs=VMEM,
+            input_output_aliases={1: 0} if filled else {},
+            scratch_shapes=[pltpu.VMEM((count, nv + 16, 128), jnp.float32)] * 7,
             cost_estimate=pl.CostEstimate(
                 flops=100 * nx * nh * ny * nv, bytes_accessed=8 * nx * nh * ny * nv, transcendentals=0
             ),
-            compiler_params=pltpu.CompilerParams(vmem_limit_bytes=8 << 20),
+            compiler_params=pltpu.CompilerParams(vmem_limit_bytes=12 << 20),
             name="speed",
-        )(u)
-
-    def plane_part(u, part, xlo, xhi, ylo, yhi):
+        )(u.reshape(flat), *(f.reshape(flat) for f in filled)).reshape(u.shape)
+
+    def plane_part(u, part, xlo, xhi, ymate, yother):
         return pl.pallas_call(
             plane_kernel,
             out_shape=shape,
-            in_specs=[SMEM] + [VMEM] * 8,
+            in_specs=[VMEM] * 8,
             out_specs=VMEM,
             scratch_shapes=[
                 pltpu.VMEM((nx, nh, ny + 16, nv), jnp.float32),
@@ -369,48 +398,63 @@
             ),
             compiler_params=pltpu.CompilerParams(vmem_limit_bytes=24 << 20),
             name="plane",
-        )(flags, u, part, xlo, xhi, ylo, yhi, velocity, wind)
+        )(u, part, xlo, xhi, ymate, yother, velocity, wind)
 
     def heading_part(stage, u, acc, hlo, hhi):
         outs = [shape]
         if stage < 3:
             outs += [y_face, y_face, h_face, h_face]
-        ins = [time_step, u, acc] + ([field] if stage > 1 else []) + [hlo, hhi]
+        ins = [top, u, acc] + ([field] if stage > 1 else []) + [hlo, hhi]
         return pl.pallas_call(
-            functools.partial(heading_kernel, stage=stage, d_theta=d_theta),
+            functools.partial(heading_kernel, stage=stage, d_theta=d_theta, d_speed=d_speed),
             out_shape=outs,
-            in_specs=[SMEM] + [VMEM] * (len(ins) - 1),
-            out_specs=[VMEM] * len(outs),
+            in_specs=[VMEM] * len(ins),
+            out_specs=[VMEM] * len(outs) if stage < 3 else [pl.BlockSpec(memory_space=pl.ANY)],
+            scratch_shapes=(
+                []
+                if stage < 3
+                else [pltpu.VMEM(shape.shape, jnp.float32), pltpu.SemaphoreType.DMA((nx,))]
+            ),
             cost_estimate=pl.CostEstimate(
                 flops=100 * nx * nh * ny * nv, bytes_accessed=16 * nx * nh * ny * nv, transcendentals=0
             ),
             compiler_params=pltpu.CompilerParams(vmem_limit_bytes=24 << 20),
         )(*ins)
 
-    def exchange(u, y_first, y_last, h_first, h_last):
+    def exchange(u, y_mate, y_other, h_first, h_last):
         def halo(value, axis, step):
-            return lax.ppermute(value, axis, ring(lax.axis_size(axis), step))
-
-        xlo = halo(u[nx - 3 :], "gx", 1)
-        xhi = halo(u[:3], "gx", -1)
-        ylo = halo(y_last, "gy", 1)
-        yhi = halo(y_first, "gy", -1)
-        hlo = halo(h_last, "ha", 1)
-        hhi = halo(h_first, "ha", -1)
-        return xlo, xhi, ylo, yhi, hlo, hhi
+            count = lax.axis_size(axis)
+            return lax.ppermute(value, axis, [(i, step(i) % count) for i in range(count)])
+
+        xlo = halo(u[nx - 3 :], "gx", lambda i: i + 1)
+        xhi = halo(u[:3], "gx", lambda i: i - 1)
+        ymate = halo(y_mate, "gy", lambda i: i ^ 1)
+        yother = halo(y_other, "gy", lambda i: i + 1 if i % 2 else i - 1)
+        hlo = halo(h_last, "ha", lambda i: i + 1)
+        hhi = halo(h_first, "ha", lambda i: i - 1)
+        return xlo, xhi, ymate, yother, hlo, hhi
 
     for axis, bit in [("gx", 1), ("gx", 2), ("gy", 1), ("gy", 2), ("gy", 4)]:
         other = lax.ppermute(top, axis, [(j, j ^ bit) for j in range(lax.axis_size(axis))])
         top = jnp.maximum(top, other)
-    top_rate = top[0, :1] / CELL_SIZE + TURN_MAX / d_theta + ACCEL_MAX / d_speed
-    time_step = CFL_NUMBER / top_rate
-
+
+    even = lax.axis_index("gy") % 2 == 0
+    y_first, y_last = field[:, :, :3], field[:, :, ny - 3 :]
+    faces = (
+        jnp.where(even, y_last, y_first),
+        jnp.where(even, y_first, y_last),
+        field[:, :3],
+        field[:, nh - 3 :],
+    )
     u = field
-    faces = (field[:, :, :3], field[:, :, ny - 3 :], field[:, :3], field[:, nh - 3 :])
     for stage in (1, 2, 3):
-        xlo, xhi, ylo, yhi, hlo, hhi = exchange(u, *faces)
-        part = speed_part(u)
-        acc = plane_part(u, part, xlo, xhi, ylo, yhi)
+        xlo, xhi, ymate, yother, hlo, hhi = exchange(u, *faces)
+        if stage > 1:
+            part = speed_part(u)
+        else:
+            part = speed_part(u, (0, 0.5))
+            part = speed_part(u, (0.5, 1), (part,))
+        acc = plane_part(u, part, xlo, xhi, ymate, yother)
         u, *faces = heading_part(stage, u, acc, hlo, hhi)
     return jnp.transpose(u, (0, 2, 1, 3))
 

time: 74.9 us -> 74.4 us (level)
  the two profiles are of different devices: /device:TPU:25 before, /device:TPU:6 now
where the time goes in v3:
time: 74.4 us; the launch traced here: 74.3 us
  starting transfers between devices  28.4 us (38%)
  waiting for transfers between devices  22.3 us (30%)
  Pallas kernels  20.9 us (28%)
  other arithmetic  1.3 us (2%)
  local copies, waits for them, and re-layouts  0.92 us (1%)
    ppermute x18, starting transfers between devices, halo(): lax.ppermute(value, axis, [(i, step(i) % count) for i in range(count)])  24.8 us
    ppermute x18, waiting for transfers between devices, halo(): lax.ppermute(value, axis, [(i, step(i) % count) for i in range(count)])  11.6 us
    ppermute x5, waiting for transfers between devices, body(): lax.ppermute(top, axis, [(j, j ^ bit) for j in range(lax.axis_size(axis))])  10.7 us
    pallas_call x3, Pallas kernels, plane_part(): pl.pallas_call(plane_kernel, out_shape=shape, in_specs=[VMEM] * 8, out_sp...  9.31 us
    pallas_call x4, Pallas kernels, speed_part(): pl.pallas_call(functools.partial(speed_kernel, d_speed=d_speed, blocks=tu...  5.98 us
    pallas_call x3, Pallas kernels, heading_part(): pl.pallas_call(functools.partial(heading_kernel, stage=stage, d_theta=d_t...  5.33 us
    ppermute x5, starting transfers between devices, body(): lax.ppermute(top, axis, [(j, j ^ bit) for j in range(lax.axis_size(axis))])  3.62 us
  transfers between devices with their start and end apart: 23, of which 7 were waited for; matrix products, arithmetic and copies ran while one was open for 2% of the time, Pallas kernels for 21%

profile of v3, /device:TPU:6, one launch (start us, length us, event | category | flops | bytes accessed | tf_op | source)
XLA Modules:
  0.0 74.3 jit_solution(3546077391719656489)
XLA Ops:
  0.0 0.7 copy-done.1
  0.7 0.3 rate.1
  1.0 0.9 %collective-permute-start = (f32[8,128]{1,0:T(8,128)S(1)}, f32[8,128]{1,0:T(8,128)S(1)}, u32[]{:S(2)}, u32[]{:S(2)}) collective-permute-start(f32[8,128]{1,0:T(8,128)S(1)} %rate.1), channel_id=1, source_target_pairs={{0,64},{64,0},{128,192},{192,128},{1,65},{65,1},{129,193},{193,129... | collective-permute-start | bytes 12296 | tf_op jit(solution)/shard_map/ppermute | solution.py:438
  1.9 1.1 %slice_select_fusion = (f32[8,10,3,128]{3,2,1,0:T(4,128)S(1)}, f32[8,10,3,128]{3,2,1,0:T(4,128)S(1)}) fusion(f32[8,10,16,128]{3,2,1,0:T(8,128)} %bitcast.9, pred[]{:T(512)S(6)} %eq.5), kind=kLoop, calls=%fused_computation | loop fusion | flops 61440 | bytes 491521 | tf_op jit(solution)/shard_map/jit(_where)/select_n | solution.py:445
  3.0 2.3 %collective-permute-start.8 = (f32[8,10,3,128]{3,2,1,0:T(4,128)S(1)}, f32[8,10,3,128]{3,2,1,0:T(4,128)S(1)}, u32[]{:S(2)}, u32[]{:S(2)}) collective-permute-start(f32[8,10,3,128]{3,2,1,0:T(4,128)S(1)} %get-tuple-element.31), channel_id=1, source_target_pairs={{0,56},{8,16},{16,8},{24,32},{32,24},{40,48},{48,40},{56,0},{1,57}... | collective-permute-start | bytes 368648 | tf_op jit(solution)/shard_map/ppermute | solution.py:427
  5.3 1.3 %collective-permute-start.6 = (f32[3,10,16,128]{3,2,1,0:T(8,128)S(1)}, f32[3,10,16,128]{3,2,1,0:T(8,128)S(1)}, u32[]{:S(2)}, u32[]{:S(2)}) collective-permute-start(f32[3,10,16,128]{3,2,1,0:T(8,128)S(1)} %get-tuple-element.33), channel_id=1, source_target_pairs={{0,192},{64,0},{128,64},{192,128},{1,193},{65,1},{129,65},{193,129... | collective-permute-start | bytes 737288 | tf_op jit(solution)/shard_map/ppermute | solution.py:427
  6.6 2.0 %collective-permute-start.5 = (f32[3,10,16,128]{3,2,1,0:T(8,128)S(1)}, f32[3,10,16,128]{3,2,1,0:T(8,128)S(1)}, u32[]{:S(2)}, u32[]{:S(2)}) collective-permute-start(f32[3,10,16,128]{3,2,1,0:T(8,128)S(1)} %get-tuple-element.34), channel_id=1, source_target_pairs={{0,64},{64,128},{128,192},{192,0},{1,65},{65,129},{129,193},{193,1... | collective-permute-start | bytes 737288 | tf_op jit(solution)/shard_map/ppermute | solution.py:427
  8.7 0.0 collective-permute-done
  8.7 0.2 collective-permute-start.1
  9.0 5.6 %collective-permute-done.1 = f32[8,128]{1,0:T(8,128)S(1)} collective-permute-done((f32[8,128]{1,0:T(8,128)S(1)}, f32[8,128]{1,0:T(8,128)S(1)}, u32[]{:S(2)}, u32[]{:S(2)}) %collective-permute-start.1) | collective-permute-done | bytes 4128 | tf_op jit(solution)/shard_map/ppermute | solution.py:438
  14.6 1.2 %collective-permute-done.2 = f32[8,128]{1,0:T(8,128)S(1)} collective-permute-done((f32[8,128]{1,0:T(8,128)S(1)}, f32[8,128]{1,0:T(8,128)S(1)}, u32[]{:S(2)}, u32[]{:S(2)}) %collective-permute-start.2) | collective-permute-done | bytes 4128 | tf_op jit(solution)/shard_map/ppermute | solution.py:438
  15.7 0.6 collective-permute-start.3
  16.3 3.0 %collective-permute-done.3 = f32[8,128]{1,0:T(8,128)S(1)} collective-permute-done((f32[8,128]{1,0:T(8,128)S(1)}, f32[8,128]{1,0:T(8,128)S(1)}, u32[]{:S(2)}, u32[]{:S(2)}) %collective-permute-start.3) | collective-permute-done | bytes 4128 | tf_op jit(solution)/shard_map/ppermute | solution.py:438
  19.3 1.9 %collective-permute-start.4 = (f32[8,128]{1,0:T(8,128)S(1)}, f32[8,128]{1,0:T(8,128)S(1)}, u32[]{:S(2)}, u32[]{:S(2)}) collective-permute-start(f32[8,128]{1,0:T(8,128)S(1)} %max.18), channel_id=1, source_target_pairs={{0,32},{8,40},{16,48},{24,56},{32,0},{40,8},{48,16},{56,24},{1,33}... | collective-permute-start | bytes 12296 | tf_op jit(solution)/shard_map/ppermute | solution.py:438
  21.3 0.1 broadcast_multiply_fusion.vel_ref
  21.3 1.1 %speed.4.refs_0_ = f32[1280,128]{1,0:T(8,128)S(1)} custom-call(f32[1280,128]{1,0:T(8,128)S(1)} %bitcast.12), custom_call_target="tpu_custom_call" | custom-call | flops 16384000 | bytes 1310720 | tf_op jit(solution)/shard_map/speed/pallas_call | solution.py:370
  22.4 0.0 copy-start.2
  22.4 1.1 %speed.5 = f32[1280,128]{1,0:T(8,128)S(1)} custom-call(f32[1280,128]{1,0:T(8,128)S(1)} %bitcast.13, f32[1280,128]{1,0:T(8,128)S(1)} %speed.4.refs_0_), custom_call_target="tpu_custom_call", output_to_operand_aliasing={{}: (1, {})} | custom-call | flops 16384000 | bytes 1310720 | tf_op jit(solution)/shard_map/speed/pallas_call | solution.py:370
  23.5 1.0 %collective-permute-done.4 = f32[8,128]{1,0:T(8,128)S(1)} collective-permute-done((f32[8,128]{1,0:T(8,128)S(1)}, f32[8,128]{1,0:T(8,128)S(1)}, u32[]{:S(2)}, u32[]{:S(2)}) %collective-permute-start.4) | collective-permute-done | bytes 4128 | tf_op jit(solution)/shard_map/ppermute | solution.py:438
  24.5 5.9 %collective-permute-start.10 = (f32[8,3,16,128]{3,2,1,0:T(8,128)S(1)}, f32[8,3,16,128]{3,2,1,0:T(8,128)S(1)}, u32[]{:S(2)}, u32[]{:S(2)}) collective-permute-start(f32[8,3,16,128]{3,2,1,0:T(8,128)S(1)} %get-tuple-element.29), channel_id=1, source_target_pairs={{0,7},{1,0},{2,1},{3,2},{4,3},{5,4},{6,5},{7,6},{8,15},{9,8},{10,9... | collective-permute-start | bytes 589832 | tf_op jit(solution)/shard_map/ppermute | solution.py:427
  30.3 0.0 collective-permute-start.9
  30.3 0.0 collective-permute-done.7.ymate
  30.4 0.0 collective-permute-done.5.xlo
  30.4 0.1 broadcast_in_dim.5.wind_ref
  30.5 3.1 %plane.3.acc_ref = f32[8,10,16,128]{3,2,1,0:T(8,128)S(1)} custom-call(f32[8,10,16,128]{3,2,1,0:T(8,128)S(1)} %bitcast.14, f32[8,10,16,128]{3,2,1,0:T(8,128)S(1)} %bitcast.20, f32[3,10,16,128]{3,2,1,0:T(8,128)S(1)} %collective-permute-done.5.xlo, f32[3,10,16,128]{3,2,1,0:T(8,128)S(1)} %collective-permute-done.6.xhi, ...), custom_call_target="tpu_custom_call" | custom-call | flops 32768000 | bytes 2621440 | tf_op jit(solution)/shard_map/plane/pallas_call | solution.py:387
  33.6 0.0 collective-permute-done.10.refs_1_
  33.6 3.6 %collective-permute-done.9.refs_0_ = f32[8,3,16,128]{3,2,1,0:T(8,128)S(1)} collective-permute-done((f32[8,3,16,128]{3,2,1,0:T(8,128)S(1)}, f32[8,3,16,128]{3,2,1,0:T(8,128)S(1)}, u32[]{:S(2)}, u32[]{:S(2)}) %collective-permute-start.9) | collective-permute-done | bytes 196640 | tf_op jit(solution)/shard_map/ppermute | solution.py:427
  37.2 1.5 %shard_map.28 = (f32[8,10,16,128]{3,2,1,0:T(8,128)S(1)}, f32[8,10,3,128]{3,2,1,0:T(4,128)S(1)}, f32[8,10,3,128]{3,2,1,0:T(4,128)S(1)}, f32[8,3,16,128]{3,2,1,0:T(8,128)S(1)}, f32[8,3,16,128]{3,2,1,0:T(8,128)S(1)}) custom-call(f32[8,128]{1,0:T(8,128)S(1)} %max.19.top_ref, f32[8,10,16,128]{3,2,1,0:T(8,128)S(1)} %bitcast.15, ...), custom_call_target="tpu_custom_call" | custom-call | flops 16384000 | bytes 2621440 | tf_op jit(solution)/shard_map/pallas_call | solution.py:408
  38.7 0.1 collective-permute-start.13
  38.9 1.5 %collective-permute-start.12 = (f32[3,10,16,128]{3,2,1,0:T(8,128)S(1)}, f32[3,10,16,128]{3,2,1,0:T(8,128)S(1)}, u32[]{:S(2)}, u32[]{:S(2)}) collective-permute-start(f32[3,10,16,128]{3,2,1,0:T(8,128)S(1)} %get-tuple-element.27), channel_id=1, source_target_pairs={{0,192},{64,0},{128,64},{192,128},{1,193},{65,1},{129,65},{193,129... | collective-permute-start | bytes 737288 | tf_op jit(solution)/shard_map/ppermute | solution.py:427
  40.3 1.8 %collective-permute-start.11 = (f32[3,10,16,128]{3,2,1,0:T(8,128)S(1)}, f32[3,10,16,128]{3,2,1,0:T(8,128)S(1)}, u32[]{:S(2)}, u32[]{:S(2)}) collective-permute-start(f32[3,10,16,128]{3,2,1,0:T(8,128)S(1)} %get-tuple-element.28), channel_id=1, source_target_pairs={{0,64},{64,128},{128,192},{192,0},{1,65},{65,129},{129,193},{193,1... | collective-permute-start | bytes 737288 | tf_op jit(solution)/shard_map/ppermute | solution.py:427
  42.2 0.0 collective-permute-start.15
  42.2 3.2 %collective-permute-start.16 = (f32[8,3,16,128]{3,2,1,0:T(8,128)S(1)}, f32[8,3,16,128]{3,2,1,0:T(8,128)S(1)}, u32[]{:S(2)}, u32[]{:S(2)}) collective-permute-start(f32[8,3,16,128]{3,2,1,0:T(8,128)S(1)} %get-tuple-element.19), channel_id=1, source_target_pairs={{0,7},{1,0},{2,1},{3,2},{4,3},{5,4},{6,5},{7,6},{8,15},{9,8},{10,9... | collective-permute-start | bytes 589832 | tf_op jit(solution)/shard_map/ppermute | solution.py:427
  45.4 0.0 collective-permute-done.13.ymate
  45.4 0.1 collective-permute-start.14
  45.5 1.9 %speed.6 = f32[1280,128]{1,0:T(8,128)S(1)} custom-call(f32[1280,128]{1,0:T(8,128)S(1)} %bitcast.18), custom_call_target="tpu_custom_call" | custom-call | flops 16384000 | bytes 1310720 | tf_op jit(solution)/shard_map/speed/pallas_call | solution.py:370
  47.4 4.0 %collective-permute-done.14.yother = f32[8,10,3,128]{3,2,1,0:T(4,128)S(1)} collective-permute-done((f32[8,10,3,128]{3,2,1,0:T(4,128)S(1)}, f32[8,10,3,128]{3,2,1,0:T(4,128)S(1)}, u32[]{:S(2)}, u32[]{:S(2)}) %collective-permute-start.14) | collective-permute-done | bytes 122912 | tf_op jit(solution)/shard_map/ppermute | solution.py:427
  51.4 0.0 collective-permute-done.11.xlo
  51.4 3.1 %plane.4.acc_ref = f32[8,10,16,128]{3,2,1,0:T(8,128)S(1)} custom-call(f32[8,10,16,128]{3,2,1,0:T(8,128)S(1)} %get-tuple-element.15.u_ref, f32[8,10,16,128]{3,2,1,0:T(8,128)S(1)} %bitcast.22, f32[3,10,16,128]{3,2,1,0:T(8,128)S(1)} %collective-permute-done.11.xlo, f32[3,10,16,128]{3,2,1,0:T(8,128)S(1)} %collective-permute-done.12.xhi, ...), custom_call_target="tpu_custom_call" | custom-call | flops 32768000 | bytes 2621440 | tf_op jit(solution)/shard_map/plane/pallas_call | solution.py:387
  54.5 1.6 %shard_map.29 = (f32[8,10,16,128]{3,2,1,0:T(8,128)S(1)}, f32[8,10,3,128]{3,2,1,0:T(4,128)S(1)}, f32[8,10,3,128]{3,2,1,0:T(4,128)S(1)}, f32[8,3,16,128]{3,2,1,0:T(8,128)S(1)}, f32[8,3,16,128]{3,2,1,0:T(8,128)S(1)}) custom-call(f32[8,128]{1,0:T(8,128)S(1)} %max.19.top_ref, f32[8,10,16,128]{3,2,1,0:T(8,128)S(1)} %get-tuple-element.15.u_ref, ...), custom_call_target="tpu_custom_call" | custom-call | flops 16384000 | bytes 2621440 | tf_op jit(solution)/shard_map/pallas_call | solution.py:408
  56.1 0.1 collective-permute-start.19
  56.3 0.3 collective-permute-start.18
  56.5 3.1 %collective-permute-start.17 = (f32[3,10,16,128]{3,2,1,0:T(8,128)S(1)}, f32[3,10,16,128]{3,2,1,0:T(8,128)S(1)}, u32[]{:S(2)}, u32[]{:S(2)}) collective-permute-start(f32[3,10,16,128]{3,2,1,0:T(8,128)S(1)} %get-tuple-element.26), channel_id=1, source_target_pairs={{0,64},{64,128},{128,192},{192,0},{1,65},{65,129},{129,193},{193,1... | collective-permute-start | bytes 737288 | tf_op jit(solution)/shard_map/ppermute | solution.py:427
  59.6 3.2 %collective-permute-start.22 = (f32[8,3,16,128]{3,2,1,0:T(8,128)S(1)}, f32[8,3,16,128]{3,2,1,0:T(8,128)S(1)}, u32[]{:S(2)}, u32[]{:S(2)}) collective-permute-start(f32[8,3,16,128]{3,2,1,0:T(8,128)S(1)} %get-tuple-element.24), channel_id=1, source_target_pairs={{0,7},{1,0},{2,1},{3,2},{4,3},{5,4},{6,5},{7,6},{8,15},{9,8},{10,9... | collective-permute-start | bytes 589832 | tf_op jit(solution)/shard_map/ppermute | solution.py:427
  62.8 1.9 %speed.7 = f32[1280,128]{1,0:T(8,128)S(1)} custom-call(f32[1280,128]{1,0:T(8,128)S(1)} %bitcast.19), custom_call_target="tpu_custom_call" | custom-call | flops 16384000 | bytes 1310720 | tf_op jit(solution)/shard_map/speed/pallas_call | solution.py:370
  64.8 4.0 %collective-permute-done.20.yother = f32[8,10,3,128]{3,2,1,0:T(4,128)S(1)} collective-permute-done((f32[8,10,3,128]{3,2,1,0:T(4,128)S(1)}, f32[8,10,3,128]{3,2,1,0:T(4,128)S(1)}, u32[]{:S(2)}, u32[]{:S(2)}) %collective-permute-start.20) | collective-permute-done | bytes 122912 | tf_op jit(solution)/shard_map/ppermute | solution.py:427
  68.8 3.1 %plane.5.acc_ref = f32[8,10,16,128]{3,2,1,0:T(8,128)S(1)} custom-call(f32[8,10,16,128]{3,2,1,0:T(8,128)S(1)} %get-tuple-element.20.u_ref, f32[8,10,16,128]{3,2,1,0:T(8,128)S(1)} %bitcast.21, f32[3,10,16,128]{3,2,1,0:T(8,128)S(1)} %collective-permute-done.17.xlo, f32[3,10,16,128]{3,2,1,0:T(8,128)S(1)} %collective-permute-done.18.xhi, ...), custom_call_target="tpu_custom_call" | custom-call | flops 32768000 | bytes 2621440 | tf_op jit(solution)/shard_map/plane/pallas_call | solution.py:387
  71.9 2.2 %shard_map.30 = f32[8,10,16,128]{3,2,1,0:T(8,128)} custom-call(f32[8,128]{1,0:T(8,128)S(1)} %max.19.top_ref, f32[8,10,16,128]{3,2,1,0:T(8,128)S(1)} %get-tuple-element.20.u_ref, f32[8,10,16,128]{3,2,1,0:T(8,128)S(1)} %plane.5.acc_ref, f32[8,10,16,128]{3,2,1,0:T(8,128)S(1)} %bitcast.17, f32[8,3,16,128]{3,2,1,0:T(8,128)S(1)} %collective-permute-done.21.refs_1_, ...), custom_call_target="tpu_custom_call" | custom-call | flops 16384000 | bytes 2621440 | tf_op jit(solution)/shard_map/pallas_call | solution.py:408
  (31 shorter events, 0.3 us)
Async XLA Ops:
  0.0 0.7 copy-start.1
  0.7 4.6 %copy-start = (f32[8,16,10,128]{3,1,2,0:T(8,128)S(1)}, f32[8,16,10,128]{3,1,2,0:T(8,128)}, u32[]{:S(2)}) copy-start(f32[8,16,10,128]{3,1,2,0:T(8,128)} %param.2) | copy-start | bytes 1966084
  1.0 7.7 %collective-permute-start = (f32[8,128]{1,0:T(8,128)S(1)}, f32[8,128]{1,0:T(8,128)S(1)}, u32[]{:S(2)}, u32[]{:S(2)}) collective-permute-start(f32[8,128]{1,0:T(8,128)S(1)} %rate.1), channel_id=1, source_target_pairs={{0,64},{64,0},{128,192},{192,128},{1,65},{65,1},{129,193},{193,129... | collective-permute-start | bytes 12296 | tf_op jit(solution)/shard_map/ppermute | solution.py:438
  3.0 27.3 %collective-permute-start.8 = (f32[8,10,3,128]{3,2,1,0:T(4,128)S(1)}, f32[8,10,3,128]{3,2,1,0:T(4,128)S(1)}, u32[]{:S(2)}, u32[]{:S(2)}) collective-permute-start(f32[8,10,3,128]{3,2,1,0:T(4,128)S(1)} %get-tuple-element.31), channel_id=1, source_target_pairs={{0,56},{8,16},{16,8},{24,32},{32,24},{40,48},{48,40},{56,0},{1,57}... | collective-permute-start | bytes 368648 | tf_op jit(solution)/shard_map/ppermute | solution.py:427
  5.3 25.0 %collective-permute-start.7 = (f32[8,10,3,128]{3,2,1,0:T(4,128)S(1)}, f32[8,10,3,128]{3,2,1,0:T(4,128)S(1)}, u32[]{:S(2)}, u32[]{:S(2)}) collective-permute-start(f32[8,10,3,128]{3,2,1,0:T(4,128)S(1)} %get-tuple-element.32), channel_id=1, source_target_pairs={{0,8},{8,0},{16,24},{24,16},{32,40},{40,32},{48,56},{56,48},{1,9},... | collective-permute-start | bytes 368648 | tf_op jit(solution)/shard_map/ppermute | solution.py:427
  5.3 25.0 %collective-permute-start.6 = (f32[3,10,16,128]{3,2,1,0:T(8,128)S(1)}, f32[3,10,16,128]{3,2,1,0:T(8,128)S(1)}, u32[]{:S(2)}, u32[]{:S(2)}) collective-permute-start(f32[3,10,16,128]{3,2,1,0:T(8,128)S(1)} %get-tuple-element.33), channel_id=1, source_target_pairs={{0,192},{64,0},{128,64},{192,128},{1,193},{65,1},{129,65},{193,129... | collective-permute-start | bytes 737288 | tf_op jit(solution)/shard_map/ppermute | solution.py:427
  6.6 23.7 %collective-permute-start.5 = (f32[3,10,16,128]{3,2,1,0:T(8,128)S(1)}, f32[3,10,16,128]{3,2,1,0:T(8,128)S(1)}, u32[]{:S(2)}, u32[]{:S(2)}) collective-permute-start(f32[3,10,16,128]{3,2,1,0:T(8,128)S(1)} %get-tuple-element.34), channel_id=1, source_target_pairs={{0,64},{64,128},{128,192},{192,0},{1,65},{65,129},{129,193},{193,1... | collective-permute-start | bytes 737288 | tf_op jit(solution)/shard_map/ppermute | solution.py:427
  8.7 5.8 %collective-permute-start.1 = (f32[8,128]{1,0:T(8,128)S(1)}, f32[8,128]{1,0:T(8,128)S(1)}, u32[]{:S(2)}, u32[]{:S(2)}) collective-permute-start(f32[8,128]{1,0:T(8,128)S(1)} %max.15), channel_id=1, source_target_pairs={{0,128},{64,192},{128,0},{192,64},{1,129},{65,193},{129,1},{193,65... | collective-permute-start | bytes 12296 | tf_op jit(solution)/shard_map/ppermute | solution.py:438
  14.6 1.2 %collective-permute-start.2 = (f32[8,128]{1,0:T(8,128)S(1)}, f32[8,128]{1,0:T(8,128)S(1)}, u32[]{:S(2)}, u32[]{:S(2)}) collective-permute-start(f32[8,128]{1,0:T(8,128)S(1)} %max.16), channel_id=1, source_target_pairs={{0,8},{8,0},{16,24},{24,16},{32,40},{40,32},{48,56},{56,48},{1,9},... | collective-permute-start | bytes 12296 | tf_op jit(solution)/shard_map/ppermute | solution.py:438
  15.7 3.6 %collective-permute-start.3 = (f32[8,128]{1,0:T(8,128)S(1)}, f32[8,128]{1,0:T(8,128)S(1)}, u32[]{:S(2)}, u32[]{:S(2)}) collective-permute-start(f32[8,128]{1,0:T(8,128)S(1)} %max.17), channel_id=1, source_target_pairs={{0,16},{8,24},{16,0},{24,8},{32,48},{40,56},{48,32},{56,40},{1,17}... | collective-permute-start | bytes 12296 | tf_op jit(solution)/shard_map/ppermute | solution.py:438
  19.3 5.1 %collective-permute-start.4 = (f32[8,128]{1,0:T(8,128)S(1)}, f32[8,128]{1,0:T(8,128)S(1)}, u32[]{:S(2)}, u32[]{:S(2)}) collective-permute-start(f32[8,128]{1,0:T(8,128)S(1)} %max.18), channel_id=1, source_target_pairs={{0,32},{8,40},{16,48},{24,56},{32,0},{40,8},{48,16},{56,24},{1,33}... | collective-permute-start | bytes 12296 | tf_op jit(solution)/shard_map/ppermute | solution.py:438
  22.4 7.9 %copy-start.2 = (f32[2,8,16]{2,1,0:T(8,128)S(1)}, f32[2,8,16]{2,1,0:T(8,128)}, u32[]{:S(2)}) copy-start(f32[2,8,16]{2,1,0:T(8,128)} %wind_ref.1) | copy-start | bytes 3076
  24.5 9.1 %collective-permute-start.10 = (f32[8,3,16,128]{3,2,1,0:T(8,128)S(1)}, f32[8,3,16,128]{3,2,1,0:T(8,128)S(1)}, u32[]{:S(2)}, u32[]{:S(2)}) collective-permute-start(f32[8,3,16,128]{3,2,1,0:T(8,128)S(1)} %get-tuple-element.29), channel_id=1, source_target_pairs={{0,7},{1,0},{2,1},{3,2},{4,3},{5,4},{6,5},{7,6},{8,15},{9,8},{10,9... | collective-permute-start | bytes 589832 | tf_op jit(solution)/shard_map/ppermute | solution.py:427
  30.3 6.9 %collective-permute-start.9 = (f32[8,3,16,128]{3,2,1,0:T(8,128)S(1)}, f32[8,3,16,128]{3,2,1,0:T(8,128)S(1)}, u32[]{:S(2)}, u32[]{:S(2)}) collective-permute-start(f32[8,3,16,128]{3,2,1,0:T(8,128)S(1)} %get-tuple-element.30), channel_id=1, source_target_pairs={{0,1},{1,2},{2,3},{3,4},{4,5},{5,6},{6,7},{7,0},{8,9},{9,10},{10,1... | collective-permute-start | bytes 589832 | tf_op jit(solution)/shard_map/ppermute | solution.py:427
  38.7 6.7 %collective-permute-start.13 = (f32[8,10,3,128]{3,2,1,0:T(4,128)S(1)}, f32[8,10,3,128]{3,2,1,0:T(4,128)S(1)}, u32[]{:S(2)}, u32[]{:S(2)}) collective-permute-start(f32[8,10,3,128]{3,2,1,0:T(4,128)S(1)} %get-tuple-element.16), channel_id=1, source_target_pairs={{0,8},{8,0},{16,24},{24,16},{32,40},{40,32},{48,56},{56,48},{1,9},... | collective-permute-start | bytes 368648 | tf_op jit(solution)/shard_map/ppermute | solution.py:427
  38.9 12.5 %collective-permute-start.12 = (f32[3,10,16,128]{3,2,1,0:T(8,128)S(1)}, f32[3,10,16,128]{3,2,1,0:T(8,128)S(1)}, u32[]{:S(2)}, u32[]{:S(2)}) collective-permute-start(f32[3,10,16,128]{3,2,1,0:T(8,128)S(1)} %get-tuple-element.27), channel_id=1, source_target_pairs={{0,192},{64,0},{128,64},{192,128},{1,193},{65,1},{129,65},{193,129... | collective-permute-start | bytes 737288 | tf_op jit(solution)/shard_map/ppermute | solution.py:427
  40.3 11.0 %collective-permute-start.11 = (f32[3,10,16,128]{3,2,1,0:T(8,128)S(1)}, f32[3,10,16,128]{3,2,1,0:T(8,128)S(1)}, u32[]{:S(2)}, u32[]{:S(2)}) collective-permute-start(f32[3,10,16,128]{3,2,1,0:T(8,128)S(1)} %get-tuple-element.28), channel_id=1, source_target_pairs={{0,64},{64,128},{128,192},{192,0},{1,65},{65,129},{129,193},{193,1... | collective-permute-start | bytes 737288 | tf_op jit(solution)/shard_map/ppermute | solution.py:427
  42.2 12.3 %collective-permute-start.15 = (f32[8,3,16,128]{3,2,1,0:T(8,128)S(1)}, f32[8,3,16,128]{3,2,1,0:T(8,128)S(1)}, u32[]{:S(2)}, u32[]{:S(2)}) collective-permute-start(f32[8,3,16,128]{3,2,1,0:T(8,128)S(1)} %get-tuple-element.18), channel_id=1, source_target_pairs={{0,1},{1,2},{2,3},{3,4},{4,5},{5,6},{6,7},{7,0},{8,9},{9,10},{10,1... | collective-permute-start | bytes 589832 | tf_op jit(solution)/shard_map/ppermute | solution.py:427
  42.2 12.3 %collective-permute-start.16 = (f32[8,3,16,128]{3,2,1,0:T(8,128)S(1)}, f32[8,3,16,128]{3,2,1,0:T(8,128)S(1)}, u32[]{:S(2)}, u32[]{:S(2)}) collective-permute-start(f32[8,3,16,128]{3,2,1,0:T(8,128)S(1)} %get-tuple-element.19), channel_id=1, source_target_pairs={{0,7},{1,0},{2,1},{3,2},{4,3},{5,4},{6,5},{7,6},{8,15},{9,8},{10,9... | collective-permute-start | bytes 589832 | tf_op jit(solution)/shard_map/ppermute | solution.py:427
  45.4 6.0 %collective-permute-start.14 = (f32[8,10,3,128]{3,2,1,0:T(4,128)S(1)}, f32[8,10,3,128]{3,2,1,0:T(4,128)S(1)}, u32[]{:S(2)}, u32[]{:S(2)}) collective-permute-start(f32[8,10,3,128]{3,2,1,0:T(4,128)S(1)} %get-tuple-element.17), channel_id=1, source_target_pairs={{0,56},{8,16},{16,8},{24,32},{32,24},{40,48},{48,40},{56,0},{1,57}... | collective-permute-start | bytes 368648 | tf_op jit(solution)/shard_map/ppermute | solution.py:427
  56.1 6.7 %collective-permute-start.19 = (f32[8,10,3,128]{3,2,1,0:T(4,128)S(1)}, f32[8,10,3,128]{3,2,1,0:T(4,128)S(1)}, u32[]{:S(2)}, u32[]{:S(2)}) collective-permute-start(f32[8,10,3,128]{3,2,1,0:T(4,128)S(1)} %get-tuple-element.21), channel_id=1, source_target_pairs={{0,8},{8,0},{16,24},{24,16},{32,40},{40,32},{48,56},{56,48},{1,9},... | collective-permute-start | bytes 368648 | tf_op jit(solution)/shard_map/ppermute | solution.py:427
  56.3 12.5 %collective-permute-start.18 = (f32[3,10,16,128]{3,2,1,0:T(8,128)S(1)}, f32[3,10,16,128]{3,2,1,0:T(8,128)S(1)}, u32[]{:S(2)}, u32[]{:S(2)}) collective-permute-start(f32[3,10,16,128]{3,2,1,0:T(8,128)S(1)} %get-tuple-element.25), channel_id=1, source_target_pairs={{0,192},{64,0},{128,64},{192,128},{1,193},{65,1},{129,65},{193,129... | collective-permute-start | bytes 737288 | tf_op jit(solution)/shard_map/ppermute | solution.py:427
  56.5 12.3 %collective-permute-start.17 = (f32[3,10,16,128]{3,2,1,0:T(8,128)S(1)}, f32[3,10,16,128]{3,2,1,0:T(8,128)S(1)}, u32[]{:S(2)}, u32[]{:S(2)}) collective-permute-start(f32[3,10,16,128]{3,2,1,0:T(8,128)S(1)} %get-tuple-element.26), channel_id=1, source_target_pairs={{0,64},{64,128},{128,192},{192,0},{1,65},{65,129},{129,193},{193,1... | collective-permute-start | bytes 737288 | tf_op jit(solution)/shard_map/ppermute | solution.py:427
  59.6 12.3 %collective-permute-start.21 = (f32[8,3,16,128]{3,2,1,0:T(8,128)S(1)}, f32[8,3,16,128]{3,2,1,0:T(8,128)S(1)}, u32[]{:S(2)}, u32[]{:S(2)}) collective-permute-start(f32[8,3,16,128]{3,2,1,0:T(8,128)S(1)} %get-tuple-element.23), channel_id=1, source_target_pairs={{0,1},{1,2},{2,3},{3,4},{4,5},{5,6},{6,7},{7,0},{8,9},{9,10},{10,1... | collective-permute-start | bytes 589832 | tf_op jit(solution)/shard_map/ppermute | solution.py:427
  59.6 12.3 %collective-permute-start.22 = (f32[8,3,16,128]{3,2,1,0:T(8,128)S(1)}, f32[8,3,16,128]{3,2,1,0:T(8,128)S(1)}, u32[]{:S(2)}, u32[]{:S(2)}) collective-permute-start(f32[8,3,16,128]{3,2,1,0:T(8,128)S(1)} %get-tuple-element.24), channel_id=1, source_target_pairs={{0,7},{1,0},{2,1},{3,2},{4,3},{5,4},{6,5},{7,6},{8,15},{9,8},{10,9... | collective-permute-start | bytes 589832 | tf_op jit(solution)/shard_map/ppermute | solution.py:427
  62.8 6.0 %collective-permute-start.20 = (f32[8,10,3,128]{3,2,1,0:T(4,128)S(1)}, f32[8,10,3,128]{3,2,1,0:T(4,128)S(1)}, u32[]{:S(2)}, u32[]{:S(2)}) collective-permute-start(f32[8,10,3,128]{3,2,1,0:T(4,128)S(1)} %get-tuple-element.22), channel_id=1, source_target_pairs={{0,56},{8,16},{16,8},{24,32},{32,24},{40,48},{48,40},{56,0},{1,57}... | collective-permute-start | bytes 368648 | tf_op jit(solution)/shard_map/ppermute | solution.py:427

commit v4 on v3

--- a/solution.py
+++ b/solution.py
@@ -101,7 +101,8 @@
 
 
 def speed_kernel(u_ref, *refs, d_speed, blocks):
-    out_ref, turned, bent, up_ref, down_ref, pair_ref, fourth_ref, done_ref = refs[-8:]
+    out_ref, turned, done_ref, *scratch = refs[-13:]
+    sets = scratch[:5], scratch[5:]
     nv = u_ref.shape[1]
     floor = floor_of(d_speed)
     top = 1.0 / (floor * floor)
@@ -109,70 +110,62 @@
 
     for b in range(*blocks):
         turned[b, first:last] = u_ref[128 * b : 128 * b + 128].T
-
-    def bends(b, carry):
-        zero = jnp.zeros((8, 128), jnp.float32)
+    if blocks[0] > 0:
+        out_ref[0 : 128 * blocks[0]] = refs[0][0 : 128 * blocks[0]]
+    zero = jnp.zeros((8, 128), jnp.float32)
+    for bent, up_ref, down_ref, pair_ref, fourth_ref in sets:
+        for ref in (bent, fourth_ref):
+            ref[first - 8 : first] = zero
+            ref[last : last + 8] = zero
+        down_ref[first - 8 : first] = zero + top
+        up_ref[last : last + 8] = zero + top
+        pair_ref[last : last + 8] = zero + 6.0 * top
+    for b in range(*blocks):
         turned[b, first - 1 : first] = (
             2.0 * turned[b, first : first + 1] - turned[b, first + 1 : first + 2]
         )
         turned[b, last : last + 1] = (
             2.0 * turned[b, last - 1 : last] - turned[b, last - 2 : last - 1]
         )
-        for ref, low, high in (
-            (bent, zero, zero),
-            (fourth_ref, zero, zero),
-            (down_ref, zero + top, None),
-            (up_ref, None, zero + top),
-            (pair_ref, None, zero + 6.0 * top),
-        ):
-            if low is not None:
-                ref[b, first - 8 : first] = low
-            if high is not None:
-                ref[b, last : last + 8] = high
+
+    def work(b, bent, up_ref, down_ref, pair_ref, fourth_ref):
         for r in range(first, last, 8):
             here = turned[b, r : r + 8]
-            bent[b, r : r + 8] = (turned[b, r + 1 : r + 9] - here) - (
-                here - turned[b, r - 1 : r + 7]
-            )
-        return carry
-
-    lax.fori_loop(*blocks, bends, 0)
-
-    def weights(b, carry):
+            bent[r : r + 8] = (turned[b, r + 1 : r + 9] - here) - (here - turned[b, r - 1 : r + 7])
         for r in range(first, last, 8):
-            below, bend, above = (bent[b, r + d : r + d + 8] for d in (-1, 0, 1))
+            below, bend, above = (bent[r + d : r + d + 8] for d in (-1, 0, 1))
             rest = squared(bend) * REST + floor
             lean = bend * LEAN
-            up_ref[b, r : r + 8] = inverse_square(squared(above - lean) + rest)
-            down_ref[b, r : r + 8] = inverse_square(squared(below - lean) + rest)
-            pair_ref[b, r : r + 8] = inverse_square(squared(below - bend * LEVEL) + rest) * 6.0
-            fourth_ref[b, r : r + 8] = ((above - bend) - (bend - below)) * (2.0 / 3.0)
-        return carry
-
-    lax.fori_loop(*blocks, weights, 0)
-
-    def combine(b, carry):
+            up_ref[r : r + 8] = inverse_square(squared(above - lean) + rest)
+            down_ref[r : r + 8] = inverse_square(squared(below - lean) + rest)
+            pair_ref[r : r + 8] = inverse_square(squared(below - bend * LEVEL) + rest) * 6.0
+            fourth_ref[r : r + 8] = ((above - bend) - (bend - below)) * (2.0 / 3.0)
         for r in range(first, last, 8):
-            half = 0.5 * fourth_ref[b, r : r + 8]
-            up_3 = up_ref[b, r : r + 8] * 3.0
-            down_3 = down_ref[b, r : r + 8] * 3.0
-            up_after = up_ref[b, r + 1 : r + 9]
-            down_before = down_ref[b, r - 1 : r + 7]
+            half = 0.5 * fourth_ref[r : r + 8]
+            up_3 = up_ref[r : r + 8] * 3.0
+            down_3 = down_ref[r : r + 8] * 3.0
+            up_after = up_ref[r + 1 : r + 9]
+            down_before = down_ref[r - 1 : r + 7]
             middle = (turned[b, r + 1 : r + 9] - turned[b, r - 1 : r + 7]) - (
-                bent[b, r + 1 : r + 9] - bent[b, r - 1 : r + 7]
+                bent[r + 1 : r + 9] - bent[r - 1 : r + 7]
             ) * (1.0 / 6.0)
-            right = (up_after * fourth_ref[b, r + 1 : r + 9] + down_3 * half) / (
-                up_after + down_3 + pair_ref[b, r + 1 : r + 9]
+            right = (up_after * fourth_ref[r + 1 : r + 9] + down_3 * half) / (
+                up_after + down_3 + pair_ref[r + 1 : r + 9]
             )
-            left = (down_before * fourth_ref[b, r - 1 : r + 7] + up_3 * half) / (
-                down_before + up_3 + pair_ref[b, r : r + 8]
+            left = (down_before * fourth_ref[r - 1 : r + 7] + up_3 * half) / (
+                down_before + up_3 + pair_ref[r : r + 8]
             )
             done_ref[b, r : r + 8] = (jnp.maximum(right + middle, left - middle) - 0.5 * half) * (
                 0.5 * ACCEL_MAX / d_speed
             )
+
+    def two(i, carry):
+        b = blocks[0] + 2 * i
+        work(b, *sets[0])
+        work(b + 1, *sets[1])
         return carry
 
-    lax.fori_loop(*blocks, combine, 0)
+    lax.fori_loop(0, (blocks[1] - blocks[0]) // 2, two, 0)
     for b in range(*blocks):
         out_ref[128 * b : 128 * b + 128] = done_ref[b, first:last].T
 
@@ -184,15 +177,12 @@
     return one, two, two + slope
 
 
-def plane_kernel(
-    u_ref, part_ref, xlo, xhi, ymate, yother, vel_ref, wind_ref, acc_ref, pad_ref, bend_ref
+def rows_kernel(
+    u_ref, part_ref, ymate, yother, vel_ref, wind_ref, acc_ref, pad_ref, bend_ref
 ):
     nx, nh, ny, nv = u_ref.shape
-    halves = ny // 8
     floor = floor_of(CELL_SIZE)
-    gx, gy = lax.axis_index("gx"), lax.axis_index("gy")
-    start_x = gx == 0
-    end_x = gx == lax.axis_size("gx") - 1
+    gy = lax.axis_index("gy")
     at_edge = jnp.logical_or(gy == 0, gy == lax.axis_size("gy") - 1)
     odd = lax.rem(gy, 2)
     mate_at = 8 + ny - odd * (ny + 3)
@@ -234,45 +224,64 @@
 
     lax.fori_loop(0, nx, along_y, 0)
 
-    def along_x(h, carry):
+
+def columns_kernel(u_ref, part_ref, xmate, xother, vel_ref, wind_ref, acc_ref):
+    nx, nh, ny, _ = u_ref.shape
+    halves = ny // 8
+    floor = floor_of(CELL_SIZE)
+    gx = lax.axis_index("gx")
+    at_x_edge = jnp.logical_or(gx == 0, gx == lax.axis_size("gx") - 1)
+    x_even = lax.rem(gx, 2) == 0
+
+    def along_x(h, carry, mate_above):
         for half in range(halves):
             rows = slice(8 * half, 8 * half + 8)
             mine = [u_ref[x, h, rows] for x in range(nx)]
-            low = ghosts(mine[0], mine[1])
-            high = ghosts(mine[nx - 1], mine[nx - 2])
-            line = (
-                [jnp.where(start_x, low[2 - r], xlo[r, h, rows]) for r in range(3)]
-                + mine
-                + [jnp.where(end_x, high[r], xhi[r, h, rows]) for r in range(3)]
-            )
+            near = [xmate[r, h, rows] for r in range(3)]
+            if mate_above:
+                past = ghosts(mine[0], mine[1])[::-1]
+            else:
+                past = ghosts(mine[nx - 1], mine[nx - 2])
+            away = [jnp.where(at_x_edge, past[r], xother[r, h, rows]) for r in range(3)]
+            line = away + mine + near if mate_above else near + mine + away
             fourth, to_up, to_down, pair, middle = column_parts(line, floor)
             speed = vel_ref[0, h]
             for x in range(nx):
                 flow = speed + wind_ref[0, x, rows]
-                acc_ref[x, h, rows] = acc_ref[x, h, rows] + picked(
+                acc_ref[x, h, rows] = part_ref[x, h, rows] + picked(
                     flow, fourth, to_up, to_down, pair, middle, x
                 )
         return carry
 
-    lax.fori_loop(0, nh, along_x, 0)
+    @pl.when(x_even)
+    def _():
+        lax.fori_loop(0, nh, functools.partial(along_x, mate_above=True), 0)
+
+    @pl.when(jnp.logical_not(x_even))
+    def _():
+        lax.fori_loop(0, nh, functools.partial(along_x, mate_above=False), 0)
 
 
 def heading_kernel(top_ref, u_ref, acc_ref, *refs, stage, d_theta, d_speed):
     refs = list(refs)
     base_ref = refs.pop(0) if stage > 1 else None
-    hlo, hhi, out_ref, *faces = refs
+    hmate, hother, out_ref, *faces = refs
     if stage == 3:
         whole_ref, out_ref, sent = out_ref, *faces
         faces = None
     nx, nh, ny, _ = u_ref.shape
     halves = ny // 8
-    mate_row = (1 - lax.rem(lax.axis_index("gy"), 2)) * (ny - 3)
+    x_even, y_even, h_even = (1 - lax.rem(lax.axis_index(a), 2) for a in ("gx", "gy", "ha"))
+    mate_row = y_even * (ny - 3)
+    mate_head = h_even * (nh - 3)
+    mate_x = x_even * (nx - 3)
     dt = CFL_NUMBER / (
         top_ref[...] * (1.0 / CELL_SIZE) + (TURN_MAX / d_theta + ACCEL_MAX / d_speed)
     )
     theta_floor = floor_of(d_theta)
 
-    def along_heading(x, carry):
+    def along_heading(x, carry, mate_above):
+        hlo, hhi = (hother, hmate) if mate_above else (hmate, hother)
         for half in range(halves):
             rows = slice(8 * half, 8 * half + 8)
             line = (
@@ -296,23 +305,56 @@
                 else:
                     value = (2.0 / 3.0) * ((u - base_ref[x, h, rows]) + change)
                 out_ref[x, h, rows] = value
-                if stage < 3:
-                    if h < 3:
-                        faces[2][x, h, rows] = value
-                    if h >= nh - 3:
-                        faces[3][x, h - nh + 3, rows] = value
         if stage < 3:
             for h in range(nh):
                 faces[0][x, h] = out_ref[x, h, pl.ds(mate_row, 3)]
                 faces[1][x, h] = out_ref[x, h, pl.ds(ny - 3 - mate_row, 3)]
+            for r in range(3):
+                faces[2][x, r] = out_ref[x, mate_head + r]
+                faces[3][x, r] = out_ref[x, nh - 3 - mate_head + r]
         else:
             pltpu.make_async_copy(out_ref.at[x], whole_ref.at[x], sent.at[x]).start()
         return carry
 
-    lax.fori_loop(0, nx, along_heading, 0)
+    @pl.when(h_even == 1)
+    def _():
+        lax.fori_loop(0, nx, functools.partial(along_heading, mate_above=True), 0)
+
+    @pl.when(h_even == 0)
+    def _():
+        lax.fori_loop(0, nx, functools.partial(along_heading, mate_above=False), 0)
+
+    if stage < 3:
+        for r in range(3):
+            for h in range(nh):
+                faces[4][r, h] = out_ref[mate_x + r, h]
+                faces[5][r, h] = out_ref[nx - 3 - mate_x + r, h]
     if stage == 3:
         for x in range(nx):
             pltpu.make_async_copy(out_ref.at[x], whole_ref.at[x], sent.at[x]).wait()
+
+
+def face_kernel(u_ref, *faces):
+    nx, nh, ny, _ = u_ref.shape
+    x_even, y_even, h_even = (1 - lax.rem(lax.axis_index(a), 2) for a in ("gx", "gy", "ha"))
+    mate_row = y_even * (ny - 3)
+    mate_head = h_even * (nh - 3)
+    mate_x = x_even * (nx - 3)
+
+    def planes(x, carry):
+        for h in range(nh):
+            faces[0][x, h] = u_ref[x, h, pl.ds(mate_row, 3)]
+            faces[1][x, h] = u_ref[x, h, pl.ds(ny - 3 - mate_row, 3)]
+        for r in range(3):
+            faces[2][x, r] = u_ref[x, mate_head + r]
+            faces[3][x, r] = u_ref[x, nh - 3 - mate_head + r]
+        return carry
+
+    lax.fori_loop(0, nx, planes, 0)
+    for r in range(3):
+        for h in range(nh):
+            faces[4][r, h] = u_ref[mate_x + r, h]
+            faces[5][r, h] = u_ref[nx - 3 - mate_x + r, h]
 
 
 def rate_kernel(wind_ref, out_ref, *, spots):
@@ -361,8 +403,18 @@
     wind = jnp.broadcast_to((wind_field * (0.5 / CELL_SIZE))[..., None], (2, nx, ny, nv))
 
     shape = jax.ShapeDtypeStruct(field.shape, jnp.float32)
+    x_face = jax.ShapeDtypeStruct((3, nh, ny, nv), jnp.float32)
     y_face = jax.ShapeDtypeStruct((nx, nh, 3, nv), jnp.float32)
     h_face = jax.ShapeDtypeStruct((nx, 3, ny, nv), jnp.float32)
+    all_faces = [y_face, y_face, h_face, h_face, x_face, x_face]
+    faces = pl.pallas_call(
+        face_kernel,
+        out_shape=all_faces,
+        in_specs=[VMEM],
+        out_specs=[VMEM] * 6,
+        compiler_params=pltpu.CompilerParams(vmem_limit_bytes=8 << 20),
+        name="faces",
+    )(field)
 
     def speed_part(u, share=(0, 1), filled=()):
         flat = (nx * nh * ny, nv)
@@ -374,8 +426,8 @@
             out_shape=jax.ShapeDtypeStruct(flat, jnp.float32),
             in_specs=[VMEM] * (1 + len(filled)),
             out_specs=VMEM,
-            input_output_aliases={1: 0} if filled else {},
-            scratch_shapes=[pltpu.VMEM((count, nv + 16, 128), jnp.float32)] * 7,
+            scratch_shapes=[pltpu.VMEM((count, nv + 16, 128), jnp.float32)] * 2
+            + [pltpu.VMEM((nv + 16, 128), jnp.float32)] * 10,
             cost_estimate=pl.CostEstimate(
                 flops=100 * nx * nh * ny * nv, bytes_accessed=8 * nx * nh * ny * nv, transcendentals=0
             ),
@@ -383,28 +435,41 @@
             name="speed",
         )(u.reshape(flat), *(f.reshape(flat) for f in filled)).reshape(u.shape)
 
-    def plane_part(u, part, xlo, xhi, ymate, yother):
+    def rows_part(u, part, ymate, yother):
         return pl.pallas_call(
-            plane_kernel,
+            rows_kernel,
             out_shape=shape,
-            in_specs=[VMEM] * 8,
+            in_specs=[VMEM] * 6,
             out_specs=VMEM,
             scratch_shapes=[
                 pltpu.VMEM((nx, nh, ny + 16, nv), jnp.float32),
                 pltpu.VMEM((nx, nh, UP, nv), jnp.float32),
             ],
             cost_estimate=pl.CostEstimate(
-                flops=200 * nx * nh * ny * nv, bytes_accessed=16 * nx * nh * ny * nv, transcendentals=0
+                flops=100 * nx * nh * ny * nv, bytes_accessed=16 * nx * nh * ny * nv, transcendentals=0
             ),
             compiler_params=pltpu.CompilerParams(vmem_limit_bytes=24 << 20),
-            name="plane",
-        )(u, part, xlo, xhi, ymate, yother, velocity, wind)
-
-    def heading_part(stage, u, acc, hlo, hhi):
+            name="rows",
+        )(u, part, ymate, yother, velocity, wind)
+
+    def columns_part(u, part, xmate, xother):
+        return pl.pallas_call(
+            columns_kernel,
+            out_shape=shape,
+            in_specs=[VMEM] * 6,
+            out_specs=VMEM,
+            cost_estimate=pl.CostEstimate(
+                flops=100 * nx * nh * ny * nv, bytes_accessed=16 * nx * nh * ny * nv, transcendentals=0
+            ),
+            compiler_params=pltpu.CompilerParams(vmem_limit_bytes=24 << 20),
+            name="columns",
+        )(u, part, xmate, xother, velocity, wind)
+
+    def heading_part(stage, u, acc, hmate, hother):
         outs = [shape]
         if stage < 3:
-            outs += [y_face, y_face, h_face, h_face]
-        ins = [top, u, acc] + ([field] if stage > 1 else []) + [hlo, hhi]
+            outs += all_faces
+        ins = [top, u, acc] + ([field] if stage > 1 else []) + [hmate, hother]
         return pl.pallas_call(
             functools.partial(heading_kernel, stage=stage, d_theta=d_theta, d_speed=d_speed),
             out_shape=outs,
@@ -421,41 +486,39 @@
             compiler_params=pltpu.CompilerParams(vmem_limit_bytes=24 << 20),
         )(*ins)
 
-    def exchange(u, y_mate, y_other, h_first, h_last):
-        def halo(value, axis, step):
+    def exchange(y_mate, y_other, h_mate, h_other, x_mate, x_other):
+        def halo(name, value, axis):
             count = lax.axis_size(axis)
-            return lax.ppermute(value, axis, [(i, step(i) % count) for i in range(count)])
-
-        xlo = halo(u[nx - 3 :], "gx", lambda i: i + 1)
-        xhi = halo(u[:3], "gx", lambda i: i - 1)
-        ymate = halo(y_mate, "gy", lambda i: i ^ 1)
-        yother = halo(y_other, "gy", lambda i: i + 1 if i % 2 else i - 1)
-        hlo = halo(h_last, "ha", lambda i: i + 1)
-        hhi = halo(h_first, "ha", lambda i: i - 1)
-        return xlo, xhi, ymate, yother, hlo, hhi
+            if name[1] == "a":
+                pairs = [(i, i ^ 1) for i in range(count)]
+            else:
+                pairs = [(i, (i + 1 if i % 2 else i - 1) % count) for i in range(count)]
+            return lax.ppermute(value, axis, pairs)
+
+        return (
+            halo("xa", x_mate, "gx"),
+            halo("xb", x_other, "gx"),
+            halo("ya", y_mate, "gy"),
+            halo("yb", y_other, "gy"),
+            halo("ha", h_mate, "ha"),
+            halo("hb", h_other, "ha"),
+        )
 
     for axis, bit in [("gx", 1), ("gx", 2), ("gy", 1), ("gy", 2), ("gy", 4)]:
         other = lax.ppermute(top, axis, [(j, j ^ bit) for j in range(lax.axis_size(axis))])
         top = jnp.maximum(top, other)
 
-    even = lax.axis_index("gy") % 2 == 0
-    y_first, y_last = field[:, :, :3], field[:, :, ny - 3 :]
-    faces = (
-        jnp.where(even, y_last, y_first),
-        jnp.where(even, y_first, y_last),
-        field[:, :3],
-        field[:, nh - 3 :],
-    )
     u = field
     for stage in (1, 2, 3):
-        xlo, xhi, ymate, yother, hlo, hhi = exchange(u, *faces)
+        xmate, xother, ymate, yother, hmate, hother = exchange(*faces)
         if stage > 1:
             part = speed_part(u)
         else:
-            part = speed_part(u, (0, 0.5))
-            part = speed_part(u, (0.5, 1), (part,))
-        acc = plane_part(u, part, xlo, xhi, ymate, yother)
-        u, *faces = heading_part(stage, u, acc, hlo, hhi)
+            part = speed_part(u, (0, 0.4))
+            part = speed_part(u, (0.4, 1), (part,))
+        acc = rows_part(u, part, ymate, yother)
+        acc = columns_part(u, acc, xmate, xother)
+        u, *faces = heading_part(stage, u, acc, hmate, hother)
     return jnp.transpose(u, (0, 2, 1, 3))
 
 

time: 74.4 us -> 70.5 us (0.948)
  the two profiles are of different devices: /device:TPU:6 before, /device:TPU:1 now
where the time goes in v4:
time: 70.5 us; the launch traced here: 70.4 us
  starting transfers between devices  36.2 us (51%)
  Pallas kernels  20.4 us (29%)
  waiting for transfers between devices  11.4 us (16%)
  local copies, waits for them, and re-layouts  1.88 us (3%)
    ppermute x18, starting transfers between devices, halo(): return lax.ppermute(value, axis, pairs)  27.5 us
    ppermute x5, starting transfers between devices, body(): lax.ppermute(top, axis, [(j, j ^ bit) for j in range(lax.axis_size(axis))])  8.68 us
    ppermute x5, waiting for transfers between devices, body(): lax.ppermute(top, axis, [(j, j ^ bit) for j in range(lax.axis_size(axis))])  6.52 us
    pallas_call x3, Pallas kernels, heading_part(): pl.pallas_call(functools.partial(heading_kernel, stage=stage, d_theta=d_t...  5.48 us
    pallas_call x4, Pallas kernels, speed_part(): pl.pallas_call(functools.partial(speed_kernel, d_speed=d_speed, blocks=tu...  5.2 us
    pallas_call x3, Pallas kernels, rows_part(): pl.pallas_call(rows_kernel, out_shape=shape, in_specs=[VMEM] * 6, out_spe...  5.06 us
    ppermute x18, waiting for transfers between devices, halo(): return lax.ppermute(value, axis, pairs)  4.83 us
    pallas_call x3, Pallas kernels, columns_part(): pl.pallas_call(columns_kernel, out_shape=shape, in_specs=[VMEM] * 6, out_...  4.18 us
  transfers between devices with their start and end apart: 23, of which 5 were waited for; matrix products, arithmetic and copies ran while one was open for 0% of the time, Pallas kernels for 21%

profile of v4, /device:TPU:1, one launch (start us, length us, event | category | flops | bytes accessed | tf_op | source)
XLA Modules:
  0.0 70.4 jit_solution(18212664421199472498)
XLA Ops:
  0.0 0.7 copy-done.2
  0.7 0.3 rate.1
  1.0 2.1 %collective-permute-start = (f32[8,128]{1,0:T(8,128)S(1)}, f32[8,128]{1,0:T(8,128)S(1)}, u32[]{:S(2)}, u32[]{:S(2)}) collective-permute-start(f32[8,128]{1,0:T(8,128)S(1)} %rate.1), channel_id=1, source_target_pairs={{0,64},{64,0},{128,192},{192,128},{1,65},{65,1},{129,193},{193,129... | collective-permute-start | bytes 12296 | tf_op jit(solution)/shard_map/ppermute | solution.py:508
  3.1 1.1 %copy-done = f32[8,16,10,128]{3,1,2,0:T(8,128)S(1)} copy-done((f32[8,16,10,128]{3,1,2,0:T(8,128)S(1)}, f32[8,16,10,128]{3,1,2,0:T(8,128)}, u32[]{:S(2)}) %copy-start) | copy-done | bytes 655384
  4.2 0.2 faces.1
  4.4 1.3 %collective-permute-start.5 = (f32[8,10,3,128]{3,2,1,0:T(4,128)S(1)}, f32[8,10,3,128]{3,2,1,0:T(4,128)S(1)}, u32[]{:S(2)}, u32[]{:S(2)}) collective-permute-start(f32[8,10,3,128]{3,2,1,0:T(4,128)S(1)} %get-tuple-element.25), channel_id=1, source_target_pairs={{0,8},{8,0},{16,24},{24,16},{32,40},{40,32},{48,56},{56,48},{1,9},... | collective-permute-start | bytes 368648 | tf_op jit(solution)/shard_map/ppermute | solution.py:496
  5.6 1.0 %collective-permute-start.6 = (f32[8,10,3,128]{3,2,1,0:T(4,128)S(1)}, f32[8,10,3,128]{3,2,1,0:T(4,128)S(1)}, u32[]{:S(2)}, u32[]{:S(2)}) collective-permute-start(f32[8,10,3,128]{3,2,1,0:T(4,128)S(1)} %get-tuple-element.26), channel_id=1, source_target_pairs={{0,56},{8,16},{16,8},{24,32},{32,24},{40,48},{48,40},{56,0},{1,57}... | collective-permute-start | bytes 368648 | tf_op jit(solution)/shard_map/ppermute | solution.py:496
  6.7 0.7 collective-permute-start.7
  7.4 2.0 %collective-permute-start.8 = (f32[3,10,16,128]{3,2,1,0:T(8,128)S(1)}, f32[3,10,16,128]{3,2,1,0:T(8,128)S(1)}, u32[]{:S(2)}, u32[]{:S(2)}) collective-permute-start(f32[3,10,16,128]{3,2,1,0:T(8,128)S(1)} %get-tuple-element.28), channel_id=1, source_target_pairs={{0,192},{64,128},{128,64},{192,0},{1,193},{65,129},{129,65},{193,1... | collective-permute-start | bytes 737288 | tf_op jit(solution)/shard_map/ppermute | solution.py:496
  9.4 0.5 collective-permute-start.1
  10.0 3.7 %collective-permute-done.1 = f32[8,128]{1,0:T(8,128)S(1)} collective-permute-done((f32[8,128]{1,0:T(8,128)S(1)}, f32[8,128]{1,0:T(8,128)S(1)}, u32[]{:S(2)}, u32[]{:S(2)}) %collective-permute-start.1) | collective-permute-done | bytes 4128 | tf_op jit(solution)/shard_map/ppermute | solution.py:508
  13.7 3.4 %collective-permute-start.2 = (f32[8,128]{1,0:T(8,128)S(1)}, f32[8,128]{1,0:T(8,128)S(1)}, u32[]{:S(2)}, u32[]{:S(2)}) collective-permute-start(f32[8,128]{1,0:T(8,128)S(1)} %max.16), channel_id=1, source_target_pairs={{0,8},{8,0},{16,24},{24,16},{32,40},{40,32},{48,56},{56,48},{1,9},... | collective-permute-start | bytes 12296 | tf_op jit(solution)/shard_map/ppermute | solution.py:508
  17.1 0.8 %collective-permute-done.2 = f32[8,128]{1,0:T(8,128)S(1)} collective-permute-done((f32[8,128]{1,0:T(8,128)S(1)}, f32[8,128]{1,0:T(8,128)S(1)}, u32[]{:S(2)}, u32[]{:S(2)}) %collective-permute-start.2) | collective-permute-done | bytes 4128 | tf_op jit(solution)/shard_map/ppermute | solution.py:508
  17.9 0.4 collective-permute-start.3
  18.3 2.0 %collective-permute-done.3 = f32[8,128]{1,0:T(8,128)S(1)} collective-permute-done((f32[8,128]{1,0:T(8,128)S(1)}, f32[8,128]{1,0:T(8,128)S(1)}, u32[]{:S(2)}, u32[]{:S(2)}) %collective-permute-start.3) | collective-permute-done | bytes 4128 | tf_op jit(solution)/shard_map/ppermute | solution.py:508
  20.3 2.3 %collective-permute-start.4 = (f32[8,128]{1,0:T(8,128)S(1)}, f32[8,128]{1,0:T(8,128)S(1)}, u32[]{:S(2)}, u32[]{:S(2)}) collective-permute-start(f32[8,128]{1,0:T(8,128)S(1)} %max.18), channel_id=1, source_target_pairs={{0,32},{8,40},{16,48},{24,56},{32,0},{40,8},{48,16},{56,24},{1,33}... | collective-permute-start | bytes 12296 | tf_op jit(solution)/shard_map/ppermute | solution.py:508
  22.6 0.1 broadcast_multiply_fusion.vel_ref
  22.7 0.8 %speed.4.refs_0_ = f32[1280,128]{1,0:T(8,128)S(1)} custom-call(f32[1280,128]{1,0:T(8,128)S(1)} %bitcast.10), custom_call_target="tpu_custom_call" | custom-call | flops 16384000 | bytes 1310720 | tf_op jit(solution)/shard_map/speed/pallas_call | solution.py:422
  23.5 0.0 copy-start.3
  23.5 1.1 %speed.5 = f32[1280,128]{1,0:T(8,128)S(1)} custom-call(f32[1280,128]{1,0:T(8,128)S(1)} %bitcast.11, f32[1280,128]{1,0:T(8,128)S(1)} %speed.4.refs_0_), custom_call_target="tpu_custom_call" | custom-call | flops 16384000 | bytes 1310720 | tf_op jit(solution)/shard_map/speed/pallas_call | solution.py:422
  24.6 0.0 collective-permute-done.4
  24.6 1.7 %collective-permute-start.9 = (f32[8,3,16,128]{3,2,1,0:T(8,128)S(1)}, f32[8,3,16,128]{3,2,1,0:T(8,128)S(1)}, u32[]{:S(2)}, u32[]{:S(2)}) collective-permute-start(f32[8,3,16,128]{3,2,1,0:T(8,128)S(1)} %get-tuple-element.29), channel_id=1, source_target_pairs={{0,1},{1,0},{2,3},{3,2},{4,5},{5,4},{6,7},{7,6},{8,9},{9,8},{10,11... | collective-permute-start | bytes 589832 | tf_op jit(solution)/shard_map/ppermute | solution.py:496
  26.3 0.0 collective-permute-done.5.ymate
  26.3 4.7 %collective-permute-start.10 = (f32[8,3,16,128]{3,2,1,0:T(8,128)S(1)}, f32[8,3,16,128]{3,2,1,0:T(8,128)S(1)}, u32[]{:S(2)}, u32[]{:S(2)}) collective-permute-start(f32[8,3,16,128]{3,2,1,0:T(8,128)S(1)} %get-tuple-element.30), channel_id=1, source_target_pairs={{0,7},{1,2},{2,1},{3,4},{4,3},{5,6},{6,5},{7,0},{8,15},{9,10},{10,... | collective-permute-start | bytes 589832 | tf_op jit(solution)/shard_map/ppermute | solution.py:496
  31.0 0.1 broadcast_in_dim.5.wind_ref
  31.1 1.7 %rows.3.part_ref = f32[8,10,16,128]{3,2,1,0:T(8,128)S(1)} custom-call(f32[8,10,16,128]{3,2,1,0:T(8,128)S(1)} %bitcast.12, f32[8,10,16,128]{3,2,1,0:T(8,128)S(1)} %bitcast.21, f32[8,10,3,128]{3,2,1,0:T(4,128)S(1)} %collective-permute-done.5.ymate, f32[8,10,3,128]{3,2,1,0:T(4,128)S(1)} %collective-permute-done.6.yother, ...), custom_call_target="tpu_custom_call" | custom-call | flops 16384000 | bytes 2621440 | tf_op jit(solution)/shard_map/rows/pallas_call | solution.py:439
  32.8 1.4 %columns.3.acc_ref = f32[8,10,16,128]{3,2,1,0:T(8,128)S(1)} custom-call(f32[8,10,16,128]{3,2,1,0:T(8,128)S(1)} %bitcast.13, f32[8,10,16,128]{3,2,1,0:T(8,128)S(1)} %rows.3.part_ref, f32[3,10,16,128]{3,2,1,0:T(8,128)S(1)} %collective-permute-done.7.xmate, f32[3,10,16,128]{3,2,1,0:T(8,128)S(1)} %collective-permute-done.8.xother, ...), custom_call_target="tpu_custom_call" | custom-call | flops 16384000 | bytes 2621440 | tf_op jit(solution)/shard_map/columns/pallas_call | solution.py:456
  34.2 1.6 %shard_map.28 = (f32[8,10,16,128]{3,2,1,0:T(8,128)S(1)}, f32[8,10,3,128]{3,2,1,0:T(4,128)S(1)}, f32[8,10,3,128]{3,2,1,0:T(4,128)S(1)}, f32[8,3,16,128]{3,2,1,0:T...) custom-call(f32[8,128]{1,0:T(8,128)S(1)} %max.19.top_ref, ...), custom_call_target="tpu_custom_call" | custom-call | flops 16384000 | bytes 2621440 | tf_op jit(solution)/shard_map/pallas_call | solution.py:473
  35.8 3.2 %collective-permute-start.11 = (f32[8,10,3,128]{3,2,1,0:T(4,128)S(1)}, f32[8,10,3,128]{3,2,1,0:T(4,128)S(1)}, u32[]{:S(2)}, u32[]{:S(2)}) collective-permute-start(f32[8,10,3,128]{3,2,1,0:T(4,128)S(1)} %get-tuple-element.32), channel_id=1, source_target_pairs={{0,8},{8,0},{16,24},{24,16},{32,40},{40,32},{48,56},{56,48},{1,9},... | collective-permute-start | bytes 368648 | tf_op jit(solution)/shard_map/ppermute | solution.py:496
  39.1 0.0 collective-permute-start.13
  39.1 0.9 %collective-permute-start.14 = (f32[3,10,16,128]{3,2,1,0:T(8,128)S(1)}, f32[3,10,16,128]{3,2,1,0:T(8,128)S(1)}, u32[]{:S(2)}, u32[]{:S(2)}) collective-permute-start(f32[3,10,16,128]{3,2,1,0:T(8,128)S(1)} %get-tuple-element.35), channel_id=1, source_target_pairs={{0,192},{64,128},{128,64},{192,0},{1,193},{65,129},{129,65},{193,1... | collective-permute-start | bytes 737288 | tf_op jit(solution)/shard_map/ppermute | solution.py:496
  40.0 3.0 %collective-permute-start.16 = (f32[8,3,16,128]{3,2,1,0:T(8,128)S(1)}, f32[8,3,16,128]{3,2,1,0:T(8,128)S(1)}, u32[]{:S(2)}, u32[]{:S(2)}) collective-permute-start(f32[8,3,16,128]{3,2,1,0:T(8,128)S(1)} %get-tuple-element.37), channel_id=1, source_target_pairs={{0,7},{1,2},{2,1},{3,4},{4,3},{5,6},{6,5},{7,0},{8,15},{9,10},{10,... | collective-permute-start | bytes 589832 | tf_op jit(solution)/shard_map/ppermute | solution.py:496
  42.9 1.1 %collective-permute-start.12 = (f32[8,10,3,128]{3,2,1,0:T(4,128)S(1)}, f32[8,10,3,128]{3,2,1,0:T(4,128)S(1)}, u32[]{:S(2)}, u32[]{:S(2)}) collective-permute-start(f32[8,10,3,128]{3,2,1,0:T(4,128)S(1)} %get-tuple-element.33), channel_id=1, source_target_pairs={{0,56},{8,16},{16,8},{24,32},{32,24},{40,48},{48,40},{56,0},{1,57}... | collective-permute-start | bytes 368648 | tf_op jit(solution)/shard_map/ppermute | solution.py:496
  44.0 1.7 %speed.6 = f32[1280,128]{1,0:T(8,128)S(1)} custom-call(f32[1280,128]{1,0:T(8,128)S(1)} %bitcast.17), custom_call_target="tpu_custom_call" | custom-call | flops 16384000 | bytes 1310720 | tf_op jit(solution)/shard_map/speed/pallas_call | solution.py:422
  45.7 2.2 %collective-permute-done.12.yother = f32[8,10,3,128]{3,2,1,0:T(4,128)S(1)} collective-permute-done((f32[8,10,3,128]{3,2,1,0:T(4,128)S(1)}, f32[8,10,3,128]{3,2,1,0:T(4,128)S(1)}, u32[]{:S(2)}, u32[]{:S(2)}) %collective-permute-start.12) | collective-permute-done | bytes 122912 | tf_op jit(solution)/shard_map/ppermute | solution.py:496
  48.0 1.7 %rows.4.part_ref = f32[8,10,16,128]{3,2,1,0:T(8,128)S(1)} custom-call(f32[8,10,16,128]{3,2,1,0:T(8,128)S(1)} %get-tuple-element.31.u_ref, f32[8,10,16,128]{3,2,1,0:T(8,128)S(1)} %bitcast.19, f32[8,10,3,128]{3,2,1,0:T(4,128)S(1)} %collective-permute-done.11.ymate, f32[8,10,3,128]{3,2,1,0:T(4,128)S(1)} %collective-permute-done.12.yother, ...), custom_call_target="tpu_custom_call" | custom-call | flops 16384000 | bytes 2621440 | tf_op jit(solution)/shard_map/rows/pallas_call | solution.py:439
  49.7 1.4 %columns.4.acc_ref = f32[8,10,16,128]{3,2,1,0:T(8,128)S(1)} custom-call(f32[8,10,16,128]{3,2,1,0:T(8,128)S(1)} %get-tuple-element.31.u_ref, f32[8,10,16,128]{3,2,1,0:T(8,128)S(1)} %rows.4.part_ref, f32[3,10,16,128]{3,2,1,0:T(8,128)S(1)} %collective-permute-done.13.xmate, f32[3,10,16,128]{3,2,1,0:T(8,128)S(1)} %collective-permute-done.14.xother, ...), custom_call_target="tpu_custom_call" | custom-call | flops 16384000 | bytes 2621440 | tf_op jit(solution)/shard_map/columns/pallas_call | solution.py:456
  51.1 1.7 %shard_map.29 = (f32[8,10,16,128]{3,2,1,0:T(8,128)S(1)}, f32[8,10,3,128]{3,2,1,0:T(4,128)S(1)}, f32[8,10,3,128]{3,2,1,0:T(4,128)S(1)}, f32[8,3,16,128]{3,2,1,0:T...) custom-call(f32[8,128]{1,0:T(8,128)S(1)} %max.19.top_ref, ...), custom_call_target="tpu_custom_call" | custom-call | flops 16384000 | bytes 2621440 | tf_op jit(solution)/shard_map/pallas_call | solution.py:473
  52.8 1.9 %collective-permute-start.17 = (f32[8,10,3,128]{3,2,1,0:T(4,128)S(1)}, f32[8,10,3,128]{3,2,1,0:T(4,128)S(1)}, u32[]{:S(2)}, u32[]{:S(2)}) collective-permute-start(f32[8,10,3,128]{3,2,1,0:T(4,128)S(1)} %get-tuple-element.39), channel_id=1, source_target_pairs={{0,8},{8,0},{16,24},{24,16},{32,40},{40,32},{48,56},{56,48},{1,9},... | collective-permute-start | bytes 368648 | tf_op jit(solution)/shard_map/ppermute | solution.py:496
  54.7 0.7 collective-permute-start.19
  55.4 2.0 %collective-permute-start.20 = (f32[3,10,16,128]{3,2,1,0:T(8,128)S(1)}, f32[3,10,16,128]{3,2,1,0:T(8,128)S(1)}, u32[]{:S(2)}, u32[]{:S(2)}) collective-permute-start(f32[3,10,16,128]{3,2,1,0:T(8,128)S(1)} %get-tuple-element.42), channel_id=1, source_target_pairs={{0,192},{64,128},{128,64},{192,0},{1,193},{65,129},{129,65},{193,1... | collective-permute-start | bytes 737288 | tf_op jit(solution)/shard_map/ppermute | solution.py:496
  57.4 2.5 %collective-permute-start.22 = (f32[8,3,16,128]{3,2,1,0:T(8,128)S(1)}, f32[8,3,16,128]{3,2,1,0:T(8,128)S(1)}, u32[]{:S(2)}, u32[]{:S(2)}) collective-permute-start(f32[8,3,16,128]{3,2,1,0:T(8,128)S(1)} %get-tuple-element.44), channel_id=1, source_target_pairs={{0,7},{1,2},{2,1},{3,4},{4,3},{5,6},{6,5},{7,0},{8,15},{9,10},{10,... | collective-permute-start | bytes 589832 | tf_op jit(solution)/shard_map/ppermute | solution.py:496
  59.8 0.8 %collective-permute-start.18 = (f32[8,10,3,128]{3,2,1,0:T(4,128)S(1)}, f32[8,10,3,128]{3,2,1,0:T(4,128)S(1)}, u32[]{:S(2)}, u32[]{:S(2)}) collective-permute-start(f32[8,10,3,128]{3,2,1,0:T(4,128)S(1)} %get-tuple-element.40), channel_id=1, source_target_pairs={{0,56},{8,16},{16,8},{24,32},{32,24},{40,48},{48,40},{56,0},{1,57}... | collective-permute-start | bytes 368648 | tf_op jit(solution)/shard_map/ppermute | solution.py:496
  60.6 1.7 %speed.7 = f32[1280,128]{1,0:T(8,128)S(1)} custom-call(f32[1280,128]{1,0:T(8,128)S(1)} %bitcast.18), custom_call_target="tpu_custom_call" | custom-call | flops 16384000 | bytes 1310720 | tf_op jit(solution)/shard_map/speed/pallas_call | solution.py:422
  62.3 2.6 %collective-permute-done.18.yother = f32[8,10,3,128]{3,2,1,0:T(4,128)S(1)} collective-permute-done((f32[8,10,3,128]{3,2,1,0:T(4,128)S(1)}, f32[8,10,3,128]{3,2,1,0:T(4,128)S(1)}, u32[]{:S(2)}, u32[]{:S(2)}) %collective-permute-start.18) | collective-permute-done | bytes 122912 | tf_op jit(solution)/shard_map/ppermute | solution.py:496
  64.9 1.7 %rows.5.part_ref = f32[8,10,16,128]{3,2,1,0:T(8,128)S(1)} custom-call(f32[8,10,16,128]{3,2,1,0:T(8,128)S(1)} %get-tuple-element.38.u_ref, f32[8,10,16,128]{3,2,1,0:T(8,128)S(1)} %bitcast.20, f32[8,10,3,128]{3,2,1,0:T(4,128)S(1)} %collective-permute-done.17.ymate, f32[8,10,3,128]{3,2,1,0:T(4,128)S(1)} %collective-permute-done.18.yother, ...), custom_call_target="tpu_custom_call" | custom-call | flops 16384000 | bytes 2621440 | tf_op jit(solution)/shard_map/rows/pallas_call | solution.py:439
  66.6 1.4 %columns.5.acc_ref = f32[8,10,16,128]{3,2,1,0:T(8,128)S(1)} custom-call(f32[8,10,16,128]{3,2,1,0:T(8,128)S(1)} %get-tuple-element.38.u_ref, f32[8,10,16,128]{3,2,1,0:T(8,128)S(1)} %rows.5.part_ref, f32[3,10,16,128]{3,2,1,0:T(8,128)S(1)} %collective-permute-done.19.xmate, f32[3,10,16,128]{3,2,1,0:T(8,128)S(1)} %collective-permute-done.20.xother, ...), custom_call_target="tpu_custom_call" | custom-call | flops 16384000 | bytes 2621440 | tf_op jit(solution)/shard_map/columns/pallas_call | solution.py:456
  68.0 2.2 %shard_map.30 = f32[8,10,16,128]{3,2,1,0:T(8,128)} custom-call(f32[8,128]{1,0:T(8,128)S(1)} %max.19.top_ref, f32[8,10,16,128]{3,2,1,0:T(8,128)S(1)} %get-tuple-element.38.u_ref, f32[8,10,16,128]{3,2,1,0:T(8,128)S(1)} %columns.5.acc_ref, f32[8,10,16,128]{3,2,1,0:T(8,128)S(1)} %bitcast.16, f32[8,3,16,128]{3,2,1,0:T(8,128)S(1)} %collective-permute-done.21.refs_1_, ...), custom_call_target="tpu_custom_call" | custom-call | flops 16384000 | bytes 2621440 | tf_op jit(solution)/shard_map/pallas_call | solution.py:473
  (32 shorter events, 0.1 us)
Async XLA Ops:
  0.0 0.7 copy-start.2
  1.0 8.4 %collective-permute-start = (f32[8,128]{1,0:T(8,128)S(1)}, f32[8,128]{1,0:T(8,128)S(1)}, u32[]{:S(2)}, u32[]{:S(2)}) collective-permute-start(f32[8,128]{1,0:T(8,128)S(1)} %rate.1), channel_id=1, source_target_pairs={{0,64},{64,0},{128,192},{192,128},{1,65},{65,1},{129,193},{193,129... | collective-permute-start | bytes 12296 | tf_op jit(solution)/shard_map/ppermute | solution.py:508
  3.1 1.1 %copy-start = (f32[8,16,10,128]{3,1,2,0:T(8,128)S(1)}, f32[8,16,10,128]{3,1,2,0:T(8,128)}, u32[]{:S(2)}) copy-start(f32[8,16,10,128]{3,1,2,0:T(8,128)} %param.2) | copy-start | bytes 1966084
  4.2 18.5 %copy-start.1 = (f32[8,16,10,128]{3,1,2,0:T(8,128)S(1)}, f32[8,16,10,128]{3,1,2,0:T(8,128)}, u32[]{:S(2)}) copy-start(f32[8,16,10,128]{3,1,2,0:T(8,128)} %param.2) | copy-start | bytes 1966084
  4.4 21.9 %collective-permute-start.5 = (f32[8,10,3,128]{3,2,1,0:T(4,128)S(1)}, f32[8,10,3,128]{3,2,1,0:T(4,128)S(1)}, u32[]{:S(2)}, u32[]{:S(2)}) collective-permute-start(f32[8,10,3,128]{3,2,1,0:T(4,128)S(1)} %get-tuple-element.25), channel_id=1, source_target_pairs={{0,8},{8,0},{16,24},{24,16},{32,40},{40,32},{48,56},{56,48},{1,9},... | collective-permute-start | bytes 368648 | tf_op jit(solution)/shard_map/ppermute | solution.py:496
  5.6 25.3 %collective-permute-start.6 = (f32[8,10,3,128]{3,2,1,0:T(4,128)S(1)}, f32[8,10,3,128]{3,2,1,0:T(4,128)S(1)}, u32[]{:S(2)}, u32[]{:S(2)}) collective-permute-start(f32[8,10,3,128]{3,2,1,0:T(4,128)S(1)} %get-tuple-element.26), channel_id=1, source_target_pairs={{0,56},{8,16},{16,8},{24,32},{32,24},{40,48},{48,40},{56,0},{1,57}... | collective-permute-start | bytes 368648 | tf_op jit(solution)/shard_map/ppermute | solution.py:496
  6.7 26.1 %collective-permute-start.7 = (f32[3,10,16,128]{3,2,1,0:T(8,128)S(1)}, f32[3,10,16,128]{3,2,1,0:T(8,128)S(1)}, u32[]{:S(2)}, u32[]{:S(2)}) collective-permute-start(f32[3,10,16,128]{3,2,1,0:T(8,128)S(1)} %get-tuple-element.27), channel_id=1, source_target_pairs={{0,64},{64,0},{128,192},{192,128},{1,65},{65,1},{129,193},{193,129... | collective-permute-start | bytes 737288 | tf_op jit(solution)/shard_map/ppermute | solution.py:496
  7.4 25.4 %collective-permute-start.8 = (f32[3,10,16,128]{3,2,1,0:T(8,128)S(1)}, f32[3,10,16,128]{3,2,1,0:T(8,128)S(1)}, u32[]{:S(2)}, u32[]{:S(2)}) collective-permute-start(f32[3,10,16,128]{3,2,1,0:T(8,128)S(1)} %get-tuple-element.28), channel_id=1, source_target_pairs={{0,192},{64,128},{128,64},{192,0},{1,193},{65,129},{129,65},{193,1... | collective-permute-start | bytes 737288 | tf_op jit(solution)/shard_map/ppermute | solution.py:496
  9.4 4.3 %collective-permute-start.1 = (f32[8,128]{1,0:T(8,128)S(1)}, f32[8,128]{1,0:T(8,128)S(1)}, u32[]{:S(2)}, u32[]{:S(2)}) collective-permute-start(f32[8,128]{1,0:T(8,128)S(1)} %max.15), channel_id=1, source_target_pairs={{0,128},{64,192},{128,0},{192,64},{1,129},{65,193},{129,1},{193,65... | collective-permute-start | bytes 12296 | tf_op jit(solution)/shard_map/ppermute | solution.py:508
  13.7 4.2 %collective-permute-start.2 = (f32[8,128]{1,0:T(8,128)S(1)}, f32[8,128]{1,0:T(8,128)S(1)}, u32[]{:S(2)}, u32[]{:S(2)}) collective-permute-start(f32[8,128]{1,0:T(8,128)S(1)} %max.16), channel_id=1, source_target_pairs={{0,8},{8,0},{16,24},{24,16},{32,40},{40,32},{48,56},{56,48},{1,9},... | collective-permute-start | bytes 12296 | tf_op jit(solution)/shard_map/ppermute | solution.py:508
  17.9 2.5 %collective-permute-start.3 = (f32[8,128]{1,0:T(8,128)S(1)}, f32[8,128]{1,0:T(8,128)S(1)}, u32[]{:S(2)}, u32[]{:S(2)}) collective-permute-start(f32[8,128]{1,0:T(8,128)S(1)} %max.17), channel_id=1, source_target_pairs={{0,16},{8,24},{16,0},{24,8},{32,48},{40,56},{48,32},{56,40},{1,17}... | collective-permute-start | bytes 12296 | tf_op jit(solution)/shard_map/ppermute | solution.py:508
  20.3 4.2 %collective-permute-start.4 = (f32[8,128]{1,0:T(8,128)S(1)}, f32[8,128]{1,0:T(8,128)S(1)}, u32[]{:S(2)}, u32[]{:S(2)}) collective-permute-start(f32[8,128]{1,0:T(8,128)S(1)} %max.18), channel_id=1, source_target_pairs={{0,32},{8,40},{16,48},{24,56},{32,0},{40,8},{48,16},{56,24},{1,33}... | collective-permute-start | bytes 12296 | tf_op jit(solution)/shard_map/ppermute | solution.py:508
  23.5 7.5 %copy-start.3 = (f32[2,8,16]{2,1,0:T(8,128)S(1)}, f32[2,8,16]{2,1,0:T(8,128)}, u32[]{:S(2)}) copy-start(f32[2,8,16]{2,1,0:T(8,128)} %wind_ref.1) | copy-start | bytes 3076
  24.6 9.6 %collective-permute-start.9 = (f32[8,3,16,128]{3,2,1,0:T(8,128)S(1)}, f32[8,3,16,128]{3,2,1,0:T(8,128)S(1)}, u32[]{:S(2)}, u32[]{:S(2)}) collective-permute-start(f32[8,3,16,128]{3,2,1,0:T(8,128)S(1)} %get-tuple-element.29), channel_id=1, source_target_pairs={{0,1},{1,0},{2,3},{3,2},{4,5},{5,4},{6,7},{7,6},{8,9},{9,8},{10,11... | collective-permute-start | bytes 589832 | tf_op jit(solution)/shard_map/ppermute | solution.py:496
  26.3 7.9 %collective-permute-start.10 = (f32[8,3,16,128]{3,2,1,0:T(8,128)S(1)}, f32[8,3,16,128]{3,2,1,0:T(8,128)S(1)}, u32[]{:S(2)}, u32[]{:S(2)}) collective-permute-start(f32[8,3,16,128]{3,2,1,0:T(8,128)S(1)} %get-tuple-element.30), channel_id=1, source_target_pairs={{0,7},{1,2},{2,1},{3,4},{4,3},{5,6},{6,5},{7,0},{8,15},{9,10},{10,... | collective-permute-start | bytes 589832 | tf_op jit(solution)/shard_map/ppermute | solution.py:496
  35.8 7.1 %collective-permute-start.11 = (f32[8,10,3,128]{3,2,1,0:T(4,128)S(1)}, f32[8,10,3,128]{3,2,1,0:T(4,128)S(1)}, u32[]{:S(2)}, u32[]{:S(2)}) collective-permute-start(f32[8,10,3,128]{3,2,1,0:T(4,128)S(1)} %get-tuple-element.32), channel_id=1, source_target_pairs={{0,8},{8,0},{16,24},{24,16},{32,40},{40,32},{48,56},{56,48},{1,9},... | collective-permute-start | bytes 368648 | tf_op jit(solution)/shard_map/ppermute | solution.py:496
  39.1 10.6 %collective-permute-start.13 = (f32[3,10,16,128]{3,2,1,0:T(8,128)S(1)}, f32[3,10,16,128]{3,2,1,0:T(8,128)S(1)}, u32[]{:S(2)}, u32[]{:S(2)}) collective-permute-start(f32[3,10,16,128]{3,2,1,0:T(8,128)S(1)} %get-tuple-element.34), channel_id=1, source_target_pairs={{0,64},{64,0},{128,192},{192,128},{1,65},{65,1},{129,193},{193,129... | collective-permute-start | bytes 737288 | tf_op jit(solution)/shard_map/ppermute | solution.py:496
  39.1 10.6 %collective-permute-start.14 = (f32[3,10,16,128]{3,2,1,0:T(8,128)S(1)}, f32[3,10,16,128]{3,2,1,0:T(8,128)S(1)}, u32[]{:S(2)}, u32[]{:S(2)}) collective-permute-start(f32[3,10,16,128]{3,2,1,0:T(8,128)S(1)} %get-tuple-element.35), channel_id=1, source_target_pairs={{0,192},{64,128},{128,64},{192,0},{1,193},{65,129},{129,65},{193,1... | collective-permute-start | bytes 737288 | tf_op jit(solution)/shard_map/ppermute | solution.py:496
  40.0 11.1 %collective-permute-start.15 = (f32[8,3,16,128]{3,2,1,0:T(8,128)S(1)}, f32[8,3,16,128]{3,2,1,0:T(8,128)S(1)}, u32[]{:S(2)}, u32[]{:S(2)}) collective-permute-start(f32[8,3,16,128]{3,2,1,0:T(8,128)S(1)} %get-tuple-element.36), channel_id=1, source_target_pairs={{0,1},{1,0},{2,3},{3,2},{4,5},{5,4},{6,7},{7,6},{8,9},{9,8},{10,11... | collective-permute-start | bytes 589832 | tf_op jit(solution)/shard_map/ppermute | solution.py:496
  40.0 11.1 %collective-permute-start.16 = (f32[8,3,16,128]{3,2,1,0:T(8,128)S(1)}, f32[8,3,16,128]{3,2,1,0:T(8,128)S(1)}, u32[]{:S(2)}, u32[]{:S(2)}) collective-permute-start(f32[8,3,16,128]{3,2,1,0:T(8,128)S(1)} %get-tuple-element.37), channel_id=1, source_target_pairs={{0,7},{1,2},{2,1},{3,4},{4,3},{5,6},{6,5},{7,0},{8,15},{9,10},{10,... | collective-permute-start | bytes 589832 | tf_op jit(solution)/shard_map/ppermute | solution.py:496
  42.9 5.0 %collective-permute-start.12 = (f32[8,10,3,128]{3,2,1,0:T(4,128)S(1)}, f32[8,10,3,128]{3,2,1,0:T(4,128)S(1)}, u32[]{:S(2)}, u32[]{:S(2)}) collective-permute-start(f32[8,10,3,128]{3,2,1,0:T(4,128)S(1)} %get-tuple-element.33), channel_id=1, source_target_pairs={{0,56},{8,16},{16,8},{24,32},{32,24},{40,48},{48,40},{56,0},{1,57}... | collective-permute-start | bytes 368648 | tf_op jit(solution)/shard_map/ppermute | solution.py:496
  52.8 7.0 %collective-permute-start.17 = (f32[8,10,3,128]{3,2,1,0:T(4,128)S(1)}, f32[8,10,3,128]{3,2,1,0:T(4,128)S(1)}, u32[]{:S(2)}, u32[]{:S(2)}) collective-permute-start(f32[8,10,3,128]{3,2,1,0:T(4,128)S(1)} %get-tuple-element.39), channel_id=1, source_target_pairs={{0,8},{8,0},{16,24},{24,16},{32,40},{40,32},{48,56},{56,48},{1,9},... | collective-permute-start | bytes 368648 | tf_op jit(solution)/shard_map/ppermute | solution.py:496
  54.7 11.8 %collective-permute-start.19 = (f32[3,10,16,128]{3,2,1,0:T(8,128)S(1)}, f32[3,10,16,128]{3,2,1,0:T(8,128)S(1)}, u32[]{:S(2)}, u32[]{:S(2)}) collective-permute-start(f32[3,10,16,128]{3,2,1,0:T(8,128)S(1)} %get-tuple-element.41), channel_id=1, source_target_pairs={{0,64},{64,0},{128,192},{192,128},{1,65},{65,1},{129,193},{193,129... | collective-permute-start | bytes 737288 | tf_op jit(solution)/shard_map/ppermute | solution.py:496
  55.4 11.2 %collective-permute-start.20 = (f32[3,10,16,128]{3,2,1,0:T(8,128)S(1)}, f32[3,10,16,128]{3,2,1,0:T(8,128)S(1)}, u32[]{:S(2)}, u32[]{:S(2)}) collective-permute-start(f32[3,10,16,128]{3,2,1,0:T(8,128)S(1)} %get-tuple-element.42), channel_id=1, source_target_pairs={{0,192},{64,128},{128,64},{192,0},{1,193},{65,129},{129,65},{193,1... | collective-permute-start | bytes 737288 | tf_op jit(solution)/shard_map/ppermute | solution.py:496
  57.4 10.6 %collective-permute-start.21 = (f32[8,3,16,128]{3,2,1,0:T(8,128)S(1)}, f32[8,3,16,128]{3,2,1,0:T(8,128)S(1)}, u32[]{:S(2)}, u32[]{:S(2)}) collective-permute-start(f32[8,3,16,128]{3,2,1,0:T(8,128)S(1)} %get-tuple-element.43), channel_id=1, source_target_pairs={{0,1},{1,0},{2,3},{3,2},{4,5},{5,4},{6,7},{7,6},{8,9},{9,8},{10,11... | collective-permute-start | bytes 589832 | tf_op jit(solution)/shard_map/ppermute | solution.py:496
  57.4 10.6 %collective-permute-start.22 = (f32[8,3,16,128]{3,2,1,0:T(8,128)S(1)}, f32[8,3,16,128]{3,2,1,0:T(8,128)S(1)}, u32[]{:S(2)}, u32[]{:S(2)}) collective-permute-start(f32[8,3,16,128]{3,2,1,0:T(8,128)S(1)} %get-tuple-element.44), channel_id=1, source_target_pairs={{0,7},{1,2},{2,1},{3,4},{4,3},{5,6},{6,5},{7,0},{8,15},{9,10},{10,... | collective-permute-start | bytes 589832 | tf_op jit(solution)/shard_map/ppermute | solution.py:496
  59.8 5.0 %collective-permute-start.18 = (f32[8,10,3,128]{3,2,1,0:T(4,128)S(1)}, f32[8,10,3,128]{3,2,1,0:T(4,128)S(1)}, u32[]{:S(2)}, u32[]{:S(2)}) collective-permute-start(f32[8,10,3,128]{3,2,1,0:T(4,128)S(1)} %get-tuple-element.40), channel_id=1, source_target_pairs={{0,56},{8,16},{16,8},{24,32},{32,24},{40,48},{48,40},{56,0},{1,57}... | collective-permute-start | bytes 368648 | tf_op jit(solution)/shard_map/ppermute | solution.py:496
